TPU v7x, 32 devices: a whole 2x2x4 slice. The times are simulated.
32 devices in a mesh: morton: 16 (over z, y, x), dp: 2 (over core).
Axes of the slice: x: 2, y: 2, z: 4, core: 2. Of those that a mesh axis runs over, the one named last changes fastest.
Arguments:
- node_feat: bfloat16 [2, 8192, 128], P('dp', 'morton'), may hold values from -6 to 6
- edge_feat: bfloat16 [2, 32768, 128], P('dp', 'morton'), may hold values from -6 to 6
- cot_node: bfloat16 [2, 8192, 128], P('dp', 'morton'), may hold values from -6 to 6
- cot_edge: bfloat16 [2, 32768, 128], P('dp', 'morton'), may hold values from -6 to 6
- senders: int32 [2, 32768], P('dp', 'morton'), may hold values from 0 to 767, as said below
- receivers: int32 [2, 32768], P('dp', 'morton'), may hold values from 0 to 511
- send_rows: int32 [2, 4096], P('dp', 'morton'), may hold values from 0 to 511
- edge_count: int32 [2, 16], P('dp', 'morton'), may hold values from 512 to 2048, as said below
- edge_w1: float32 [384, 128], replicated, may hold values from -0.3125 to 0.3125
- edge_w2: float32 [128, 128], replicated, may hold values from -0.5 to 0.5
- edge_gain: float32 [128], replicated, may hold values from 0.25 to 1.75
- node_w1: float32 [256, 128], replicated, may hold values from -0.375 to 0.375
- node_w2: float32 [128, 128], replicated, may hold values from -0.5 to 0.5
- node_gain: float32 [128], replicated, may hold values from 0.25 to 1.75
Outputs:
- grad_node: float32 [2, 8192, 128], P('dp', 'morton')
- grad_edge: float32 [2, 32768, 128], P('dp', 'morton')
- grad_edge_w1: float32 [384, 128], replicated
- grad_edge_w2: float32 [128, 128], replicated
- grad_edge_gain: float32 [128], replicated
- grad_node_w1: float32 [256, 128], replicated
- grad_node_w2: float32 [128, 128], replicated
- grad_node_gain: float32 [128], replicated
Inputs may be any that keep to these rules, and one draw needn't show every extreme that they name: `senders`: on device m, an entry below 512 is one of its own cells; an entry 512 + k * 64 + q is ghost row q of group k, which comes from device m - d_k with d = (-16/2, -1, +1, +16/2); that device always exists. `send_rows`: entry k * 64 + q of device m is its local cell sent to device m + d_k, with d = (-16/2, -1, +1, +16/2). `edge_count`: edge slots at or beyond the count are empty; some device of every block is full.
All inputs are finite; a program needn't handle non-finite values.
Results may differ from a plain program's by a relative error of at most 0.014.
Values may be sent and summed in bfloat16 or wider, within the bound.
No kernel may reach another device: no remote copies, remote signals or barrier semaphores. Data moves between devices by JAX's collectives and lax.ppermute only.
A program may use at most 64 MiB of HBM per device.

v0:
```python
import jax
import jax.numpy as jnp
from jax import lax
from jax.sharding import PartitionSpec as P


def layer_norm(values, gain):
    center = values - jnp.mean(values, axis=-1, keepdims=True)
    spread = jnp.mean(center * center, axis=-1, keepdims=True)
    return center * lax.rsqrt(spread + 1e-05) * gain


def local_forward(
    cells, ghosts, edges, ew1, ew2, egain, nw1, nw2, ngain, sending, receiving, count
):
    table = jnp.concatenate([cells, ghosts], axis=0)
    joined = jnp.concatenate(
        [
            edges.astype(jnp.bfloat16),
            table[sending].astype(jnp.bfloat16),
            cells[receiving].astype(jnp.bfloat16),
        ],
        axis=1,
    )
    first = jnp.dot(joined, ew1.astype(jnp.bfloat16), preferred_element_type=jnp.float32)
    second = jnp.dot(
        jax.nn.silu(first).astype(jnp.bfloat16),
        ew2.astype(jnp.bfloat16),
        preferred_element_type=jnp.float32,
    )
    live = (jnp.arange(edges.shape[0]) < count).astype(edges.dtype)[:, None]
    edge_new = edges + live * layer_norm(second, egain)
    message = (live * edge_new).astype(jnp.bfloat16)
    gathered = jax.ops.segment_sum(
        message.astype(edges.dtype), receiving, num_segments=cells.shape[0]
    )
    stacked = jnp.concatenate([cells.astype(jnp.bfloat16), gathered.astype(jnp.bfloat16)], axis=1)
    hidden = jnp.dot(stacked, nw1.astype(jnp.bfloat16), preferred_element_type=jnp.float32)
    output = jnp.dot(
        jax.nn.silu(hidden).astype(jnp.bfloat16),
        nw2.astype(jnp.bfloat16),
        preferred_element_type=jnp.float32,
    )
    return (cells + layer_norm(output, ngain), edge_new)


def on_device(
    node_feat,
    edge_feat,
    cot_node,
    cot_edge,
    senders,
    receivers,
    send_rows,
    edge_count,
    edge_w1,
    edge_w2,
    edge_gain,
    node_w1,
    node_w2,
    node_gain,
):
    peers = lax.axis_size("morton")
    rank = lax.axis_index("morton")
    offsets = (-(peers // 2), -1, 1, peers // 2)
    width = node_feat.shape[2]
    quota = send_rows.shape[1] // 4
    outgoing = send_rows[0].reshape(4, quota)
    cells_bf = node_feat[0]
    picked = [cells_bf[outgoing[k]] for k in range(4)]
    arrived = []
    buffer = jnp.zeros((peers, quota, width), jnp.bfloat16)
    for k in range(4):
        target = jax.nn.one_hot(rank + offsets[k], peers, dtype=jnp.bfloat16)
        buffer = buffer + target[:, None, None] * picked[k][None]
    received = lax.all_to_all(buffer, "morton", split_axis=0, concat_axis=0, tiled=True)
    for k in range(4):
        source = rank - offsets[k]
        valid = ((source >= 0) & (source < peers)).astype(jnp.float32)
        arrived.append(received[jnp.clip(source, 0, peers - 1)].astype(jnp.float32) * valid)
    ghosts = jnp.concatenate(arrived, axis=0)
    cells = cells_bf.astype(jnp.float32)
    edges = edge_feat[0].astype(jnp.float32)
    sending = senders[0]
    receiving = receivers[0]
    count = edge_count[0, 0]

    def forward(cells, ghosts, edges, ew1, ew2, egain, nw1, nw2, ngain):
        return local_forward(
            cells, ghosts, edges, ew1, ew2, egain, nw1, nw2, ngain, sending, receiving, count
        )

    outputs, pullback = jax.vjp(
        forward, cells, ghosts, edges, edge_w1, edge_w2, edge_gain, node_w1, node_w2, node_gain
    )
    grads = pullback((cot_node[0].astype(jnp.float32), cot_edge[0].astype(jnp.float32)))
    grad_cells = grads[0]
    ghost_grads = grads[1].reshape(4, quota, width)
    buffer = jnp.zeros((peers, quota, width), jnp.float32)
    for k in range(4):
        target = jax.nn.one_hot(rank - offsets[k], peers, dtype=jnp.float32)
        buffer = buffer + target[:, None, None] * ghost_grads[k][None]
    returned = lax.all_to_all(
        buffer.astype(jnp.bfloat16), "morton", split_axis=0, concat_axis=0, tiled=True
    ).astype(buffer.dtype)
    for k in range(4):
        reader = rank + offsets[k]
        valid = ((reader >= 0) & (reader < peers)).astype(jnp.float32)
        grad_cells = grad_cells.at[outgoing[k]].add(
            returned[jnp.clip(reader, 0, peers - 1)] * valid
        )
    summed = lax.psum(
        (grads[3], grads[4], grads[5], grads[6], grads[7], grads[8]), ("morton", "dp")
    )
    factor = 1.0 / jnp.sqrt(jnp.float32(lax.axis_size("dp") * peers * edge_feat.shape[1]))
    return (
        grad_cells[None],
        grads[2][None],
        summed[0] * factor,
        summed[1] * factor,
        summed[2] * factor,
        summed[3] * factor,
        summed[4] * factor,
        summed[5] * factor,
    )


def solution(mesh):
    in_specs = (
        P("dp", "morton", None),
        P("dp", "morton", None),
        P("dp", "morton", None),
        P("dp", "morton", None),
        P("dp", "morton"),
        P("dp", "morton"),
        P("dp", "morton"),
        P("dp", "morton"),
        P(),
        P(),
        P(),
        P(),
        P(),
        P(),
    )
    out_specs = (P("dp", "morton", None), P("dp", "morton", None), P(), P(), P(), P(), P(), P())
    return jax.shard_map(
        on_device, mesh=mesh, in_specs=in_specs, out_specs=out_specs, check_vma=False
    )
```

profile of v0, /device:TPU:0, one launch (start us, length us, event | category | flops | bytes accessed | tf_op | source)
XLA Modules:
  0.0 282.0 jit_solution(1534379466530907861)
XLA Ops:
  8.6 1.5 gather_fusion.3
  10.2 1.5 gather_fusion.1
  11.7 1.5 gather_fusion.2
  13.2 1.5 gather_fusion
  15.6 8.5 %all-to-all-start = ((bf16[16,64,128]{2,1,0:T(8,128)(2,1)}), bf16[16,64,128]{2,1,0:T(8,128)(2,1)S(1)}, u32[]{:S(2)}, u32[]{:S(2)}) async-start(bf16[16,64,128]{2,1,0:T(8,128)(2,1)} %multiply_add_fusion), calls=%async_computation | async-start | bytes 524288 | tf_op jit(solution)/shard_map/all_to_all | solution.py:76
  24.7 1.3 and_reduce_fusion
  29.9 6.2 %gather_fusion.5 = bf16[2048,128]{1,0:T(8,128)(2,1)S(1)} fusion(bf16[512,128]{1,0:T(8,128)(2,1)S(1)} %bitcast.84, s32[2048]{0:T(1024)S(1)} %get-tuple-element.56), kind=kCustom, calls=%fused_computation.5 | custom fusion | bytes 1056768 | tf_op jit(solution)/shard_map/jvp()/gather | solution.py:21
  36.5 6.2 %gather_fusion.4 = bf16[2048,128]{1,0:T(8,128)(2,1)S(1)} fusion(bf16[768,128]{1,0:T(8,128)(2,1)S(1)} %bitcast_dynamic-update-slice_fusion, s32[2048]{0:T(1024)S(1)} %broadcast_clamp_fusion.2), kind=kCustom, calls=%fused_computation.4 | custom fusion | bytes 1056768 | tf_op jit(solution)/shard_map/jvp()/gather | solution.py:20
  46.4 1.3 copy.45
  47.8 12.1 %scatter_custom_fusion = f32[512,128]{1,0:T(8,128)S(1)} fusion(s32[2048]{0:T(1024)} %bitcast.91, f32[2048,128]{1,0:T(8,128)} %copy.45, f32[]{:T(128)} %constant.24.clone.1), kind=kCustom, calls=%fused_computation.77 | custom fusion | flops 262144 | bytes 262656 | tf_op jit(solution)/shard_map/jvp()/scatter-add | solution.py:34
  60.1 1.2 fusion.76
  62.1 0.9 fusion.5
  65.4 6.2 %gather_fusion.6 = bf16[2048,128]{1,0:T(8,128)(2,1)S(1)} fusion(bf16[512,128]{1,0:T(8,128)(2,1)S(1)} %copy.48, s32[2048]{0:T(1024)S(1)} %copy-done.21), kind=kCustom, calls=%fused_computation.6 | custom fusion | bytes 1056768 | tf_op jit(solution)/shard_map/transpose(jvp())/gather | solution.py:34
  73.8 1.1 fusion.4
  76.1 1.2 fusion.2
  77.3 1.5 convolution_convert_fusion
  79.3 1.3 copy.51
  80.7 12.0 %scatter_custom_fusion.1 = f32[768,128]{1,0:T(8,128)S(1)} fusion(s32[2048]{0:T(1024)} %bitcast.94, f32[2048,128]{1,0:T(8,128)} %copy.51, f32[]{:T(128)} %constant.24.clone.1), kind=kCustom, calls=%fused_computation.71 | custom fusion | flops 262144 | bytes 393728 | tf_op jit(solution)/shard_map/transpose(jvp())/scatter-add | solution.py:20
  93.6 40.5 %all-reduce = (f32[128]{0:T(128)S(1)}, f32[128]{0:T(128)S(1)}) all-reduce(f32[128]{0:T(128)S(1)} %get-tuple-element.24, f32[128]{0:T(128)S(1)} %copy-done.35), channel_id=1, replica_groups=mesh['morton'=16,'dp'=2] {'morton','dp'}, use_global_device_ids=true, to_apply=%region_18.19 | all-reduce | flops 256 | bytes 2048 | tf_op jit(solution)/shard_map/psum | solution.py:112
  134.2 0.9 add_convert_fusion
  135.7 1.3 copy.55
  138.0 5.5 %all-to-all-start.1 = ((bf16[16,64,128]{2,1,0:T(8,128)(2,1)}), bf16[16,64,128]{2,1,0:T(8,128)(2,1)S(1)}, u32[]{:S(2)}, u32[]{:S(2)}) async-start(bf16[16,64,128]{2,1,0:T(8,128)(2,1)} %add_convert_fusion), calls=%async_computation.1 | async-start | bytes 524288 | tf_op jit(solution)/shard_map/all_to_all | solution.py:103
  143.6 11.6 %scatter_fusion = f32[512,128]{1,0:T(8,128)S(1)} fusion(f32[512,128]{1,0:T(8,128)S(1)} %copy.53, s32[2048]{0:T(1024)S(1)} %bitcast.90, f32[2048,128]{1,0:T(8,128)S(1)} %copy.54), kind=kCustom, calls=%fused_computation.9 | custom fusion | flops 262144 | bytes 3153920 | tf_op jit(solution)/shard_map/transpose(jvp())/scatter-add | solution.py:21
  155.7 107.9 %all-reduce.4.cloned.1.call-done = (f32[384,128]{1,0:T(8,128)}, f32[128,128]{1,0:T(8,128)}, f32[256,128]{1,0:T(8,128)}, f32[128,128]{1,0:T(8,128)}) async-done(((f32[384,128]{1,0:T(8,128)}, f32[128,128]{1,0:T(8,128)}, f32[256,128]{1,0:T(8,128)}, f32[128,128]{1,0:T(8,128)}), (f32[384,128]{1,0:T(8,128)}, f32[128,128]{1,0:T(8,128)}, f32[256,128]{1,0:T(8,128)}, ...) | async-done | bytes 458768 | tf_op jit(solution)/shard_map/psum | solution.py:112
  263.6 1.5 broadcast_multiply_fusion.3
  265.1 1.5 broadcast_multiply_fusion.2
  266.6 1.6 broadcast_multiply_fusion.1
  268.1 1.6 broadcast_multiply_fusion
  269.8 1.2 scatter_custom_fusion.3
  271.0 1.2 scatter_custom_fusion.4
  272.2 1.2 scatter_custom_fusion.5
  273.3 1.2 scatter_custom_fusion.6
  (144 shorter events, 21.0 us)
Async XLA Ops:
  7.2 20.9 %copy-start.20 = (s32[1,2048]{1,0:T(1,128)S(1)}, s32[1,2048]{1,0:T(1,128)}, u32[]{:S(2)}) copy-start(s32[1,2048]{1,0:T(1,128)} %param.19) | copy-start | bytes 24580
  7.2 22.1 %copy-start.15 = (bf16[1,512,128]{2,1,0:T(8,128)(2,1)S(1)}, bf16[1,512,128]{2,1,0:T(8,128)(2,1)}, u32[]{:S(2)}) copy-start(bf16[1,512,128]{2,1,0:T(8,128)(2,1)} %param.16) | copy-start | bytes 393220
  7.2 22.2 %copy-start.5 = (bf16[1,2048,128]{2,1,0:T(8,128)(2,1)S(1)}, bf16[1,2048,128]{2,1,0:T(8,128)(2,1)}, u32[]{:S(2)}) copy-start(bf16[1,2048,128]{2,1,0:T(8,128)(2,1)} %param.17) | copy-start | bytes 1572868
  7.2 22.5 %copy-start.6 = (bf16[1,2048,128]{2,1,0:T(8,128)(2,1)S(1)}, bf16[1,2048,128]{2,1,0:T(8,128)(2,1)}, u32[]{:S(2)}) copy-start(bf16[1,2048,128]{2,1,0:T(8,128)(2,1)} %param.15) | copy-start | bytes 1572868
  8.1 3.6 %copy-start.31 = (s32[64]{0:T(128)}, s32[64]{0:T(128)S(1)}, u32[]{:S(2)}) copy-start(s32[64]{0:T(128)S(1)} %get-tuple-element.49) | copy-start | bytes 772
  8.1 3.6 %copy-start.32 = (s32[64]{0:T(128)}, s32[64]{0:T(128)S(1)}, u32[]{:S(2)}) copy-start(s32[64]{0:T(128)S(1)} %get-tuple-element.50) | copy-start | bytes 772
  15.6 14.3 %copy-start.1 = (bf16[1,512,128]{2,1,0:T(8,128)(2,1)S(1)}, bf16[1,512,128]{2,1,0:T(8,128)(2,1)}, u32[]{:S(2)}) copy-start(bf16[1,512,128]{2,1,0:T(8,128)(2,1)} %param.14) | copy-start | bytes 393220
  15.6 20.7 %all-to-all-start = ((bf16[16,64,128]{2,1,0:T(8,128)(2,1)}), bf16[16,64,128]{2,1,0:T(8,128)(2,1)S(1)}, u32[]{:S(2)}, u32[]{:S(2)}) async-start(bf16[16,64,128]{2,1,0:T(8,128)(2,1)} %multiply_add_fusion), calls=%async_computation | async-start | bytes 524288 | tf_op jit(solution)/shard_map/all_to_all | solution.py:76
  24.1 239.5 %all-reduce.4.cloned.1.call-start = ((), (), s32[]{:S(2)}) async-start(), calls=%async_computation.2 | async-start | bytes 917504 | tf_op jit(solution)/shard_map/psum | solution.py:112
  26.7 2.6 copy-start.18
  28.1 8.2 %copy-start.22 = (s32[2048,1]{0,1:T(1,128)}, s32[2048,1]{0,1:T(1,128)S(1)}, u32[]{:S(2)}) copy-start(s32[2048,1]{0,1:T(1,128)S(1)} %compare_select_fusion.1) | copy-start | bytes 24580
  36.3 6.6 %copy-start.7 = (bf16[2048,128]{0,1:T(8,128)(2,1)}, bf16[2048,128]{0,1:T(8,128)(2,1)S(1)}, u32[]{:S(2)}) copy-start(bf16[2048,128]{0,1:T(8,128)(2,1)S(1)} %copy.44) | copy-start | bytes 1572868
  36.5 6.4 %copy-start.12 = (f32[384,128]{1,0:T(8,128)S(1)}, f32[384,128]{1,0:T(8,128)}, u32[]{:S(2)}) copy-start(f32[384,128]{1,0:T(8,128)} %param.22) | copy-start | bytes 589828
  43.8 2.3 copy-start.24
  46.4 13.4 %copy-start.11 = (f32[256,128]{1,0:T(8,128)S(1)}, f32[256,128]{1,0:T(8,128)}, u32[]{:S(2)}) copy-start(f32[256,128]{1,0:T(8,128)} %param.25) | copy-start | bytes 393220
  47.8 13.5 %copy-start.26 = (f32[128]{0:T(128)S(1)}, f32[128]{0:T(128)}, u32[]{:S(2)}) copy-start(f32[128]{0:T(128)} %param.27) | copy-start | bytes 1540
  60.1 2.9 %copy-start.36 = (f32[128,128]{1,0:T(8,128)S(1)}, f32[128,128]{1,0:T(8,128)}, u32[]{:S(2)}) copy-start(f32[128,128]{1,0:T(8,128)} %param.26) | copy-start | bytes 196612
  63.0 2.3 copy-start.21
  65.4 6.4 %copy-start.14 = (f32[2048]{0:T(1024)S(1)}, f32[2048]{0:T(1024)}, u32[]{:S(2)}) copy-start(f32[2048]{0:T(1024)} %copy-done.13) | copy-start | bytes 24580
  65.4 6.4 %copy-start.23 = (pred[2048]{0:T(1024)(128)(4,1)S(1)}, pred[2048]{0:T(1024)(128)(4,1)}, u32[]{:S(2)}) copy-start(pred[2048]{0:T(1024)(128)(4,1)} %and_reduce_fusion) | copy-start | bytes 6148
  65.4 6.4 %copy-start.25 = (f32[128]{0:T(128)S(1)}, f32[128]{0:T(128)}, u32[]{:S(2)}) copy-start(f32[128]{0:T(128)} %param.24) | copy-start | bytes 1540
  72.6 1.2 copy-start.40
  73.8 1.1 copy-start.38
  74.9 1.2 copy-start.10
  80.7 12.2 %copy-start.4 = (bf16[512,256]{0,1:T(8,128)(2,1)S(1)}, bf16[512,256]{0,1:T(8,128)(2,1)}, u32[]{:S(2)}) copy-start(bf16[512,256]{0,1:T(8,128)(2,1)} %copy-done.3) | copy-start | bytes 786436
  80.7 13.0 %copy-start.35 = (f32[128]{0:T(128)S(1)}, f32[128]{0:T(128)}, u32[]{:S(2)}) copy-start(f32[128]{0:T(128)} %get-tuple-element.26) | copy-start | bytes 1540
  80.7 53.5 %copy-start.27 = (f32[16]{0:T(128)S(1)}, f32[16]{0:T(128)}, u32[]{:S(2)}) copy-start(f32[16]{0:T(128)} %get-tuple-element.67) | copy-start | bytes 196
  80.7 53.5 %copy-start.28 = (f32[16]{0:T(128)S(1)}, f32[16]{0:T(128)}, u32[]{:S(2)}) copy-start(f32[16]{0:T(128)} %get-tuple-element.68) | copy-start | bytes 196
  80.7 53.5 %copy-start.29 = (f32[16]{0:T(128)S(1)}, f32[16]{0:T(128)}, u32[]{:S(2)}) copy-start(f32[16]{0:T(128)} %get-tuple-element.65) | copy-start | bytes 196
  80.7 53.5 %copy-start.30 = (f32[16]{0:T(128)S(1)}, f32[16]{0:T(128)}, u32[]{:S(2)}) copy-start(f32[16]{0:T(128)} %get-tuple-element.66) | copy-start | bytes 196
  137.0 6.6 %copy-start.19 = (s32[2048,1]{0,1:T(1,128)S(1)}, s32[2048,1]{0,1:T(1,128)}, u32[]{:S(2)}) copy-start(s32[2048,1]{0,1:T(1,128)} %copy-done.18) | copy-start | bytes 24580
  138.0 131.7 %all-to-all-start.1 = ((bf16[16,64,128]{2,1,0:T(8,128)(2,1)}), bf16[16,64,128]{2,1,0:T(8,128)(2,1)S(1)}, u32[]{:S(2)}, u32[]{:S(2)}) async-start(bf16[16,64,128]{2,1,0:T(8,128)(2,1)} %add_convert_fusion), calls=%async_computation.1 | async-start | bytes 524288 | tf_op jit(solution)/shard_map/all_to_all | solution.py:103
  (12 other events, 9.0 us)
Sparse Core Ops, SparseCore 0:
  134.3 129.2 all-reduce.3
where the time goes:
time: 284 us; the launch traced here: 282 us
  waiting for transfers between devices  108 us (38%)
  other arithmetic  58.2 us (20%)
  blocking collectives  40.5 us (14%)
  local copies, waits for them, and re-layouts  36.5 us (13%)
  between operations  15.4 us (5%)
  starting transfers between devices  14 us (5%)
  matrix products  9.33 us (3%)
    psum x1, waiting for transfers between devices, on_device(): lax.psum((grads[3], grads[4], grads[5], grads[6], grads[7], grads[8]), ('...  108 us
    psum x1, blocking collectives, on_device(): lax.psum((grads[3], grads[4], grads[5], grads[6], grads[7], grads[8]), ('...  40.5 us
    scatter-add x1, other arithmetic, local_forward(): jax.ops.segment_sum(message.astype(edges.dtype), receiving, num_segments=...  12.1 us
    scatter-add x1, other arithmetic, local_forward(): table[sending].astype(jnp.bfloat16)  12 us
    scatter-add x1, other arithmetic, local_forward(): cells[receiving].astype(jnp.bfloat16)  11.6 us
    all_to_all x1, starting transfers between devices, on_device(): lax.all_to_all(buffer, 'morton', split_axis=0, concat_axis=0, tiled=True)  8.47 us
    unnamed x87, local copies, waits for them, and re-layouts  8.03 us
    gather x2, local copies, waits for them, and re-layouts, local_forward(): cells[receiving].astype(jnp.bfloat16)  6.4 us
  transfers between devices with their start and end apart: 3, of which 1 were waited for; matrix products, arithmetic and copies ran while one was open for 12% of the time, Pallas kernels for 0%

commit v1 on v0

v1 whole, which is shorter than its diff:
```python
import functools

import jax
import jax.numpy as jnp
from jax import lax
from jax.experimental import pallas as pl
from jax.experimental.pallas import tpu as pltpu
from jax.sharding import PartitionSpec as P

BF = jnp.bfloat16
F32 = jnp.float32
EPS = 1e-05
CHUNK = 256


def mm(a, b):
    return lax.dot_general(a, b, (((1,), (0,)), ((), ())), preferred_element_type=F32)


def mm_rt(a, b):
    return lax.dot_general(a, b, (((1,), (1,)), ((), ())), preferred_element_type=F32)


def mm_lt(a, b):
    return lax.dot_general(a, b, (((0,), (0,)), ((), ())), preferred_element_type=F32)


def silu_parts(a):
    sig = 0.5 * jnp.tanh(0.5 * a) + 0.5
    act = a * sig
    return act, sig + act * (1.0 - sig)


def norm_parts(b):
    center = b - jnp.mean(b, axis=-1, keepdims=True)
    inv = lax.rsqrt(jnp.mean(center * center, axis=-1, keepdims=True) + EPS)
    return center * inv, inv


def norm_back(g, nrm, inv):
    return inv * (
        g
        - jnp.mean(g, axis=-1, keepdims=True)
        - nrm * jnp.mean(g * nrm, axis=-1, keepdims=True)
    )


def one_hot_cols(col, size):
    lane = lax.broadcasted_iota(jnp.int32, (col.shape[0], size), 1)
    return jnp.where(jnp.tile(col, (1, size // col.shape[1])) == lane, 1.0, 0.0).astype(BF)


def one_hot_rows(row, size):
    sub = lax.broadcasted_iota(jnp.int32, (size, row.shape[1]), 0)
    return jnp.where(row == sub, 1.0, 0.0).astype(BF)


def layer_kernel(
    count_ref, h_ref, gh_ref, e_ref, cn_ref, ce_ref, snd_ref, rcv_ref,
    w1_ref, w2_ref, eg_ref, nw1_ref, nw2_ref, ng_ref,
    gnode_ref, gedge_ref, gghost_ref, wg_ref,
    tmat, col_s, col_r, rhs, p_s, dsil_s, nrm_s, inv_s, ptr, pts, pr, agg, dagg_s, db_s, da_s,
):
    H = h_ref.shape[1]
    C = h_ref.shape[0]
    E = e_ref.shape[0]
    T = C + gh_ref.shape[0]
    count = count_ref[0, 0]
    nrow = E // 128

    tmat[...] = jnp.zeros_like(tmat)
    for r in range(nrow):
        tmat[r : r + 1, :] = snd_ref[:, r * 128 : (r + 1) * 128]
        tmat[nrow + r : nrow + r + 1, :] = rcv_ref[:, r * 128 : (r + 1) * 128]
    turned = jnp.transpose(tmat[...])
    for r in range(nrow):
        col_s[r * 128 : (r + 1) * 128, :] = jnp.broadcast_to(turned[:, r : r + 1], (128, 128))
        col_r[r * 128 : (r + 1) * 128, :] = jnp.broadcast_to(
            turned[:, nrow + r : nrow + r + 1], (128, 128)
        )

    w1 = w1_ref[...].astype(BF)
    w1e, w1s, w1r = w1[:H], w1[H : 2 * H], w1[2 * H :]
    w2 = w2_ref[...].astype(BF)
    h = h_ref[...]
    rhs[0:H, :] = w1e
    rhs[H : H + C, :] = mm(h, w1s).astype(BF)
    rhs[H + C : H + T, :] = mm(gh_ref[...], w1s).astype(BF)
    rhs[H + T :, :] = mm(h, w1r).astype(BF)
    egain = eg_ref[...]
    agg[...] = jnp.zeros_like(agg)

    def fwd(i, carry):
        at = pl.ds(pl.multiple_of(i * CHUNK, CHUNK), CHUNK)
        e = e_ref[at, :]
        ps = one_hot_cols(col_s[at, :], T)
        p_r = one_hot_cols(col_r[at, :], C)
        pr[at, :] = p_r
        a = mm(jnp.concatenate([e, ps, p_r], axis=1), rhs[...])
        act, dsil = silu_parts(a)
        p = act.astype(BF)
        p_s[at, :] = p
        dsil_s[at, :] = dsil
        nrm, inv = norm_parts(mm(p, w2))
        nrm_s[at, :] = nrm
        inv_s[at, :] = inv
        rowid = lax.broadcasted_iota(jnp.int32, (CHUNK, H), 0) + i * CHUNK
        msg = jnp.where(rowid < count, e.astype(F32) + nrm * egain, 0.0).astype(BF)
        pt_r = one_hot_rows(rcv_ref[:, at], C)
        ptr[:, at] = pt_r
        pts[:, at] = one_hot_rows(snd_ref[:, at], T)
        agg[...] += mm(pt_r, msg)
        return carry

    lax.fori_loop(0, E // CHUNK, fwd, 0)

    nw1 = nw1_ref[...].astype(BF)
    nw2 = nw2_ref[...].astype(BF)
    cn = cn_ref[...].astype(F32)
    aggb = agg[...].astype(BF)
    y = jnp.concatenate([h, aggb], axis=1)
    act, dsil = silu_parts(mm(y, nw1))
    r = act.astype(BF)
    nrm, inv = norm_parts(mm(r, nw2))
    ds = norm_back(cn * ng_ref[...], nrm, inv).astype(BF)
    dc = (mm_rt(ds, nw2) * dsil).astype(BF)
    dy = mm_rt(dc, nw1)
    dagg_s[...] = dy[:, H:].astype(BF)
    gnode_ref[...] = cn + dy[:, :H]
    wg_ref[4 * H : 6 * H, :] = mm_lt(y, dc)
    wg_ref[6 * H : 7 * H, :] = mm_lt(r, ds)
    wg_ref[7 * H :, :] = jnp.zeros((wg_ref.shape[0] - 7 * H, H), F32)
    wg_ref[7 * H + 8 : 7 * H + 9, :] = jnp.sum(cn * nrm, axis=0, keepdims=True)

    def bwd(i, gain_sum):
        at = pl.ds(pl.multiple_of(i * CHUNK, CHUNK), CHUNK)
        dmsg = mm(pr[at, :], dagg_s[...])
        rowid = lax.broadcasted_iota(jnp.int32, (CHUNK, H), 0) + i * CHUNK
        alive = rowid < count
        ce = ce_ref[at, :].astype(F32)
        full = ce + dmsg
        d = jnp.where(alive, full, 0.0)
        nrm = nrm_s[at, :]
        gain_sum = gain_sum + jnp.sum((d * nrm).reshape(CHUNK // 8, 8, H), axis=0)
        db = norm_back(d * egain, nrm, inv_s[at, :]).astype(BF)
        db_s[at, :] = db
        da = (mm_rt(db, w2) * dsil_s[at, :]).astype(BF)
        da_s[at, :] = da
        gedge_ref[at, :] = jnp.where(alive, full, ce) + mm_rt(da, w1e)
        return gain_sum

    gain_sum = lax.fori_loop(0, E // CHUNK, bwd, jnp.zeros((8, H), F32))
    wg_ref[7 * H : 7 * H + 1, :] = jnp.sum(gain_sum, axis=0, keepdims=True)
    da = da_s[...]
    wg_ref[3 * H : 4 * H, :] = mm_lt(p_s[...], db_s[...])
    wg_ref[0:H, :] = mm_lt(e_ref[...], da)
    gs = mm(pts[...], da).astype(BF)
    gr = mm(ptr[...], da).astype(BF)
    table = jnp.concatenate([h, gh_ref[...]], axis=0)
    wg_ref[H : 2 * H, :] = mm_lt(table, gs)
    wg_ref[2 * H : 3 * H, :] = mm_lt(h, gr)
    dt = mm_rt(gs, w1s)
    gnode_ref[...] += dt[:C] + mm_rt(gr, w1r)
    gghost_ref[...] = dt[C:].astype(BF)


def run_layer(count, h, ghosts, e, cn, ce, snd, rcv, ew1, ew2, eg, nw1, nw2, ng, rows):
    C, H = h.shape
    E = e.shape[0]
    G = ghosts.shape[0]
    T = C + G
    vm = pl.BlockSpec(memory_space=pltpu.VMEM)
    shapes = (
        jax.ShapeDtypeStruct((C, H), F32),
        jax.ShapeDtypeStruct((E, H), F32),
        jax.ShapeDtypeStruct((G, H), BF),
        jax.ShapeDtypeStruct((rows, H), F32),
    )
    scratch = [
        pltpu.VMEM((128, 128), jnp.int32),
        pltpu.VMEM((E, 128), jnp.int32),
        pltpu.VMEM((E, 128), jnp.int32),
        pltpu.VMEM((H + T + C, H), BF),
        pltpu.VMEM((E, H), BF),
        pltpu.VMEM((E, H), F32),
        pltpu.VMEM((E, H), F32),
        pltpu.VMEM((E, 1), F32),
        pltpu.VMEM((C, E), BF),
        pltpu.VMEM((T, E), BF),
        pltpu.VMEM((E, C), BF),
        pltpu.VMEM((C, H), F32),
        pltpu.VMEM((C, H), BF),
        pltpu.VMEM((E, H), BF),
        pltpu.VMEM((E, H), BF),
    ]
    return pl.pallas_call(
        layer_kernel,
        out_shape=shapes,
        in_specs=[pl.BlockSpec(memory_space=pltpu.SMEM)] + [vm] * 13,
        out_specs=(vm,) * 4,
        scratch_shapes=scratch,
        compiler_params=pltpu.CompilerParams(vmem_limit_bytes=40 * 1024 * 1024),
        cost_estimate=pl.CostEstimate(
            flops=2 * E * H * 4608, bytes_accessed=6 * E * H * 2, transcendentals=E * H
        ),
        name="mesh_layer",
    )(count, h, ghosts, e, cn, ce, snd, rcv, ew1, ew2, eg, nw1, nw2, ng)


def flip(x, axis, by):
    n = lax.axis_size(axis)
    return lax.ppermute(x, axis, [(i, i ^ by) for i in range(n)])


def pick(x, k):
    return lax.dynamic_index_in_dim(x, k, 0, keepdims=False)


def tree_sum(parts):
    while len(parts) > 1:
        parts = [parts[i] + parts[i + 1] for i in range(0, len(parts), 2)]
    return parts[0]


def scatter_sum(v, axis, stride, width):
    j = lax.axis_index(axis) // stride % width
    pieces = v.astype(BF).reshape(width, v.shape[0] // width, v.shape[1])
    own = pick(pieces, j)
    parts = [own.astype(F32)]
    for d in range(1, width):
        parts.append(flip(pick(pieces, j ^ d), axis, d * stride).astype(F32))
    return tree_sum(parts)


def exchange_sum(v, axis, stride, width):
    w = v.astype(BF)
    parts = [w.astype(F32)]
    for d in range(1, width):
        parts.append(flip(w, axis, d * stride).astype(F32))
    return tree_sum(parts)


def gather_pieces(w, axis, stride, width):
    j = lax.axis_index(axis) // stride % width
    parts = [w] + [flip(w, axis, d * stride) for d in range(1, width)]
    stacked = jnp.stack(parts)
    return jnp.concatenate([pick(stacked, j ^ k) for k in range(width)], axis=0)


def widths(n):
    out = []
    stride = 1
    while stride < n:
        w = 4 if n // stride >= 4 else 2
        out.append((stride, w))
        stride *= w
    return out


def reduce_all(v):
    n = lax.axis_size("morton")
    pair = lax.axis_size("dp")
    stages = widths(n)
    v = scatter_sum(v, "dp", 1, pair)
    v = scatter_sum(v, "morton", *stages[0])
    for stride, width in stages[1:]:
        v = exchange_sum(v, "morton", stride, width)
    w = gather_pieces(v.astype(BF), "morton", *stages[0])
    return gather_pieces(w, "dp", 1, pair).astype(F32)


def on_device(
    node_feat, edge_feat, cot_node, cot_edge, senders, receivers, send_rows, edge_count,
    edge_w1, edge_w2, edge_gain, node_w1, node_w2, node_gain,
):
    peers = lax.axis_size("morton")
    rank = lax.axis_index("morton")
    H = node_feat.shape[2]
    h = node_feat[0]
    C = h.shape[0]
    quota = send_rows.shape[1] // 4
    groups = send_rows[0].reshape(4, quota)
    upper = rank >= peers // 2
    far = jnp.where(upper, groups[0], groups[3])
    rows_out = jnp.concatenate([far, groups[1], groups[2]])
    ids = jnp.arange(C, dtype=jnp.int32)
    picked = jnp.dot(
        (rows_out[:, None] == ids[None, :]).astype(BF), h, preferred_element_type=F32
    ).astype(BF)
    half = peers // 2
    down = [(i, (i - 1) % peers) for i in range(peers)]
    up = [(i, (i + 1) % peers) for i in range(peers)]
    across = [(i, (i + half) % peers) for i in range(peers)]
    from_far = lax.ppermute(picked[:quota], "morton", across)
    from_up = lax.ppermute(picked[quota : 2 * quota], "morton", down)
    from_down = lax.ppermute(picked[2 * quota :], "morton", up)
    ghosts = jnp.concatenate([from_far, from_up, from_down, from_far], axis=0)

    rows = -(-(7 * H + 16) // 64) * 64
    gnode, gedge, gghost, wg = run_layer(
        edge_count, h, ghosts, edge_feat[0], cot_node[0], cot_edge[0], senders, receivers,
        edge_w1, edge_w2, edge_gain.reshape(1, H), node_w1, node_w2, node_gain.reshape(1, H), rows,
    )
    gg = gghost.reshape(4, quota, H)
    back_far = jnp.where(upper, gg[3], gg[0])
    ret_far = lax.ppermute(back_far, "morton", across)
    ret_down = lax.ppermute(gg[1], "morton", up)
    ret_up = lax.ppermute(gg[2], "morton", down)
    returned = jnp.concatenate([ret_far, ret_down, ret_up], axis=0)
    grad_node = gnode + jnp.dot(
        (ids[:, None] == rows_out[None, :]).astype(BF), returned, preferred_element_type=F32
    )

    total = lax.axis_size("dp") * peers * edge_feat.shape[1]
    wsum = reduce_all(wg) * (1.0 / jnp.sqrt(jnp.float32(total)))
    return (
        grad_node[None],
        gedge[None],
        wsum[0 : 3 * H],
        wsum[3 * H : 4 * H],
        wsum[7 * H],
        wsum[4 * H : 6 * H],
        wsum[6 * H : 7 * H],
        wsum[7 * H + 8],
    )


def solution(mesh):
    cells = P("dp", "morton", None)
    flat = P("dp", "morton")
    in_specs = (cells,) * 4 + (flat,) * 4 + (P(),) * 6
    out_specs = (cells, cells) + (P(),) * 6
    return jax.shard_map(
        on_device, mesh=mesh, in_specs=in_specs, out_specs=out_specs, check_vma=False
    )
```

time: 284 us -> 69.6 us (0.25)
  waiting for transfers between devices: 108 us -> 12.1 us
  other arithmetic: 58.2 us -> 1.94 us
  blocking collectives: 40.5 us -> 0 us
  local copies, waits for them, and re-layouts: 36.5 us -> 10.3 us
  Pallas kernels: 0 us -> 16.9 us
  between operations: 15.4 us -> 1.55 us
  starting transfers between devices: 14 us -> 25 us
  matrix products: 9.33 us -> 1.38 us
    psum x1 -> x0, waiting for transfers between devices: 108 us -> none  [on_device(): lax.psum((grads[3], grads[4], grads[5], grads[6], grads[7], grads[8]), ('...]
    psum x1 -> x0, blocking collectives: 40.5 us -> none  [on_device(): lax.psum((grads[3], grads[4], grads[5], grads[6], grads[7], grads[8]), ('...]
    scatter-add x7 -> x0, other arithmetic: 40.3 us -> none  [the longest x1 12.1 us: local_forward(): jax.ops.segment_sum(message.astype(edges.dtype), receiving, num_segments=...]
    gather x10 -> x0, local copies, waits for them, and re-layouts: 25.3 us -> none  [the longest x2 6.4 us: local_forward(): cells[receiving].astype(jnp.bfloat16)]
    ppermute x0 -> x17, starting transfers between devices: none -> 25 us  [the longest x11 11.7 us: flip(): return lax.ppermute(x, axis, [(i, i ^ by) for i in range(n)])]
    pallas_call x0 -> x1, Pallas kernels: none -> 16.9 us  [run_layer(): pl.pallas_call(layer_kernel, out_shape=shapes, in_specs=[pl.BlockSpec(mem...]
    all_to_all x2 -> x0, starting transfers between devices: 14 us -> none  [the longest x1 8.47 us: on_device(): lax.all_to_all(buffer, 'morton', split_axis=0, concat_axis=0, tiled=True)]
    ppermute x0 -> x17, waiting for transfers between devices: none -> 12.1 us  [the longest x1 5.89 us: on_device(): from_down = lax.ppermute(picked[2 * quota:], 'morton', up)]
  transfers between devices with their start and end apart: 3 -> 17, of which waited for: 1 -> 9; matrix products, arithmetic and copies ran while one was open for 12% -> 1% of each run, Pallas kernels for 0% -> 0%
where the time goes in v1:
time: 69.6 us; the launch traced here: 69.1 us
  starting transfers between devices  25 us (36%)
  Pallas kernels  16.9 us (24%)
  waiting for transfers between devices  12.1 us (17%)
  local copies, waits for them, and re-layouts  10.3 us (15%)
  other arithmetic  1.94 us (3%)
  between operations  1.55 us (2%)
  matrix products  1.38 us (2%)
    pallas_call x1, Pallas kernels, run_layer(): pl.pallas_call(layer_kernel, out_shape=shapes, in_specs=[pl.BlockSpec(mem...  16.9 us
    ppermute x11, starting transfers between devices, flip(): return lax.ppermute(x, axis, [(i, i ^ by) for i in range(n)])  11.7 us
    unnamed x24, local copies, waits for them, and re-layouts  7.73 us
    ppermute x1, starting transfers between devices, on_device(): from_up = lax.ppermute(picked[quota:2 * quota], 'morton', down)  7.01 us
    ppermute x1, waiting for transfers between devices, on_device(): from_down = lax.ppermute(picked[2 * quota:], 'morton', up)  5.89 us
    ppermute x11, waiting for transfers between devices, flip(): return lax.ppermute(x, axis, [(i, i ^ by) for i in range(n)])  5.38 us
    ppermute x1, starting transfers between devices, on_device(): ret_up = lax.ppermute(gg[2], 'morton', down)  3.67 us
    ppermute x1, starting transfers between devices, on_device(): ret_down = lax.ppermute(gg[1], 'morton', up)  1.95 us
  transfers between devices with their start and end apart: 17, of which 9 were waited for; matrix products, arithmetic and copies ran while one was open for 1% of the time, Pallas kernels for 0%

profile of v1, /device:TPU:0, one launch (start us, length us, event | category | flops | bytes accessed | tf_op | source)
XLA Modules:
  0.0 69.1 jit_solution(3945116409900414658)
XLA Ops:
  0.7 0.8 %fusion.15 = (s32[64]{0:T(128)S(1)}, s32[64]{0:T(128)S(1)}, s32[64]{0:T(128)S(1)}) fusion(pred[]{:T(512)S(6)} %ge.3, s32[1,256]{1,0:T(1,128)} %param.20), kind=kLoop, calls=%fused_computation.41 | loop fusion | flops 64 | bytes 1793 | tf_op jit(solution)/shard_map/jit(_where)/select_n | solution.py:284
  1.6 1.2 %convolution_convert_fusion = bf16[192,128]{1,0:T(8,128)(2,1)S(1)} fusion(s32[192]{0:T(256)S(1)} %pad_add_fusion, bf16[1,512,128]{2,1,0:T(8,128)(2,1)} %param.14), kind=kOutput, calls=%fused_computation | convolution fusion | flops 25288704 | bytes 180992 | tf_op jit(solution)/shard_map/dot_general | solution.py:287
  2.7 7.0 %collective-permute-start.1 = (bf16[64,128]{1,0:T(8,128)(2,1)S(1)}, bf16[64,128]{1,0:T(8,128)(2,1)S(1)}, u32[]{:S(2)}, u32[]{:S(2)}) collective-permute-start(bf16[64,128]{1,0:T(8,128)(2,1)S(1)} %get-tuple-element.34), channel_id=1, source_target_pairs={{0,30},{2,0},{4,2},{6,4},{8,6},{10,8},{12,10},{14,12},{16,14},{18,... | collective-permute-start | bytes 49160 | tf_op jit(solution)/shard_map/ppermute | solution.py:295
  10.4 0.8 %collective-permute-done.1 = bf16[64,128]{1,0:T(8,128)(2,1)S(1)} collective-permute-done((bf16[64,128]{1,0:T(8,128)(2,1)S(1)}, bf16[64,128]{1,0:T(8,128)(2,1)S(1)}, u32[]{:S(2)}, u32[]{:S(2)}) %collective-permute-start.1) | collective-permute-done | bytes 16416 | tf_op jit(solution)/shard_map/ppermute | solution.py:295
  11.2 5.9 %collective-permute-done.2 = bf16[64,128]{1,0:T(8,128)(2,1)S(1)} collective-permute-done((bf16[64,128]{1,0:T(8,128)(2,1)S(1)}, bf16[64,128]{1,0:T(8,128)(2,1)S(1)}, u32[]{:S(2)}, u32[]{:S(2)}) %collective-permute-start.2) | collective-permute-done | bytes 16416 | tf_op jit(solution)/shard_map/ppermute | solution.py:296
  17.1 0.7 copy-done.8
  17.8 1.0 %copy-done.1 = bf16[1,2048,128]{2,1,0:T(8,128)(2,1)S(1)} copy-done((bf16[1,2048,128]{2,1,0:T(8,128)(2,1)S(1)}, bf16[1,2048,128]{2,1,0:T(8,128)(2,1)}, u32[]{:S(2)}) %copy-start.1) | copy-done | bytes 524312
  18.9 0.9 %copy-done.2 = f32[384,128]{1,0:T(8,128)S(1)} copy-done((f32[384,128]{1,0:T(8,128)S(1)}, f32[384,128]{1,0:T(8,128)}, u32[]{:S(2)}) %copy-start.2) | copy-done | bytes 196632
  19.8 0.9 %copy-done.3 = bf16[1,512,128]{2,1,0:T(8,128)(2,1)S(1)} copy-done((bf16[1,512,128]{2,1,0:T(8,128)(2,1)S(1)}, bf16[1,512,128]{2,1,0:T(8,128)(2,1)}, u32[]{:S(2)}) %copy-start.3) | copy-done | bytes 131096
  20.7 0.9 %copy-done.4 = bf16[1,512,128]{2,1,0:T(8,128)(2,1)S(1)} copy-done((bf16[1,512,128]{2,1,0:T(8,128)(2,1)S(1)}, bf16[1,512,128]{2,1,0:T(8,128)(2,1)}, u32[]{:S(2)}) %copy-start.4) | copy-done | bytes 131096
  21.6 0.9 %copy-done.5 = f32[256,128]{1,0:T(8,128)S(1)} copy-done((f32[256,128]{1,0:T(8,128)S(1)}, f32[256,128]{1,0:T(8,128)}, u32[]{:S(2)}) %copy-start.5) | copy-done | bytes 131096
  22.5 0.8 %copy-done.6 = f32[128,128]{1,0:T(8,128)S(1)} copy-done((f32[128,128]{1,0:T(8,128)S(1)}, f32[128,128]{1,0:T(8,128)}, u32[]{:S(2)}) %copy-start.6) | copy-done | bytes 65560
  23.3 0.8 %copy-done.7 = f32[128,128]{1,0:T(8,128)S(1)} copy-done((f32[128,128]{1,0:T(8,128)S(1)}, f32[128,128]{1,0:T(8,128)}, u32[]{:S(2)}) %copy-start.7) | copy-done | bytes 65560
  24.2 0.7 %copy-done.9 = s32[1,2048]{1,0:T(1,128)S(1)} copy-done((s32[1,2048]{1,0:T(1,128)S(1)}, s32[1,2048]{1,0:T(1,128)}, u32[]{:S(2)}) %copy-start.9) | copy-done | bytes 8216
  24.9 16.9 %mesh_layer.1 = (f32[512,128]{1,0:T(8,128)S(1)}, f32[2048,128]{1,0:T(8,128)}, bf16[256,128]{1,0:T(8,128)(2,1)S(1)}, f32[960,128]{1,0:T(8,128)S(1)}) custom-call(s32[1,1]{1,0:T(1,128)S(6)} %copy.22.count_ref, bf16[512,128]{1,0:T(8,128)(2,1)S(1)} %bitcast.58, bf16[256,128]{1,0:T(8,128)(2,1)S(1)} %pad_maximum_fusion.2.gh_ref, bf16[2048,128]{1,0:T(8,128)(2,1)S(1)} %bitcast.56, ...), custom_call_target="tpu_custom_call" | custom-call | flops 2415919104 | bytes 3145728 | tf_op jit(solution)/shard_map/mesh_layer/pallas_call | solution.py:196
  41.9 1.3 %collective-permute-done.6 = bf16[480,128]{1,0:T(8,128)(2,1)S(1)} collective-permute-done((bf16[480,128]{1,0:T(8,128)(2,1)S(1)}, bf16[480,128]{1,0:T(8,128)(2,1)S(1)}, u32[]{:S(2)}, u32[]{:S(2)}) %collective-permute-start.6) | collective-permute-done | bytes 122912 | tf_op jit(solution)/shard_map/ppermute | solution.py:212
  43.4 3.4 %collective-permute-start.8 = (bf16[120,128]{1,0:T(8,128)(2,1)S(1)}, bf16[120,128]{1,0:T(8,128)(2,1)S(1)}, u32[]{:S(2)}, u32[]{:S(2)}) collective-permute-start(bf16[120,128]{1,0:T(8,128)(2,1)S(1)} %get-tuple-element.30), channel_id=1, source_target_pairs={{0,4},{2,6},{4,0},{6,2},{8,12},{10,14},{12,8},{14,10},{16,20},{18,... | collective-permute-start | bytes 92168 | tf_op jit(solution)/shard_map/ppermute | solution.py:212
  47.2 1.0 %collective-permute-done.9 = bf16[120,128]{1,0:T(8,128)(2,1)S(1)} collective-permute-done((bf16[120,128]{1,0:T(8,128)(2,1)S(1)}, bf16[120,128]{1,0:T(8,128)(2,1)S(1)}, u32[]{:S(2)}, u32[]{:S(2)}) %collective-permute-start.9) | collective-permute-done | bytes 30752 | tf_op jit(solution)/shard_map/ppermute | solution.py:212
  48.7 2.2 %collective-permute-start.12 = (bf16[120,128]{1,0:T(8,128)(2,1)S(1)}, bf16[120,128]{1,0:T(8,128)(2,1)S(1)}, u32[]{:S(2)}, u32[]{:S(2)}) collective-permute-start(bf16[120,128]{1,0:T(8,128)(2,1)S(1)} %fusion.9), channel_id=1, source_target_pairs={{0,24},{2,26},{4,28},{6,30},{8,16},{10,18},{12,20},{14,22},{16,8},... | collective-permute-start | bytes 92168 | tf_op jit(solution)/shard_map/ppermute | solution.py:212
  50.9 2.3 %collective-permute-start.10 = (bf16[120,128]{1,0:T(8,128)(2,1)S(1)}, bf16[120,128]{1,0:T(8,128)(2,1)S(1)}, u32[]{:S(2)}, u32[]{:S(2)}) collective-permute-start(bf16[120,128]{1,0:T(8,128)(2,1)S(1)} %fusion.9), channel_id=1, source_target_pairs={{0,8},{2,10},{4,12},{6,14},{8,0},{10,2},{12,4},{14,6},{16,24},{18,... | collective-permute-start | bytes 92168 | tf_op jit(solution)/shard_map/ppermute | solution.py:212
  53.2 0.7 %collective-permute-start.3 = (bf16[64,128]{1,0:T(8,128)(2,1)S(1)}, bf16[64,128]{1,0:T(8,128)(2,1)S(1)}, u32[]{:S(2)}, u32[]{:S(2)}) collective-permute-start(bf16[64,128]{1,0:T(8,128)(2,1)S(1)} %get-tuple-element.31), channel_id=1, source_target_pairs={{0,16},{2,18},{4,20},{6,22},{8,24},{10,26},{12,28},{14,30},{16,0},... | collective-permute-start | bytes 49160 | tf_op jit(solution)/shard_map/ppermute | solution.py:306
  53.9 1.9 %collective-permute-start.4 = (bf16[64,128]{1,0:T(8,128)(2,1)S(1)}, bf16[64,128]{1,0:T(8,128)(2,1)S(1)}, u32[]{:S(2)}, u32[]{:S(2)}) collective-permute-start(bf16[64,128]{1,0:T(8,128)(2,1)S(1)} %get-tuple-element.32), channel_id=1, source_target_pairs={{0,2},{2,4},{4,6},{6,8},{8,10},{10,12},{12,14},{14,16},{16,18},{18... | collective-permute-start | bytes 49160 | tf_op jit(solution)/shard_map/ppermute | solution.py:307
  55.8 3.7 %collective-permute-start.5 = (bf16[64,128]{1,0:T(8,128)(2,1)S(1)}, bf16[64,128]{1,0:T(8,128)(2,1)S(1)}, u32[]{:S(2)}, u32[]{:S(2)}) collective-permute-start(bf16[64,128]{1,0:T(8,128)(2,1)S(1)} %get-tuple-element.33), channel_id=1, source_target_pairs={{0,30},{2,0},{4,2},{6,4},{8,6},{10,8},{12,10},{14,12},{16,14},{18,... | collective-permute-start | bytes 49160 | tf_op jit(solution)/shard_map/ppermute | solution.py:308
  59.7 3.4 %collective-permute-start.13 = (bf16[120,128]{1,0:T(8,128)(2,1)S(1)}, bf16[120,128]{1,0:T(8,128)(2,1)S(1)}, u32[]{:S(2)}, u32[]{:S(2)}) collective-permute-start(bf16[120,128]{1,0:T(8,128)(2,1)S(1)} %add_convert_fusion), channel_id=1, source_target_pairs={{0,2},{2,0},{4,6},{6,4},{8,10},{10,8},{12,14},{14,12},{16,18},{18,... | collective-permute-start | bytes 92168 | tf_op jit(solution)/shard_map/ppermute | solution.py:212
  63.3 1.1 %collective-permute-done.15 = bf16[120,128]{1,0:T(8,128)(2,1)S(1)} collective-permute-done((bf16[120,128]{1,0:T(8,128)(2,1)S(1)}, bf16[120,128]{1,0:T(8,128)(2,1)S(1)}, u32[]{:S(2)}, u32[]{:S(2)}) %collective-permute-start.15) | collective-permute-done | bytes 30752 | tf_op jit(solution)/shard_map/ppermute | solution.py:212
  64.4 0.6 collective-permute-done.13
  65.1 0.7 %add_bitcast_fusion = f32[1,512,128]{2,1,0:T(8,128)} fusion(f32[512,128]{1,0:T(8,128)S(1)} %get-tuple-element.12, f32[512,128]{1,0:T(8,128)S(1)} %fusion), kind=kLoop, calls=%fused_computation.9 | loop fusion | flops 65536 | bytes 786432 | tf_op jit(solution)/shard_map/broadcast_in_dim | solution.py:317
  65.9 0.6 collective-permute-done.16
  66.6 0.5 slice_bitcast_fusion
  67.1 0.7 slice.82
  67.8 0.7 fusion.19
  68.4 0.7 slice.79
  (50 shorter events, 2.0 us)
Async XLA Ops:
  0.6 16.5 %copy-start = (bf16[1,2048,128]{2,1,0:T(8,128)(2,1)S(1)}, bf16[1,2048,128]{2,1,0:T(8,128)(2,1)}, u32[]{:S(2)}) copy-start(bf16[1,2048,128]{2,1,0:T(8,128)(2,1)} %param.15) | copy-start | bytes 1572868
  2.7 8.5 %collective-permute-start.1 = (bf16[64,128]{1,0:T(8,128)(2,1)S(1)}, bf16[64,128]{1,0:T(8,128)(2,1)S(1)}, u32[]{:S(2)}, u32[]{:S(2)}) collective-permute-start(bf16[64,128]{1,0:T(8,128)(2,1)S(1)} %get-tuple-element.34), channel_id=1, source_target_pairs={{0,30},{2,0},{4,2},{6,4},{8,6},{10,8},{12,10},{14,12},{16,14},{18,... | collective-permute-start | bytes 49160 | tf_op jit(solution)/shard_map/ppermute | solution.py:295
  9.8 7.3 %collective-permute-start.2 = (bf16[64,128]{1,0:T(8,128)(2,1)S(1)}, bf16[64,128]{1,0:T(8,128)(2,1)S(1)}, u32[]{:S(2)}, u32[]{:S(2)}) collective-permute-start(bf16[64,128]{1,0:T(8,128)(2,1)S(1)} %get-tuple-element.35), channel_id=1, source_target_pairs={{0,2},{2,4},{4,6},{6,8},{8,10},{10,12},{12,14},{14,16},{16,18},{18... | collective-permute-start | bytes 49160 | tf_op jit(solution)/shard_map/ppermute | solution.py:296
  9.8 7.3 %collective-permute-start = (bf16[64,128]{1,0:T(8,128)(2,1)S(1)}, bf16[64,128]{1,0:T(8,128)(2,1)S(1)}, u32[]{:S(2)}, u32[]{:S(2)}) collective-permute-start(bf16[64,128]{1,0:T(8,128)(2,1)S(1)} %get-tuple-element.36), channel_id=1, source_target_pairs={{0,16},{2,18},{4,20},{6,22},{8,24},{10,26},{12,28},{14,30},{16,0},... | collective-permute-start | bytes 49160 | tf_op jit(solution)/shard_map/ppermute | solution.py:294
  17.1 0.7 %copy-start.8 = (s32[1,2048]{1,0:T(1,128)S(1)}, s32[1,2048]{1,0:T(1,128)}, u32[]{:S(2)}) copy-start(s32[1,2048]{1,0:T(1,128)} %snd_ref.1) | copy-start | bytes 24580
  17.1 0.7 copy-start.10
  17.1 0.7 copy-start.11
  17.8 1.0 %copy-start.1 = (bf16[1,2048,128]{2,1,0:T(8,128)(2,1)S(1)}, bf16[1,2048,128]{2,1,0:T(8,128)(2,1)}, u32[]{:S(2)}) copy-start(bf16[1,2048,128]{2,1,0:T(8,128)(2,1)} %param.17) | copy-start | bytes 1572868
  18.9 0.9 %copy-start.2 = (f32[384,128]{1,0:T(8,128)S(1)}, f32[384,128]{1,0:T(8,128)}, u32[]{:S(2)}) copy-start(f32[384,128]{1,0:T(8,128)} %w1_ref.1) | copy-start | bytes 589828
  19.8 0.9 %copy-start.3 = (bf16[1,512,128]{2,1,0:T(8,128)(2,1)S(1)}, bf16[1,512,128]{2,1,0:T(8,128)(2,1)}, u32[]{:S(2)}) copy-start(bf16[1,512,128]{2,1,0:T(8,128)(2,1)} %param.14) | copy-start | bytes 393220
  20.7 0.9 %copy-start.4 = (bf16[1,512,128]{2,1,0:T(8,128)(2,1)S(1)}, bf16[1,512,128]{2,1,0:T(8,128)(2,1)}, u32[]{:S(2)}) copy-start(bf16[1,512,128]{2,1,0:T(8,128)(2,1)} %param.16) | copy-start | bytes 393220
  21.6 0.9 %copy-start.5 = (f32[256,128]{1,0:T(8,128)S(1)}, f32[256,128]{1,0:T(8,128)}, u32[]{:S(2)}) copy-start(f32[256,128]{1,0:T(8,128)} %nw1_ref.1) | copy-start | bytes 393220
  22.5 0.8 %copy-start.6 = (f32[128,128]{1,0:T(8,128)S(1)}, f32[128,128]{1,0:T(8,128)}, u32[]{:S(2)}) copy-start(f32[128,128]{1,0:T(8,128)} %w2_ref.1) | copy-start | bytes 196612
  23.3 0.8 %copy-start.7 = (f32[128,128]{1,0:T(8,128)S(1)}, f32[128,128]{1,0:T(8,128)}, u32[]{:S(2)}) copy-start(f32[128,128]{1,0:T(8,128)} %nw2_ref.1) | copy-start | bytes 196612
  24.2 0.7 %copy-start.9 = (s32[1,2048]{1,0:T(1,128)S(1)}, s32[1,2048]{1,0:T(1,128)}, u32[]{:S(2)}) copy-start(s32[1,2048]{1,0:T(1,128)} %rcv_ref.1) | copy-start | bytes 24580
  41.8 1.4 %collective-permute-start.6 = (bf16[480,128]{1,0:T(8,128)(2,1)S(1)}, bf16[480,128]{1,0:T(8,128)(2,1)S(1)}, u32[]{:S(2)}, u32[]{:S(2)}) collective-permute-start(bf16[480,128]{1,0:T(8,128)(2,1)S(1)} %dynamic-slice_bitcast_fusion), channel_id=1, source_target_pairs={{0,1},{1,0},{2,3},{3,2},{4,5},{5,4},{6,7},{7,6},{8,9},{9,8},{10,11... | collective-permute-start | bytes 368648 | tf_op jit(solution)/shard_map/ppermute | solution.py:212
  43.3 4.0 %collective-permute-start.7 = (bf16[120,128]{1,0:T(8,128)(2,1)S(1)}, bf16[120,128]{1,0:T(8,128)(2,1)S(1)}, u32[]{:S(2)}, u32[]{:S(2)}) collective-permute-start(bf16[120,128]{1,0:T(8,128)(2,1)S(1)} %get-tuple-element.28), channel_id=1, source_target_pairs={{0,2},{2,0},{4,6},{6,4},{8,10},{10,8},{12,14},{14,12},{16,18},{18,... | collective-permute-start | bytes 92168 | tf_op jit(solution)/shard_map/ppermute | solution.py:212
  43.3 4.9 %collective-permute-start.9 = (bf16[120,128]{1,0:T(8,128)(2,1)S(1)}, bf16[120,128]{1,0:T(8,128)(2,1)S(1)}, u32[]{:S(2)}, u32[]{:S(2)}) collective-permute-start(bf16[120,128]{1,0:T(8,128)(2,1)S(1)} %get-tuple-element.29), channel_id=1, source_target_pairs={{0,6},{2,4},{4,2},{6,0},{8,14},{10,12},{12,10},{14,8},{16,22},{18,... | collective-permute-start | bytes 92168 | tf_op jit(solution)/shard_map/ppermute | solution.py:212
  43.4 5.3 %collective-permute-start.8 = (bf16[120,128]{1,0:T(8,128)(2,1)S(1)}, bf16[120,128]{1,0:T(8,128)(2,1)S(1)}, u32[]{:S(2)}, u32[]{:S(2)}) collective-permute-start(bf16[120,128]{1,0:T(8,128)(2,1)S(1)} %get-tuple-element.30), channel_id=1, source_target_pairs={{0,4},{2,6},{4,0},{6,2},{8,12},{10,14},{12,8},{14,10},{16,20},{18,... | collective-permute-start | bytes 92168 | tf_op jit(solution)/shard_map/ppermute | solution.py:212
  48.7 7.1 %collective-permute-start.12 = (bf16[120,128]{1,0:T(8,128)(2,1)S(1)}, bf16[120,128]{1,0:T(8,128)(2,1)S(1)}, u32[]{:S(2)}, u32[]{:S(2)}) collective-permute-start(bf16[120,128]{1,0:T(8,128)(2,1)S(1)} %fusion.9), channel_id=1, source_target_pairs={{0,24},{2,26},{4,28},{6,30},{8,16},{10,18},{12,20},{14,22},{16,8},... | collective-permute-start | bytes 92168 | tf_op jit(solution)/shard_map/ppermute | solution.py:212
  50.9 8.6 %collective-permute-start.11 = (bf16[120,128]{1,0:T(8,128)(2,1)S(1)}, bf16[120,128]{1,0:T(8,128)(2,1)S(1)}, u32[]{:S(2)}, u32[]{:S(2)}) collective-permute-start(bf16[120,128]{1,0:T(8,128)(2,1)S(1)} %fusion.9), channel_id=1, source_target_pairs={{0,16},{2,18},{4,20},{6,22},{8,24},{10,26},{12,28},{14,30},{16,0},... | collective-permute-start | bytes 92168 | tf_op jit(solution)/shard_map/ppermute | solution.py:212
  50.9 8.6 %collective-permute-start.10 = (bf16[120,128]{1,0:T(8,128)(2,1)S(1)}, bf16[120,128]{1,0:T(8,128)(2,1)S(1)}, u32[]{:S(2)}, u32[]{:S(2)}) collective-permute-start(bf16[120,128]{1,0:T(8,128)(2,1)S(1)} %fusion.9), channel_id=1, source_target_pairs={{0,8},{2,10},{4,12},{6,14},{8,0},{10,2},{12,4},{14,6},{16,24},{18,... | collective-permute-start | bytes 92168 | tf_op jit(solution)/shard_map/ppermute | solution.py:212
  53.2 6.5 %collective-permute-start.3 = (bf16[64,128]{1,0:T(8,128)(2,1)S(1)}, bf16[64,128]{1,0:T(8,128)(2,1)S(1)}, u32[]{:S(2)}, u32[]{:S(2)}) collective-permute-start(bf16[64,128]{1,0:T(8,128)(2,1)S(1)} %get-tuple-element.31), channel_id=1, source_target_pairs={{0,16},{2,18},{4,20},{6,22},{8,24},{10,26},{12,28},{14,30},{16,0},... | collective-permute-start | bytes 49160 | tf_op jit(solution)/shard_map/ppermute | solution.py:306
  53.9 9.2 %collective-permute-start.4 = (bf16[64,128]{1,0:T(8,128)(2,1)S(1)}, bf16[64,128]{1,0:T(8,128)(2,1)S(1)}, u32[]{:S(2)}, u32[]{:S(2)}) collective-permute-start(bf16[64,128]{1,0:T(8,128)(2,1)S(1)} %get-tuple-element.32), channel_id=1, source_target_pairs={{0,2},{2,4},{4,6},{6,8},{8,10},{10,12},{12,14},{14,16},{16,18},{18... | collective-permute-start | bytes 49160 | tf_op jit(solution)/shard_map/ppermute | solution.py:307
  55.8 7.3 %collective-permute-start.5 = (bf16[64,128]{1,0:T(8,128)(2,1)S(1)}, bf16[64,128]{1,0:T(8,128)(2,1)S(1)}, u32[]{:S(2)}, u32[]{:S(2)}) collective-permute-start(bf16[64,128]{1,0:T(8,128)(2,1)S(1)} %get-tuple-element.33), channel_id=1, source_target_pairs={{0,30},{2,0},{4,2},{6,4},{8,6},{10,8},{12,10},{14,12},{16,14},{18,... | collective-permute-start | bytes 49160 | tf_op jit(solution)/shard_map/ppermute | solution.py:308
  59.5 4.9 %collective-permute-start.15 = (bf16[120,128]{1,0:T(8,128)(2,1)S(1)}, bf16[120,128]{1,0:T(8,128)(2,1)S(1)}, u32[]{:S(2)}, u32[]{:S(2)}) collective-permute-start(bf16[120,128]{1,0:T(8,128)(2,1)S(1)} %add_convert_fusion), channel_id=1, source_target_pairs={{0,6},{2,4},{4,2},{6,0},{8,14},{10,12},{12,10},{14,8},{16,22},{18,... | collective-permute-start | bytes 92168 | tf_op jit(solution)/shard_map/ppermute | solution.py:212
  59.6 4.8 %collective-permute-start.14 = (bf16[120,128]{1,0:T(8,128)(2,1)S(1)}, bf16[120,128]{1,0:T(8,128)(2,1)S(1)}, u32[]{:S(2)}, u32[]{:S(2)}) collective-permute-start(bf16[120,128]{1,0:T(8,128)(2,1)S(1)} %add_convert_fusion), channel_id=1, source_target_pairs={{0,4},{2,6},{4,0},{6,2},{8,12},{10,14},{12,8},{14,10},{16,20},{18,... | collective-permute-start | bytes 92168 | tf_op jit(solution)/shard_map/ppermute | solution.py:212
  59.7 5.3 %collective-permute-start.13 = (bf16[120,128]{1,0:T(8,128)(2,1)S(1)}, bf16[120,128]{1,0:T(8,128)(2,1)S(1)}, u32[]{:S(2)}, u32[]{:S(2)}) collective-permute-start(bf16[120,128]{1,0:T(8,128)(2,1)S(1)} %add_convert_fusion), channel_id=1, source_target_pairs={{0,2},{2,0},{4,6},{6,4},{8,10},{10,8},{12,14},{14,12},{16,18},{18,... | collective-permute-start | bytes 92168 | tf_op jit(solution)/shard_map/ppermute | solution.py:212
  65.0 1.4 %collective-permute-start.16 = (bf16[480,128]{1,0:T(8,128)(2,1)S(1)}, bf16[480,128]{1,0:T(8,128)(2,1)S(1)}, u32[]{:S(2)}, u32[]{:S(2)}) collective-permute-start(bf16[480,128]{1,0:T(8,128)(2,1)S(1)} %get-tuple-element.22), channel_id=1, source_target_pairs={{0,1},{1,0},{2,3},{3,2},{4,5},{5,4},{6,7},{7,6},{8,9},{9,8},{10,11... | collective-permute-start | bytes 368648 | tf_op jit(solution)/shard_map/ppermute | solution.py:212

commit v2 on v1

v2 whole, which is shorter than its diff:
```python
import functools

import jax
import jax.numpy as jnp
from jax import lax
from jax.experimental import pallas as pl
from jax.experimental.pallas import tpu as pltpu
from jax.sharding import PartitionSpec as P

BF = jnp.bfloat16
F32 = jnp.float32
EPS = 1e-05
PRE_CHUNK = 1024
FWD_CHUNK = 2048
BWD_CHUNK = 2048


def mm(a, b):
    return lax.dot_general(a, b, (((1,), (0,)), ((), ())), preferred_element_type=F32)


def mm_rt(a, b):
    return lax.dot_general(a, b, (((1,), (1,)), ((), ())), preferred_element_type=F32)


def mm_lt(a, b):
    return lax.dot_general(a, b, (((0,), (0,)), ((), ())), preferred_element_type=F32)


def silu_parts(a):
    sig = 0.5 * jnp.tanh(0.5 * a) + 0.5
    act = a * sig
    return act, sig + act * (1.0 - sig)


def norm_parts(b):
    center = b - jnp.mean(b, axis=-1, keepdims=True)
    inv = lax.rsqrt(jnp.mean(center * center, axis=-1, keepdims=True) + EPS)
    return center * inv, inv


def norm_back(g, nrm, inv):
    return inv * (
        g
        - jnp.mean(g, axis=-1, keepdims=True)
        - nrm * jnp.mean(g * nrm, axis=-1, keepdims=True)
    )


def one_hot_cols(col, size):
    lane = lax.broadcasted_iota(jnp.int32, (col.shape[0], size), 1)
    return jnp.where(jnp.tile(col, (1, size // col.shape[1])) == lane, 1.0, 0.0).astype(BF)


def one_hot_rows(row, size):
    sub = lax.broadcasted_iota(jnp.int32, (size, row.shape[1]), 0)
    return jnp.where(row == sub, 1.0, 0.0).astype(BF)


def my_place():
    j = lax.axis_index("morton")
    return (j >= lax.axis_size("morton") // 2).astype(jnp.int32), j % 2


def start_all(pairs, sems):
    copies = [pltpu.make_async_copy(src, dst, sems.at[i]) for i, (src, dst) in enumerate(pairs)]
    for c in copies:
        c.start()
    return copies


def spread(row_refs, tmat, outs):
    tmat[...] = jnp.zeros_like(tmat)
    at = 0
    for ref in row_refs:
        for r in range(ref.shape[1] // 128):
            tmat[at : at + 1, :] = ref[:, r * 128 : (r + 1) * 128]
            at += 1
    turned = jnp.transpose(tmat[...])
    at = 0
    for ref, out in zip(row_refs, outs):
        for r in range(ref.shape[1] // 128):
            out[r * 128 : (r + 1) * 128, :] = jnp.broadcast_to(turned[:, at : at + 1], (128, 128))
            at += 1


def pack_kernel(rows_hbm, h_hbm, far_ref, one_ref, two_ref, rows_s, h_s, tmat, col, got, sems):
    copies = start_all([(rows_hbm, rows_s), (h_hbm, h_s)], sems)
    copies[0].wait()
    spread([rows_s], tmat, [col])
    hot = one_hot_cols(col[...], h_s.shape[0])
    copies[1].wait()
    got[...] = mm(hot, h_s[...])
    upper, odd = my_place()
    q = far_ref.shape[0]
    far_ref[...] = got[pl.ds(pl.multiple_of((1 - upper) * 3 * q, q), q), :].astype(BF)
    one_ref[...] = got[pl.ds(pl.multiple_of((2 - odd) * q, q), q), :].astype(BF)
    two_ref[...] = got[pl.ds(pl.multiple_of((1 + odd) * q, q), q), :].astype(BF)


def pre_kernel(
    h_hbm, e_hbm, snd_hbm, rcv_hbm, w1_hbm,
    part_ref, pg_ref, pr_ref, ptr_ref, pts_ref,
    h_s, e_s, snd_s, rcv_s, w1_s, tmat, col_s, col_r, rhs, sems,
):
    copies = start_all(
        [(snd_hbm, snd_s), (rcv_hbm, rcv_s), (h_hbm, h_s), (w1_hbm, w1_s), (e_hbm, e_s)], sems
    )
    C, H = h_s.shape
    E = e_s.shape[0]
    G = pg_ref.shape[1]
    copies[0].wait()
    copies[1].wait()
    spread([snd_s, rcv_s], tmat, [col_s, col_r])
    copies[2].wait()
    copies[3].wait()
    w1 = w1_s[...].astype(BF)
    h = h_s[...]
    rhs[0:H, :] = w1[:H]
    rhs[H : H + C, :] = mm(h, w1[H : 2 * H]).astype(BF)
    rhs[H + C :, :] = mm(h, w1[2 * H :]).astype(BF)
    copies[4].wait()

    def step(i, carry):
        at = pl.ds(pl.multiple_of(i * PRE_CHUNK, PRE_CHUNK), PRE_CHUNK)
        hot = one_hot_cols(col_s[at, :], C + G)
        p_r = one_hot_cols(col_r[at, :], C)
        pg_ref[at, :] = hot[:, C:]
        pr_ref[at, :] = p_r
        part_ref[at, :] = mm(jnp.concatenate([e_s[at, :], hot[:, :C], p_r], axis=1), rhs[...])
        ptr_ref[:, at] = one_hot_rows(rcv_s[:, at], C)
        pts_ref[:, at] = one_hot_rows(snd_s[:, at], C + G)
        return carry

    lax.fori_loop(0, E // PRE_CHUNK, step, 0)


def main_kernel(
    count_ref, part_ref, pg_ref, pr_ref, ptr_ref, pts_ref, far_ref, one_ref, two_ref,
    h_hbm, e_hbm, cn_hbm, ce_hbm, w1_hbm, w2_hbm, eg_hbm, nw1_hbm, nw2_hbm, ng_hbm,
    gnode_ref, gedge_hbm, bfar_ref, bone_ref, btwo_ref, wmine_ref, woth_ref,
    h_s, e_s, cn_s, ce_s, w1_s, w2_s, eg_s, nw1_s, nw2_s, ng_s,
    gh_s, p_s, dsil_s, nrm_s, inv_s, agg, dagg_s, db_s, da_s, gedge_s, wg, dgh, sems, out_sems,
):
    copies = start_all(
        [
            (w1_hbm, w1_s), (w2_hbm, w2_s), (eg_hbm, eg_s), (e_hbm, e_s), (h_hbm, h_s),
            (nw1_hbm, nw1_s), (nw2_hbm, nw2_s), (ng_hbm, ng_s), (cn_hbm, cn_s), (ce_hbm, ce_s),
        ],
        sems,
    )
    C, H = h_s.shape
    E = e_s.shape[0]
    G = pg_ref.shape[1]
    q = G // 4
    count = count_ref[0, 0]
    upper, odd = my_place()
    gh_s[0:q, :] = far_ref[...]
    gh_s[3 * q :, :] = far_ref[...]
    gh_s[pl.ds(pl.multiple_of((1 + odd) * q, q), q), :] = one_ref[...]
    gh_s[pl.ds(pl.multiple_of((2 - odd) * q, q), q), :] = two_ref[...]
    for c in copies[:4]:
        c.wait()
    w1 = w1_s[...].astype(BF)
    w1e, w1s, w1r = w1[:H], w1[H : 2 * H], w1[2 * H :]
    w2 = w2_s[...].astype(BF)
    egain = eg_s[...]
    gtab = mm(gh_s[...], w1s).astype(BF)
    agg[...] = jnp.zeros_like(agg)

    def fwd(i, carry):
        at = pl.ds(pl.multiple_of(i * FWD_CHUNK, FWD_CHUNK), FWD_CHUNK)
        act, dsil = silu_parts(part_ref[at, :] + mm(pg_ref[at, :], gtab))
        p = act.astype(BF)
        p_s[at, :] = p
        dsil_s[at, :] = dsil
        nrm, inv = norm_parts(mm(p, w2))
        nrm_s[at, :] = nrm
        inv_s[at, :] = inv
        rowid = lax.broadcasted_iota(jnp.int32, (FWD_CHUNK, H), 0) + i * FWD_CHUNK
        msg = jnp.where(rowid < count, e_s[at, :].astype(F32) + nrm * egain, 0.0).astype(BF)
        agg[...] += mm(ptr_ref[:, at], msg)
        return carry

    lax.fori_loop(0, E // FWD_CHUNK, fwd, 0)

    for c in copies[4:]:
        c.wait()
    h = h_s[...]
    nw1 = nw1_s[...].astype(BF)
    nw2 = nw2_s[...].astype(BF)
    cn = cn_s[...].astype(F32)
    aggb = agg[...].astype(BF)
    y = jnp.concatenate([h, aggb], axis=1)
    act, dsil = silu_parts(mm(y, nw1))
    r = act.astype(BF)
    nrm, inv = norm_parts(mm(r, nw2))
    ds = norm_back(cn * ng_s[...], nrm, inv).astype(BF)
    dc = (mm_rt(ds, nw2) * dsil).astype(BF)
    dy = mm_rt(dc, nw1)
    dagg_s[...] = dy[:, H:].astype(BF)
    gnode_ref[...] = cn + dy[:, :H]
    wg[4 * H : 6 * H, :] = mm_lt(y, dc)
    wg[6 * H : 7 * H, :] = mm_lt(r, ds)
    wg[7 * H :, :] = jnp.zeros((wg.shape[0] - 7 * H, H), F32)
    wg[7 * H + 8 : 7 * H + 9, :] = jnp.sum(cn * nrm, axis=0, keepdims=True)

    def out_copy(i):
        at = pl.ds(pl.multiple_of(i * BWD_CHUNK, BWD_CHUNK), BWD_CHUNK)
        return pltpu.make_async_copy(gedge_s.at[at, :], gedge_hbm.at[at, :], out_sems.at[i])

    gain_sum = jnp.zeros((8, H), F32)
    for i in range(E // BWD_CHUNK):
        at = pl.ds(i * BWD_CHUNK, BWD_CHUNK)
        dmsg = mm(pr_ref[at, :], dagg_s[...])
        rowid = lax.broadcasted_iota(jnp.int32, (BWD_CHUNK, H), 0) + i * BWD_CHUNK
        alive = rowid < count
        ce = ce_s[at, :].astype(F32)
        full = ce + dmsg
        d = jnp.where(alive, full, 0.0)
        nrm = nrm_s[at, :]
        gain_sum = gain_sum + jnp.sum((d * nrm).reshape(BWD_CHUNK // 8, 8, H), axis=0)
        db = norm_back(d * egain, nrm, inv_s[at, :]).astype(BF)
        db_s[at, :] = db
        da = (mm_rt(db, w2) * dsil_s[at, :]).astype(BF)
        da_s[at, :] = da
        gedge_s[at, :] = jnp.where(alive, full, ce) + mm_rt(da, w1e)
        out_copy(i).start()

    wg[7 * H : 7 * H + 1, :] = jnp.sum(gain_sum, axis=0, keepdims=True)
    da = da_s[...]
    gs = mm(pts_ref[...], da).astype(BF)
    gr = mm(ptr_ref[...], da).astype(BF)
    wg[3 * H : 4 * H, :] = mm_lt(p_s[...], db_s[...])
    wg[0:H, :] = mm_lt(e_s[...], da)
    wg[H : 2 * H, :] = mm_lt(jnp.concatenate([h, gh_s[...]], axis=0), gs)
    wg[2 * H : 3 * H, :] = mm_lt(h, gr)
    dt = mm_rt(gs, w1s)
    gnode_ref[...] += dt[:C] + mm_rt(gr, w1r)
    dgh[...] = dt[C:]
    bfar_ref[...] = dgh[pl.ds(pl.multiple_of(upper * 3 * q, q), q), :].astype(BF)
    bone_ref[...] = dgh[pl.ds(pl.multiple_of((1 + odd) * q, q), q), :].astype(BF)
    btwo_ref[...] = dgh[pl.ds(pl.multiple_of((2 - odd) * q, q), q), :].astype(BF)
    core = lax.axis_index("dp")
    part = wmine_ref.shape[0]
    wmine_ref[...] = wg[pl.ds(pl.multiple_of(core * part, 8), part), :].astype(BF)
    woth_ref[...] = wg[pl.ds(pl.multiple_of((1 - core) * part, 8), part), :].astype(BF)
    for i in range(E // BWD_CHUNK):
        out_copy(i).wait()


def node_kernel(rows_hbm, gnode_ref, far_ref, one_ref, two_ref, out_ref, rows_s, ret, sems):
    copies = start_all([(rows_hbm, rows_s)], sems)
    upper, odd = my_place()
    q = far_ref.shape[0]
    ret[...] = jnp.zeros_like(ret)
    ret[pl.ds(pl.multiple_of((1 - upper) * 3 * q, q), q), :] = far_ref[...]
    ret[pl.ds(pl.multiple_of((2 - odd) * q, q), q), :] = one_ref[...]
    ret[pl.ds(pl.multiple_of((1 + odd) * q, q), q), :] = two_ref[...]
    copies[0].wait()
    out_ref[...] = gnode_ref[...] + mm(one_hot_rows(rows_s[...], out_ref.shape[0]), ret[...])


def unpack_kernel(factor, mine_ref, oth_ref, g1, g2, gg, gn1, gn2, gng, wg):
    core = lax.axis_index("dp")
    part, H = mine_ref.shape
    wg[pl.ds(pl.multiple_of(core * part, 8), part), :] = mine_ref[...].astype(F32) * factor
    wg[pl.ds(pl.multiple_of((1 - core) * part, 8), part), :] = oth_ref[...].astype(F32) * factor
    g1[...] = wg[0 : 3 * H, :]
    g2[...] = wg[3 * H : 4 * H, :]
    gn1[...] = wg[4 * H : 6 * H, :]
    gn2[...] = wg[6 * H : 7 * H, :]
    gg[...] = wg[7 * H : 7 * H + 1, :]
    gng[...] = wg[7 * H + 8 : 7 * H + 9, :]


HBM = pl.BlockSpec(memory_space=pltpu.HBM)
VM = pl.BlockSpec(memory_space=pltpu.VMEM)
SM = pl.BlockSpec(memory_space=pltpu.SMEM)
MIB = 1024 * 1024


def like(x):
    return pltpu.VMEM(x.shape, x.dtype)


def sds(shape, dtype):
    return jax.ShapeDtypeStruct(shape, dtype)


def call(kernel, name, outs, in_specs, out_specs, scratch, flops, nbytes, limit):
    return pl.pallas_call(
        kernel,
        out_shape=outs,
        in_specs=in_specs,
        out_specs=out_specs,
        scratch_shapes=scratch,
        compiler_params=pltpu.CompilerParams(vmem_limit_bytes=limit * MIB),
        cost_estimate=pl.CostEstimate(flops=flops, bytes_accessed=nbytes, transcendentals=0),
        name=name,
    )


def flip(x, axis, by):
    n = lax.axis_size(axis)
    return lax.ppermute(x, axis, [(i, i ^ by) for i in range(n)])


def cross_pairs(x):
    n = lax.axis_size("morton")
    return lax.ppermute(x, "morton", [(i, (i + 1) % n if i % 2 else (i - 1) % n) for i in range(n)])


def pick(x, k):
    return lax.dynamic_index_in_dim(x, k, 0, keepdims=False)


def tree_sum(parts):
    while len(parts) > 1:
        parts = [parts[i] + parts[i + 1] for i in range(0, len(parts), 2)]
    return parts[0]


def stages_of(n):
    out = []
    stride = 1
    while stride < n:
        w = 4 if n // stride >= 4 else 2
        out.append((stride, w))
        stride *= w
    return out


def flip_with(x, by, extra, got):
    if by in extra:
        rider = extra.pop(by)
        moved = flip(jnp.concatenate([x, rider], axis=0), "morton", by)
        got[by] = moved[x.shape[0] :]
        return moved[: x.shape[0]]
    return flip(x, "morton", by)


def reduce_all(mine, oth, extra, early, finish):
    got = {}
    stages = stages_of(lax.axis_size("morton"))
    v = mine.astype(F32) + flip(oth, "dp", 1).astype(F32)
    stride, width = stages[0]
    j = lax.axis_index("morton") % width
    pieces = v.astype(BF).reshape(width, v.shape[0] // width, v.shape[1])
    parts = [pick(pieces, j).astype(F32)]
    for d in range(1, width):
        parts.append(flip_with(pick(pieces, j ^ d), d, extra, got).astype(F32))
    v, early = lax.optimization_barrier((tree_sum(parts), early))
    for stride, width in stages[1:]:
        w = v.astype(BF)
        parts = [w.astype(F32)]
        for d in range(1, width):
            parts.append(flip_with(w, d * stride, extra, got).astype(F32))
        v = tree_sum(parts)
    for by in list(extra):
        got[by] = flip(extra.pop(by), "morton", by)
    w = v.astype(BF)
    stacked = jnp.stack([w] + [flip(w, "morton", d) for d in range(1, stages[0][1])])
    mine = jnp.concatenate([pick(stacked, j ^ k) for k in range(stages[0][1])], axis=0)
    mine, done = lax.optimization_barrier((mine, finish(early, got)))
    return mine, flip(mine, "dp", 1), done


def on_device(
    node_feat, edge_feat, cot_node, cot_edge, senders, receivers, send_rows, edge_count,
    edge_w1, edge_w2, edge_gain, node_w1, node_w2, node_gain,
):
    peers = lax.axis_size("morton")
    pair = lax.axis_size("dp")
    half = peers // 2
    h, e, cn, ce = node_feat[0], edge_feat[0], cot_node[0], cot_edge[0]
    C, H = h.shape
    E = e.shape[0]
    G = send_rows.shape[1]
    q = G // 4
    T = C + G
    i32 = jnp.int32
    dma = pltpu.SemaphoreType.DMA
    egain, ngain = edge_gain.reshape(1, H), node_gain.reshape(1, H)

    ghost = sds((q, H), BF)
    far, one, two = call(
        pack_kernel, "pack_ghosts", (ghost,) * 3, [HBM] * 2, (VM,) * 3,
        [like(send_rows), like(h), pltpu.VMEM((128, 128), i32), pltpu.VMEM((G, 128), i32),
         pltpu.VMEM((G, H), F32), dma((2,))],
        4_000_000_000, 8_000_000, 8,
    )(send_rows, h)
    far = flip(far, "morton", half)
    one = flip(one, "morton", 1)
    two = cross_pairs(two)

    part, pg, pr, ptr, pts = call(
        pre_kernel, "edge_pre",
        (sds((E, H), F32), sds((E, G), BF), sds((E, C), BF), sds((C, E), BF), sds((T, E), BF)),
        [HBM] * 5, (VM,) * 5,
        [like(h), like(e), like(senders), like(receivers), like(edge_w1),
         pltpu.VMEM((128, 128), i32), pltpu.VMEM((E, 128), i32), pltpu.VMEM((E, 128), i32),
         pltpu.VMEM((H + 2 * C, H), BF), dma((5,))],
        2 * E * H * (H + 2 * C) * 4, 4 * E * (H + T), 24,
    )(h, e, senders, receivers, edge_w1)

    rows = -(-(7 * H + 16) // (pair * 32)) * (pair * 32)
    mine_shape = sds((rows // pair, H), BF)
    hbm_in = [h, e, cn, ce, edge_w1, edge_w2, egain, node_w1, node_w2, ngain]
    gnode, gedge, bfar, bone, btwo, wmine, woth = call(
        main_kernel, "mesh_layer",
        (sds((C, H), F32), sds((E, H), F32), ghost, ghost, ghost, mine_shape, mine_shape),
        [SM] + [VM] * 8 + [HBM] * 10,
        (VM, HBM, VM, VM, VM, VM, VM),
        [like(x) for x in hbm_in]
        + [pltpu.VMEM((G, H), BF), pltpu.VMEM((E, H), BF), pltpu.VMEM((E, H), F32),
           pltpu.VMEM((E, H), F32), pltpu.VMEM((E, 1), F32), pltpu.VMEM((C, H), F32),
           pltpu.VMEM((C, H), BF), pltpu.VMEM((E, H), BF), pltpu.VMEM((E, H), BF),
           pltpu.VMEM((E, H), F32), pltpu.VMEM((rows, H), F32), pltpu.VMEM((G, H), F32),
           dma((10,)), dma((E // BWD_CHUNK,))],
        2 * E * H * 4608, 8 * E * H, 36,
    )(edge_count, part, pg, pr, ptr, pts, far, one, two, *hbm_in)

    def finish(rtwo, got):
        return call(
            node_kernel, "node_grad", sds((C, H), F32), [HBM] + [VM] * 4, VM,
            [like(send_rows), pltpu.VMEM((G, H), BF), dma((1,))],
            2 * C * G * H, 8 * C * H, 8,
        )(send_rows, gnode, got[half], got[1], rtwo)

    mine, oth, grad_node = reduce_all(
        wmine, woth, {1: bone, half: bfar}, cross_pairs(btwo), finish
    )
    factor = float(pair * peers * E) ** -0.5
    g1, g2, gg, gn1, gn2, gng = call(
        functools.partial(unpack_kernel, factor), "weight_grads",
        tuple(sds(s, F32) for s in ((3 * H, H), (H, H), (1, H), (2 * H, H), (H, H), (1, H))),
        [VM] * 2, (VM,) * 6, [pltpu.VMEM((rows, H), F32)], rows * H, 8 * rows * H, 8,
    )(mine, oth)
    return (
        grad_node[None], gedge[None], g1, g2, gg.reshape(H), gn1, gn2, gng.reshape(H),
    )


def solution(mesh):
    cells = P("dp", "morton", None)
    flat = P("dp", "morton")
    in_specs = (cells,) * 4 + (flat,) * 4 + (P(),) * 6
    out_specs = (cells, cells) + (P(),) * 6
    return jax.shard_map(
        on_device, mesh=mesh, in_specs=in_specs, out_specs=out_specs, check_vma=False
    )
```

time: 69.6 us -> 51.4 us (0.74)
  local copies, waits for them, and re-layouts: 10.3 us -> 1.69 us
  starting transfers between devices: 25 us -> 22 us
  other arithmetic: 1.94 us -> 0.12 us
  waiting for transfers between devices: 12.1 us -> 10.5 us
  Pallas kernels: 16.9 us -> 15.3 us
  matrix products: 1.38 us -> 0 us
    ppermute x6 -> x2, starting transfers between devices: 13.3 us -> 5.63 us  [cross_pairs(): lax.ppermute(x, 'morton', [(i, (i + 1) % n if i % 2 else (i - 1) % n) for...]
    unnamed x24 -> x30, local copies, waits for them, and re-layouts: 7.73 us -> 1.65 us
    ppermute x11 -> x13, starting transfers between devices: 11.7 us -> 16.3 us  [flip(): return lax.ppermute(x, axis, [(i, i ^ by) for i in range(n)])]
    ppermute x6 -> x2, waiting for transfers between devices: 6.68 us -> 3.94 us  [cross_pairs(): lax.ppermute(x, 'morton', [(i, (i + 1) % n if i % 2 else (i - 1) % n) for...]
    slice x4 -> x2, local copies, waits for them, and re-layouts: 2.02 us -> 0.01 us  [flip_with(): got[by] = moved[x.shape[0]:]]
    pallas_call x1 -> x5, Pallas kernels: 16.9 us -> 15.3 us  [the longest x1 7.31 us: on_device(): call(main_kernel, 'mesh_layer', (sds((C, H), F32), sds((E, H), F32), ghos...]
    dot_general x2 -> x0, matrix products: 1.38 us -> none  [the longest x1 1.16 us: on_device(): jnp.dot((rows_out[:, None] == ids[None, :]).astype(BF), h, preferred_elem...]
    ppermute x11 -> x13, waiting for transfers between devices: 5.38 us -> 6.53 us  [flip(): return lax.ppermute(x, axis, [(i, i ^ by) for i in range(n)])]
  transfers between devices with their start and end apart: 17 -> 15, of which waited for: 9 -> 6; matrix products, arithmetic and copies ran while one was open for 1% -> 0% of each run, Pallas kernels for 0% -> 13%
where the time goes in v2:
time: 51.4 us; the launch traced here: 51.2 us
  starting transfers between devices  22 us (43%)
  Pallas kernels  15.3 us (30%)
  waiting for transfers between devices  10.5 us (20%)
  local copies, waits for them, and re-layouts  1.69 us (3%)
  between operations  1.61 us (3%)
    ppermute x13, starting transfers between devices, flip(): return lax.ppermute(x, axis, [(i, i ^ by) for i in range(n)])  16.3 us
    pallas_call x1, Pallas kernels, on_device(): call(main_kernel, 'mesh_layer', (sds((C, H), F32), sds((E, H), F32), ghos...  7.31 us
    ppermute x13, waiting for transfers between devices, flip(): return lax.ppermute(x, axis, [(i, i ^ by) for i in range(n)])  6.53 us
    ppermute x2, starting transfers between devices, cross_pairs(): lax.ppermute(x, 'morton', [(i, (i + 1) % n if i % 2 else (i - 1) % n) for...  5.63 us
    pallas_call x1, Pallas kernels, on_device(): call(pre_kernel, 'edge_pre', (sds((E, H), F32), sds((E, G), BF), sds((E,...  5.57 us
    ppermute x2, waiting for transfers between devices, cross_pairs(): lax.ppermute(x, 'morton', [(i, (i + 1) % n if i % 2 else (i - 1) % n) for...  3.94 us
    unnamed x30, local copies, waits for them, and re-layouts  1.65 us
  transfers between devices with their start and end apart: 15, of which 6 were waited for; matrix products, arithmetic and copies ran while one was open for 0% of the time, Pallas kernels for 13%

profile of v2, /device:TPU:0, one launch (start us, length us, event | category | flops | bytes accessed | tf_op | source)
XLA Modules:
  0.0 51.2 jit_solution(7423386441079132865)
XLA Ops:
  0.6 0.9 %copy-done.3 = bf16[1,512,128]{2,1,0:T(8,128)(2,1)S(1)} copy-done((bf16[1,512,128]{2,1,0:T(8,128)(2,1)S(1)}, bf16[1,512,128]{2,1,0:T(8,128)(2,1)}, u32[]{:S(2)}) %copy-start.3) | copy-done | bytes 131096
  1.5 0.7 %copy-done.9 = s32[1,256]{1,0:T(1,128)S(1)} copy-done((s32[1,256]{1,0:T(1,128)S(1)}, s32[1,256]{1,0:T(1,128)}, u32[]{:S(2)}) %copy-start.9) | copy-done | bytes 1048
  2.2 0.6 %pack_ghosts.1 = (bf16[64,128]{1,0:T(8,128)(2,1)S(1)}, bf16[64,128]{1,0:T(8,128)(2,1)S(1)}, bf16[64,128]{1,0:T(8,128)(2,1)S(1)}) custom-call(s32[1,256]{1,0:T(1,128)S(1)} %copy-done.9, bf16[512,128]{1,0:T(8,128)(2,1)S(1)} %bitcast.35), custom_call_target="tpu_custom_call" | custom-call | flops 4000000000 | bytes 8000000 | tf_op jit(solution)/shard_map/pack_ghosts/pallas_call | solution.py:387
  2.9 4.1 %collective-permute-start = (bf16[64,128]{1,0:T(8,128)(2,1)S(1)}, bf16[64,128]{1,0:T(8,128)(2,1)S(1)}, u32[]{:S(2)}, u32[]{:S(2)}) collective-permute-start(bf16[64,128]{1,0:T(8,128)(2,1)S(1)} %get-tuple-element.38), channel_id=1, source_target_pairs={{0,16},{2,18},{4,20},{6,22},{8,24},{10,26},{12,28},{14,30},{16,0},... | collective-permute-start | bytes 49160 | tf_op jit(solution)/shard_map/ppermute | solution.py:306
  7.0 1.5 %collective-permute-start.1 = (bf16[64,128]{1,0:T(8,128)(2,1)S(1)}, bf16[64,128]{1,0:T(8,128)(2,1)S(1)}, u32[]{:S(2)}, u32[]{:S(2)}) collective-permute-start(bf16[64,128]{1,0:T(8,128)(2,1)S(1)} %get-tuple-element.39), channel_id=1, source_target_pairs={{0,2},{2,0},{4,6},{6,4},{8,10},{10,8},{12,14},{14,12},{16,18},{18,... | collective-permute-start | bytes 49160 | tf_op jit(solution)/shard_map/ppermute | solution.py:306
  8.5 2.3 %collective-permute-start.2 = (bf16[64,128]{1,0:T(8,128)(2,1)S(1)}, bf16[64,128]{1,0:T(8,128)(2,1)S(1)}, u32[]{:S(2)}, u32[]{:S(2)}) collective-permute-start(bf16[64,128]{1,0:T(8,128)(2,1)S(1)} %get-tuple-element.40), channel_id=1, source_target_pairs={{0,30},{2,4},{4,2},{6,8},{8,6},{10,12},{12,10},{14,16},{16,14},{18... | collective-permute-start | bytes 49160 | tf_op jit(solution)/shard_map/ppermute | solution.py:311
  10.8 0.0 copy-start.1
  10.8 0.0 copy-start.5
  10.8 0.0 copy-start.6
  10.9 0.0 copy-start.11
  10.9 0.0 copy-start.12
  10.9 5.6 %edge_pre.1 = (f32[2048,128]{1,0:T(8,128)S(1)}, bf16[2048,256]{1,0:T(8,128)(2,1)S(1)}, bf16[2048,512]{1,0:T(8,128)(2,1)S(1)}, bf16[512,2048]{1,0:T(8,128)(2,1)S(1)}, bf16[768,2048]{1,0:T(8,128)(2,1)S(1)}) custom-call(bf16[512,128]{1,0:T(8,128)(2,1)S(1)} %bitcast.36, bf16[2048,128]{1,0:T(8,128)(2,1)S(1)} %bitcast.32, s32[1,2048]{1,0:T(1,128)S(1)} %copy-done.13, ...), custom_call_target="tpu_custom_call" | custom-call | flops 2415919104 | bytes 7340032 | tf_op jit(solution)/shard_map/edge_pre/pallas_call | solution.py:397
  17.2 0.0 copy-start.10
  17.2 7.3 %mesh_layer.1 = (f32[512,128]{1,0:T(8,128)S(1)}, f32[2048,128]{1,0:T(8,128)}, bf16[64,128]{1,0:T(8,128)(2,1)S(1)}, bf16[64,128]{1,0:T(8,128)(2,1)S(1)}, bf16[64,...) custom-call(s32[1,1]{1,0:T(1,128)S(6)} %copy.22.count_ref, ...), custom_call_target="tpu_custom_call" | custom-call | flops 2415919104 | bytes 2097152 | tf_op jit(solution)/shard_map/mesh_layer/pallas_call | solution.py:410
  24.6 0.1 collective-permute-start.3
  24.7 1.3 %collective-permute-done.3 = bf16[480,128]{1,0:T(8,128)(2,1)S(1)} collective-permute-done((bf16[480,128]{1,0:T(8,128)(2,1)S(1)}, bf16[480,128]{1,0:T(8,128)(2,1)S(1)}, u32[]{:S(2)}, u32[]{:S(2)}) %collective-permute-start.3) | collective-permute-done | bytes 122912 | tf_op jit(solution)/shard_map/ppermute | solution.py:306
  26.0 0.8 %collective-permute-start.4 = (bf16[184,128]{1,0:T(8,128)(2,1)S(1)}, bf16[184,128]{1,0:T(8,128)(2,1)S(1)}, u32[]{:S(2)}, u32[]{:S(2)}) collective-permute-start(bf16[184,128]{1,0:T(8,128)(2,1)S(1)} %pad_maximum_fusion.2), channel_id=1, source_target_pairs={{0,2},{2,0},{4,6},{6,4},{8,10},{10,8},{12,14},{14,12},{16,18},{18,... | collective-permute-start | bytes 141320 | tf_op jit(solution)/shard_map/ppermute | solution.py:306
  26.8 1.0 %collective-permute-start.6 = (bf16[120,128]{1,0:T(8,128)(2,1)S(1)}, bf16[120,128]{1,0:T(8,128)(2,1)S(1)}, u32[]{:S(2)}, u32[]{:S(2)}) collective-permute-start(bf16[120,128]{1,0:T(8,128)(2,1)S(1)} %get-tuple-element.63), channel_id=1, source_target_pairs={{0,6},{2,4},{4,2},{6,0},{8,14},{10,12},{12,10},{14,8},{16,22},{18,... | collective-permute-start | bytes 92168 | tf_op jit(solution)/shard_map/ppermute | solution.py:306
  27.9 1.7 %collective-permute-start.5 = (bf16[120,128]{1,0:T(8,128)(2,1)S(1)}, bf16[120,128]{1,0:T(8,128)(2,1)S(1)}, u32[]{:S(2)}, u32[]{:S(2)}) collective-permute-start(bf16[120,128]{1,0:T(8,128)(2,1)S(1)} %get-tuple-element.64), channel_id=1, source_target_pairs={{0,4},{2,6},{4,0},{6,2},{8,12},{10,14},{12,8},{14,10},{16,20},{18,... | collective-permute-start | bytes 92168 | tf_op jit(solution)/shard_map/ppermute | solution.py:306
  29.6 3.3 %collective-permute-start.7 = (bf16[64,128]{1,0:T(8,128)(2,1)S(1)}, bf16[64,128]{1,0:T(8,128)(2,1)S(1)}, u32[]{:S(2)}, u32[]{:S(2)}) collective-permute-start(bf16[64,128]{1,0:T(8,128)(2,1)S(1)} %get-tuple-element.44), channel_id=1, source_target_pairs={{0,30},{2,4},{4,2},{6,8},{8,6},{10,12},{12,10},{14,16},{16,14},{18... | collective-permute-start | bytes 49160 | tf_op jit(solution)/shard_map/ppermute | solution.py:311
  33.0 3.9 %collective-permute-done.7.two_ref = bf16[64,128]{1,0:T(8,128)(2,1)S(1)} collective-permute-done((bf16[64,128]{1,0:T(8,128)(2,1)S(1)}, bf16[64,128]{1,0:T(8,128)(2,1)S(1)}, u32[]{:S(2)}, u32[]{:S(2)}) %collective-permute-start.7) | collective-permute-done | bytes 16416 | tf_op jit(solution)/shard_map/ppermute | solution.py:311
  36.9 1.2 %collective-permute-start.10 = (bf16[120,128]{1,0:T(8,128)(2,1)S(1)}, bf16[120,128]{1,0:T(8,128)(2,1)S(1)}, u32[]{:S(2)}, u32[]{:S(2)}) collective-permute-start(bf16[120,128]{1,0:T(8,128)(2,1)S(1)} %fusion), channel_id=1, source_target_pairs={{0,24},{2,26},{4,28},{6,30},{8,16},{10,18},{12,20},{14,22},{16,8},... | collective-permute-start | bytes 92168 | tf_op jit(solution)/shard_map/ppermute | solution.py:306
  38.2 2.2 %collective-permute-start.8 = (bf16[120,128]{1,0:T(8,128)(2,1)S(1)}, bf16[120,128]{1,0:T(8,128)(2,1)S(1)}, u32[]{:S(2)}, u32[]{:S(2)}) collective-permute-start(bf16[120,128]{1,0:T(8,128)(2,1)S(1)} %fusion), channel_id=1, source_target_pairs={{0,8},{2,10},{4,12},{6,14},{8,0},{10,2},{12,4},{14,6},{16,24},{18,... | collective-permute-start | bytes 92168 | tf_op jit(solution)/shard_map/ppermute | solution.py:306
  40.4 2.3 %collective-permute-done.10 = bf16[120,128]{1,0:T(8,128)(2,1)S(1)} collective-permute-done((bf16[120,128]{1,0:T(8,128)(2,1)S(1)}, bf16[120,128]{1,0:T(8,128)(2,1)S(1)}, u32[]{:S(2)}, u32[]{:S(2)}) %collective-permute-start.10) | collective-permute-done | bytes 30752 | tf_op jit(solution)/shard_map/ppermute | solution.py:306
  42.7 2.3 %collective-permute-start.13 = (bf16[120,128]{1,0:T(8,128)(2,1)S(1)}, bf16[120,128]{1,0:T(8,128)(2,1)S(1)}, u32[]{:S(2)}, u32[]{:S(2)}) collective-permute-start(bf16[120,128]{1,0:T(8,128)(2,1)S(1)} %add_convert_fusion.1), channel_id=1, source_target_pairs={{0,6},{2,4},{4,2},{6,0},{8,14},{10,12},{12,10},{14,8},{16,22},{18,... | collective-permute-start | bytes 92168 | tf_op jit(solution)/shard_map/ppermute | solution.py:306
  45.0 1.3 %collective-permute-start.11 = (bf16[120,128]{1,0:T(8,128)(2,1)S(1)}, bf16[120,128]{1,0:T(8,128)(2,1)S(1)}, u32[]{:S(2)}, u32[]{:S(2)}) collective-permute-start(bf16[120,128]{1,0:T(8,128)(2,1)S(1)} %add_convert_fusion.1), channel_id=1, source_target_pairs={{0,2},{2,0},{4,6},{6,4},{8,10},{10,8},{12,14},{14,12},{16,18},{18,... | collective-permute-start | bytes 92168 | tf_op jit(solution)/shard_map/ppermute | solution.py:306
  46.3 1.0 %node_grad.1 = f32[512,128]{1,0:T(8,128)} custom-call(s32[1,256]{1,0:T(1,128)S(1)} %copy-done.10, f32[512,128]{1,0:T(8,128)S(1)} %get-tuple-element.47.gnode_ref, bf16[64,128]{1,0:T(8,128)(2,1)S(1)} %slice.18.far_ref, bf16[64,128]{1,0:T(8,128)(2,1)S(1)} %slice.19.one_ref, bf16[64,128]{1,0:T(8,128)(2,1)S(1)} %collective-permute-done.7.two_ref), custom_call_target="tpu_custom_call" | custom-call | flops 33554432 | bytes 524288 | tf_op jit(solution)/shard_map/node_grad/pallas_call | solution.py:425
  47.3 0.3 collective-permute-done.13
  47.6 1.3 %collective-permute-done.12 = bf16[120,128]{1,0:T(8,128)(2,1)S(1)} collective-permute-done((bf16[120,128]{1,0:T(8,128)(2,1)S(1)}, bf16[120,128]{1,0:T(8,128)(2,1)S(1)}, u32[]{:S(2)}, u32[]{:S(2)}) %collective-permute-start.12) | collective-permute-done | bytes 30752 | tf_op jit(solution)/shard_map/ppermute | solution.py:306
  49.0 0.1 collective-permute-start.14
  49.1 1.3 %collective-permute-done.14.oth_ref = bf16[480,128]{1,0:T(8,128)(2,1)S(1)} collective-permute-done((bf16[480,128]{1,0:T(8,128)(2,1)S(1)}, bf16[480,128]{1,0:T(8,128)(2,1)S(1)}, u32[]{:S(2)}, u32[]{:S(2)}) %collective-permute-start.14) | collective-permute-done | bytes 122912 | tf_op jit(solution)/shard_map/ppermute | solution.py:306
  50.4 0.8 %weight_grads.1 = (f32[384,128]{1,0:T(8,128)}, f32[128,128]{1,0:T(8,128)}, f32[1,128]{1,0:T(1,128)}, f32[256,128]{1,0:T(8,128)}, f32[128,128]{1,0:T(8,128)}, /*index=5*/f32[1,128]{1,0:T(1,128)}) custom-call(bf16[480,128]{1,0:T(8,128)(2,1)S(1)} %pad_maximum_fusion.1.mine_ref, bf16[480,128]{1,0:T(8,128)(2,1)S(1)} %collective-permute-done.14.oth_ref), custom_call_target="tpu_custom_call" | custom-call | flops 122880 | bytes 983040 | tf_op jit(solution)/shard_map/weight_grads/pallas_call | solution.py:435
  (44 shorter events, 0.2 us)
Async XLA Ops:
  0.6 0.9 %copy-start.3 = (bf16[1,512,128]{2,1,0:T(8,128)(2,1)S(1)}, bf16[1,512,128]{2,1,0:T(8,128)(2,1)}, u32[]{:S(2)}) copy-start(bf16[1,512,128]{2,1,0:T(8,128)(2,1)} %param.14) | copy-start | bytes 393220
  1.5 0.7 %copy-start.9 = (s32[1,256]{1,0:T(1,128)S(1)}, s32[1,256]{1,0:T(1,128)}, u32[]{:S(2)}) copy-start(s32[1,256]{1,0:T(1,128)} %rows_hbm.3) | copy-start | bytes 3076
  2.2 8.6 %copy-start = (bf16[1,2048,128]{2,1,0:T(8,128)(2,1)S(1)}, bf16[1,2048,128]{2,1,0:T(8,128)(2,1)}, u32[]{:S(2)}) copy-start(bf16[1,2048,128]{2,1,0:T(8,128)(2,1)} %param.15) | copy-start | bytes 1572868
  2.2 8.6 %copy-start.2 = (f32[384,128]{1,0:T(8,128)S(1)}, f32[384,128]{1,0:T(8,128)}, u32[]{:S(2)}) copy-start(f32[384,128]{1,0:T(8,128)} %w1_hbm.3) | copy-start | bytes 589828
  2.2 8.6 %copy-start.4 = (bf16[1,512,128]{2,1,0:T(8,128)(2,1)S(1)}, bf16[1,512,128]{2,1,0:T(8,128)(2,1)}, u32[]{:S(2)}) copy-start(bf16[1,512,128]{2,1,0:T(8,128)(2,1)} %param.14) | copy-start | bytes 393220
  2.2 8.6 %copy-start.13 = (s32[1,2048]{1,0:T(1,128)S(1)}, s32[1,2048]{1,0:T(1,128)}, u32[]{:S(2)}) copy-start(s32[1,2048]{1,0:T(1,128)} %snd_hbm.1) | copy-start | bytes 24580
  2.2 8.6 %copy-start.14 = (s32[1,2048]{1,0:T(1,128)S(1)}, s32[1,2048]{1,0:T(1,128)}, u32[]{:S(2)}) copy-start(s32[1,2048]{1,0:T(1,128)} %rcv_hbm.1) | copy-start | bytes 24580
  2.9 14.2 %collective-permute-start = (bf16[64,128]{1,0:T(8,128)(2,1)S(1)}, bf16[64,128]{1,0:T(8,128)(2,1)S(1)}, u32[]{:S(2)}, u32[]{:S(2)}) collective-permute-start(bf16[64,128]{1,0:T(8,128)(2,1)S(1)} %get-tuple-element.38), channel_id=1, source_target_pairs={{0,16},{2,18},{4,20},{6,22},{8,24},{10,26},{12,28},{14,30},{16,0},... | collective-permute-start | bytes 49160 | tf_op jit(solution)/shard_map/ppermute | solution.py:306
  7.0 10.1 %collective-permute-start.1 = (bf16[64,128]{1,0:T(8,128)(2,1)S(1)}, bf16[64,128]{1,0:T(8,128)(2,1)S(1)}, u32[]{:S(2)}, u32[]{:S(2)}) collective-permute-start(bf16[64,128]{1,0:T(8,128)(2,1)S(1)} %get-tuple-element.39), channel_id=1, source_target_pairs={{0,2},{2,0},{4,6},{6,4},{8,10},{10,8},{12,14},{14,12},{16,18},{18,... | collective-permute-start | bytes 49160 | tf_op jit(solution)/shard_map/ppermute | solution.py:306
  8.5 8.6 %collective-permute-start.2 = (bf16[64,128]{1,0:T(8,128)(2,1)S(1)}, bf16[64,128]{1,0:T(8,128)(2,1)S(1)}, u32[]{:S(2)}, u32[]{:S(2)}) collective-permute-start(bf16[64,128]{1,0:T(8,128)(2,1)S(1)} %get-tuple-element.40), channel_id=1, source_target_pairs={{0,30},{2,4},{4,2},{6,8},{8,6},{10,12},{12,10},{14,16},{16,14},{18... | collective-permute-start | bytes 49160 | tf_op jit(solution)/shard_map/ppermute | solution.py:311
  10.8 6.3 %copy-start.1 = (bf16[1,2048,128]{2,1,0:T(8,128)(2,1)S(1)}, bf16[1,2048,128]{2,1,0:T(8,128)(2,1)}, u32[]{:S(2)}) copy-start(bf16[1,2048,128]{2,1,0:T(8,128)(2,1)} %param.17) | copy-start | bytes 1572868
  10.8 6.3 %copy-start.5 = (bf16[1,512,128]{2,1,0:T(8,128)(2,1)S(1)}, bf16[1,512,128]{2,1,0:T(8,128)(2,1)}, u32[]{:S(2)}) copy-start(bf16[1,512,128]{2,1,0:T(8,128)(2,1)} %param.16) | copy-start | bytes 393220
  10.8 6.3 %copy-start.6 = (f32[256,128]{1,0:T(8,128)S(1)}, f32[256,128]{1,0:T(8,128)}, u32[]{:S(2)}) copy-start(f32[256,128]{1,0:T(8,128)} %nw1_hbm.1) | copy-start | bytes 393220
  10.8 6.3 %copy-start.7 = (f32[128,128]{1,0:T(8,128)S(1)}, f32[128,128]{1,0:T(8,128)}, u32[]{:S(2)}) copy-start(f32[128,128]{1,0:T(8,128)} %w2_hbm.1) | copy-start | bytes 196612
  10.9 6.3 %copy-start.8 = (f32[128,128]{1,0:T(8,128)S(1)}, f32[128,128]{1,0:T(8,128)}, u32[]{:S(2)}) copy-start(f32[128,128]{1,0:T(8,128)} %nw2_hbm.1) | copy-start | bytes 196612
  10.9 6.3 %copy-start.11 = (f32[128]{0:T(128)S(1)}, f32[128]{0:T(128)}, u32[]{:S(2)}) copy-start(f32[128]{0:T(128)} %param.24) | copy-start | bytes 1540
  10.9 6.3 %copy-start.12 = (f32[128]{0:T(128)S(1)}, f32[128]{0:T(128)}, u32[]{:S(2)}) copy-start(f32[128]{0:T(128)} %param.27) | copy-start | bytes 1540
  17.2 29.1 %copy-start.10 = (s32[1,256]{1,0:T(1,128)S(1)}, s32[1,256]{1,0:T(1,128)}, u32[]{:S(2)}) copy-start(s32[1,256]{1,0:T(1,128)} %rows_hbm.3) | copy-start | bytes 3076
  24.6 1.4 %collective-permute-start.3 = (bf16[480,128]{1,0:T(8,128)(2,1)S(1)}, bf16[480,128]{1,0:T(8,128)(2,1)S(1)}, u32[]{:S(2)}, u32[]{:S(2)}) collective-permute-start(bf16[480,128]{1,0:T(8,128)(2,1)S(1)} %get-tuple-element.42), channel_id=1, source_target_pairs={{0,1},{1,0},{2,3},{3,2},{4,5},{5,4},{6,7},{7,6},{8,9},{9,8},{10,11... | collective-permute-start | bytes 368648 | tf_op jit(solution)/shard_map/ppermute | solution.py:306
  26.0 6.9 %collective-permute-start.4 = (bf16[184,128]{1,0:T(8,128)(2,1)S(1)}, bf16[184,128]{1,0:T(8,128)(2,1)S(1)}, u32[]{:S(2)}, u32[]{:S(2)}) collective-permute-start(bf16[184,128]{1,0:T(8,128)(2,1)S(1)} %pad_maximum_fusion.2), channel_id=1, source_target_pairs={{0,2},{2,0},{4,6},{6,4},{8,10},{10,8},{12,14},{14,12},{16,18},{18,... | collective-permute-start | bytes 141320 | tf_op jit(solution)/shard_map/ppermute | solution.py:306
  26.8 6.1 %collective-permute-start.6 = (bf16[120,128]{1,0:T(8,128)(2,1)S(1)}, bf16[120,128]{1,0:T(8,128)(2,1)S(1)}, u32[]{:S(2)}, u32[]{:S(2)}) collective-permute-start(bf16[120,128]{1,0:T(8,128)(2,1)S(1)} %get-tuple-element.63), channel_id=1, source_target_pairs={{0,6},{2,4},{4,2},{6,0},{8,14},{10,12},{12,10},{14,8},{16,22},{18,... | collective-permute-start | bytes 92168 | tf_op jit(solution)/shard_map/ppermute | solution.py:306
  27.9 5.1 %collective-permute-start.5 = (bf16[120,128]{1,0:T(8,128)(2,1)S(1)}, bf16[120,128]{1,0:T(8,128)(2,1)S(1)}, u32[]{:S(2)}, u32[]{:S(2)}) collective-permute-start(bf16[120,128]{1,0:T(8,128)(2,1)S(1)} %get-tuple-element.64), channel_id=1, source_target_pairs={{0,4},{2,6},{4,0},{6,2},{8,12},{10,14},{12,8},{14,10},{16,20},{18,... | collective-permute-start | bytes 92168 | tf_op jit(solution)/shard_map/ppermute | solution.py:306
  29.6 7.3 %collective-permute-start.7 = (bf16[64,128]{1,0:T(8,128)(2,1)S(1)}, bf16[64,128]{1,0:T(8,128)(2,1)S(1)}, u32[]{:S(2)}, u32[]{:S(2)}) collective-permute-start(bf16[64,128]{1,0:T(8,128)(2,1)S(1)} %get-tuple-element.44), channel_id=1, source_target_pairs={{0,30},{2,4},{4,2},{6,8},{8,6},{10,12},{12,10},{14,16},{16,14},{18... | collective-permute-start | bytes 49160 | tf_op jit(solution)/shard_map/ppermute | solution.py:311
  36.9 5.8 %collective-permute-start.9 = (bf16[184,128]{1,0:T(8,128)(2,1)S(1)}, bf16[184,128]{1,0:T(8,128)(2,1)S(1)}, u32[]{:S(2)}, u32[]{:S(2)}) collective-permute-start(bf16[184,128]{1,0:T(8,128)(2,1)S(1)} %pad_maximum_fusion.3), channel_id=1, source_target_pairs={{0,16},{2,18},{4,20},{6,22},{8,24},{10,26},{12,28},{14,30},{16,0},... | collective-permute-start | bytes 141320 | tf_op jit(solution)/shard_map/ppermute | solution.py:306
  36.9 5.8 %collective-permute-start.10 = (bf16[120,128]{1,0:T(8,128)(2,1)S(1)}, bf16[120,128]{1,0:T(8,128)(2,1)S(1)}, u32[]{:S(2)}, u32[]{:S(2)}) collective-permute-start(bf16[120,128]{1,0:T(8,128)(2,1)S(1)} %fusion), channel_id=1, source_target_pairs={{0,24},{2,26},{4,28},{6,30},{8,16},{10,18},{12,20},{14,22},{16,8},... | collective-permute-start | bytes 92168 | tf_op jit(solution)/shard_map/ppermute | solution.py:306
  38.2 4.5 %collective-permute-start.8 = (bf16[120,128]{1,0:T(8,128)(2,1)S(1)}, bf16[120,128]{1,0:T(8,128)(2,1)S(1)}, u32[]{:S(2)}, u32[]{:S(2)}) collective-permute-start(bf16[120,128]{1,0:T(8,128)(2,1)S(1)} %fusion), channel_id=1, source_target_pairs={{0,8},{2,10},{4,12},{6,14},{8,0},{10,2},{12,4},{14,6},{16,24},{18,... | collective-permute-start | bytes 92168 | tf_op jit(solution)/shard_map/ppermute | solution.py:306
  42.7 4.9 %collective-permute-start.13 = (bf16[120,128]{1,0:T(8,128)(2,1)S(1)}, bf16[120,128]{1,0:T(8,128)(2,1)S(1)}, u32[]{:S(2)}, u32[]{:S(2)}) collective-permute-start(bf16[120,128]{1,0:T(8,128)(2,1)S(1)} %add_convert_fusion.1), channel_id=1, source_target_pairs={{0,6},{2,4},{4,2},{6,0},{8,14},{10,12},{12,10},{14,8},{16,22},{18,... | collective-permute-start | bytes 92168 | tf_op jit(solution)/shard_map/ppermute | solution.py:306
  45.0 3.9 %collective-permute-start.12 = (bf16[120,128]{1,0:T(8,128)(2,1)S(1)}, bf16[120,128]{1,0:T(8,128)(2,1)S(1)}, u32[]{:S(2)}, u32[]{:S(2)}) collective-permute-start(bf16[120,128]{1,0:T(8,128)(2,1)S(1)} %add_convert_fusion.1), channel_id=1, source_target_pairs={{0,4},{2,6},{4,0},{6,2},{8,12},{10,14},{12,8},{14,10},{16,20},{18,... | collective-permute-start | bytes 92168 | tf_op jit(solution)/shard_map/ppermute | solution.py:306
  45.0 3.9 %collective-permute-start.11 = (bf16[120,128]{1,0:T(8,128)(2,1)S(1)}, bf16[120,128]{1,0:T(8,128)(2,1)S(1)}, u32[]{:S(2)}, u32[]{:S(2)}) collective-permute-start(bf16[120,128]{1,0:T(8,128)(2,1)S(1)} %add_convert_fusion.1), channel_id=1, source_target_pairs={{0,2},{2,0},{4,6},{6,4},{8,10},{10,8},{12,14},{14,12},{16,18},{18,... | collective-permute-start | bytes 92168 | tf_op jit(solution)/shard_map/ppermute | solution.py:306
  49.0 1.4 %collective-permute-start.14 = (bf16[480,128]{1,0:T(8,128)(2,1)S(1)}, bf16[480,128]{1,0:T(8,128)(2,1)S(1)}, u32[]{:S(2)}, u32[]{:S(2)}) collective-permute-start(bf16[480,128]{1,0:T(8,128)(2,1)S(1)} %pad_maximum_fusion.1.mine_ref), channel_id=1, source_target_pairs={{0,1},{1,0},{2,3},{3,2},{4,5},{5,4},{6,7},{7,6},{8,9},{9,8},{10,11... | collective-permute-start | bytes 368648 | tf_op jit(solution)/shard_map/ppermute | solution.py:306

commit v3 on v2

--- a/solution.py
+++ b/solution.py
@@ -13,6 +13,7 @@
 PRE_CHUNK = 1024
 FWD_CHUNK = 2048
 BWD_CHUNK = 2048
+LANES = 128
 
 
 def mm(a, b):
@@ -47,9 +48,12 @@
     )
 
 
-def one_hot_cols(col, size):
-    lane = lax.broadcasted_iota(jnp.int32, (col.shape[0], size), 1)
-    return jnp.where(jnp.tile(col, (1, size // col.shape[1])) == lane, 1.0, 0.0).astype(BF)
+def one_hot_cols(low, high, size):
+    lane = lax.broadcasted_iota(jnp.int32, low.shape, 1).astype(F32).astype(BF)
+    one, zero = jnp.ones_like(low), jnp.zeros_like(low)
+    base = jnp.where(low == lane, one, zero)
+    tiles = [jnp.where(high == jnp.full_like(high, t), base, zero) for t in range(size // LANES)]
+    return jnp.concatenate(tiles, axis=1)
 
 
 def one_hot_rows(row, size):
@@ -60,36 +64,30 @@
 def my_place():
     j = lax.axis_index("morton")
     return (j >= lax.axis_size("morton") // 2).astype(jnp.int32), j % 2
-
-
-def start_all(pairs, sems):
-    copies = [pltpu.make_async_copy(src, dst, sems.at[i]) for i, (src, dst) in enumerate(pairs)]
-    for c in copies:
-        c.start()
-    return copies
 
 
 def spread(row_refs, tmat, outs):
     tmat[...] = jnp.zeros_like(tmat)
     at = 0
     for ref in row_refs:
-        for r in range(ref.shape[1] // 128):
-            tmat[at : at + 1, :] = ref[:, r * 128 : (r + 1) * 128]
+        for r in range(ref.shape[1] // LANES):
+            tmat[at : at + 1, :] = ref[:, r * LANES : (r + 1) * LANES]
             at += 1
     turned = jnp.transpose(tmat[...])
+    low = (turned % LANES).astype(F32).astype(BF)
+    high = (turned // LANES).astype(F32).astype(BF)
     at = 0
-    for ref, out in zip(row_refs, outs):
-        for r in range(ref.shape[1] // 128):
-            out[r * 128 : (r + 1) * 128, :] = jnp.broadcast_to(turned[:, at : at + 1], (128, 128))
+    for ref, (low_ref, high_ref) in zip(row_refs, outs):
+        for r in range(ref.shape[1] // LANES):
+            rows = slice(r * LANES, (r + 1) * LANES)
+            low_ref[rows, :] = jnp.broadcast_to(low[:, at : at + 1], (LANES, LANES))
+            high_ref[rows, :] = jnp.broadcast_to(high[:, at : at + 1], (LANES, LANES))
             at += 1
 
 
-def pack_kernel(rows_hbm, h_hbm, far_ref, one_ref, two_ref, rows_s, h_s, tmat, col, got, sems):
-    copies = start_all([(rows_hbm, rows_s), (h_hbm, h_s)], sems)
-    copies[0].wait()
-    spread([rows_s], tmat, [col])
-    hot = one_hot_cols(col[...], h_s.shape[0])
-    copies[1].wait()
+def pack_kernel(rows_s, h_s, far_ref, one_ref, two_ref, tmat, low, high, got):
+    spread([rows_s], tmat, [(low, high)])
+    hot = one_hot_cols(low[...], high[...], h_s.shape[0])
     got[...] = mm(hot, h_s[...])
     upper, odd = my_place()
     q = far_ref.shape[0]
@@ -99,78 +97,60 @@
 
 
 def pre_kernel(
-    h_hbm, e_hbm, snd_hbm, rcv_hbm, w1_hbm,
-    part_ref, pg_ref, pr_ref, ptr_ref, pts_ref,
-    h_s, e_s, snd_s, rcv_s, w1_s, tmat, col_s, col_r, rhs, sems,
+    h_s, e_s, snd_s, rcv_s, w1_s, part_ref, ps_ref, pr_ref, tmat, low_s, high_s, low_r, high_r, rhs
 ):
-    copies = start_all(
-        [(snd_hbm, snd_s), (rcv_hbm, rcv_s), (h_hbm, h_s), (w1_hbm, w1_s), (e_hbm, e_s)], sems
-    )
     C, H = h_s.shape
     E = e_s.shape[0]
-    G = pg_ref.shape[1]
-    copies[0].wait()
-    copies[1].wait()
-    spread([snd_s, rcv_s], tmat, [col_s, col_r])
-    copies[2].wait()
-    copies[3].wait()
+    T = ps_ref.shape[1]
+    spread([snd_s, rcv_s], tmat, [(low_s, high_s), (low_r, high_r)])
     w1 = w1_s[...].astype(BF)
     h = h_s[...]
     rhs[0:H, :] = w1[:H]
     rhs[H : H + C, :] = mm(h, w1[H : 2 * H]).astype(BF)
     rhs[H + C :, :] = mm(h, w1[2 * H :]).astype(BF)
-    copies[4].wait()
 
     def step(i, carry):
         at = pl.ds(pl.multiple_of(i * PRE_CHUNK, PRE_CHUNK), PRE_CHUNK)
-        hot = one_hot_cols(col_s[at, :], C + G)
-        p_r = one_hot_cols(col_r[at, :], C)
-        pg_ref[at, :] = hot[:, C:]
+        p_s = one_hot_cols(low_s[at, :], high_s[at, :], T)
+        p_r = one_hot_cols(low_r[at, :], high_r[at, :], C)
+        ps_ref[at, :] = p_s
         pr_ref[at, :] = p_r
-        part_ref[at, :] = mm(jnp.concatenate([e_s[at, :], hot[:, :C], p_r], axis=1), rhs[...])
-        ptr_ref[:, at] = one_hot_rows(rcv_s[:, at], C)
-        pts_ref[:, at] = one_hot_rows(snd_s[:, at], C + G)
+        part_ref[at, :] = mm(jnp.concatenate([e_s[at, :], p_s[:, :C], p_r], axis=1), rhs[...])
         return carry
 
     lax.fori_loop(0, E // PRE_CHUNK, step, 0)
 
 
 def main_kernel(
-    count_ref, part_ref, pg_ref, pr_ref, ptr_ref, pts_ref, far_ref, one_ref, two_ref,
-    h_hbm, e_hbm, cn_hbm, ce_hbm, w1_hbm, w2_hbm, eg_hbm, nw1_hbm, nw2_hbm, ng_hbm,
+    count_hbm, part_ref, ps_ref, pr_ref, far_ref, one_ref, two_ref,
+    h_s, e_s, cn_s, ce_s, w1_s, w2_s, eg_s, nw1_s, nw2_s, ng_s,
     gnode_ref, gedge_hbm, bfar_ref, bone_ref, btwo_ref, wmine_ref, woth_ref,
-    h_s, e_s, cn_s, ce_s, w1_s, w2_s, eg_s, nw1_s, nw2_s, ng_s,
-    gh_s, p_s, dsil_s, nrm_s, inv_s, agg, dagg_s, db_s, da_s, gedge_s, wg, dgh, sems, out_sems,
+    gh_s, p_s, dsil_s, nrm_s, inv_s, agg, dagg_s, db_s, da_s, gedge_s, wg, dgh, count_s,
+    count_sem, out_sems,
 ):
-    copies = start_all(
-        [
-            (w1_hbm, w1_s), (w2_hbm, w2_s), (eg_hbm, eg_s), (e_hbm, e_s), (h_hbm, h_s),
-            (nw1_hbm, nw1_s), (nw2_hbm, nw2_s), (ng_hbm, ng_s), (cn_hbm, cn_s), (ce_hbm, ce_s),
-        ],
-        sems,
-    )
+    count_copy = pltpu.make_async_copy(count_hbm, count_s, count_sem)
+    count_copy.start()
     C, H = h_s.shape
     E = e_s.shape[0]
-    G = pg_ref.shape[1]
+    G = gh_s.shape[0]
     q = G // 4
-    count = count_ref[0, 0]
     upper, odd = my_place()
     gh_s[0:q, :] = far_ref[...]
     gh_s[3 * q :, :] = far_ref[...]
     gh_s[pl.ds(pl.multiple_of((1 + odd) * q, q), q), :] = one_ref[...]
     gh_s[pl.ds(pl.multiple_of((2 - odd) * q, q), q), :] = two_ref[...]
-    for c in copies[:4]:
-        c.wait()
     w1 = w1_s[...].astype(BF)
     w1e, w1s, w1r = w1[:H], w1[H : 2 * H], w1[2 * H :]
     w2 = w2_s[...].astype(BF)
     egain = eg_s[...]
     gtab = mm(gh_s[...], w1s).astype(BF)
     agg[...] = jnp.zeros_like(agg)
+    count_copy.wait()
+    count = count_s[0, 0]
 
     def fwd(i, carry):
         at = pl.ds(pl.multiple_of(i * FWD_CHUNK, FWD_CHUNK), FWD_CHUNK)
-        act, dsil = silu_parts(part_ref[at, :] + mm(pg_ref[at, :], gtab))
+        act, dsil = silu_parts(part_ref[at, :] + mm(ps_ref[at, C:], gtab))
         p = act.astype(BF)
         p_s[at, :] = p
         dsil_s[at, :] = dsil
@@ -179,18 +159,16 @@
         inv_s[at, :] = inv
         rowid = lax.broadcasted_iota(jnp.int32, (FWD_CHUNK, H), 0) + i * FWD_CHUNK
         msg = jnp.where(rowid < count, e_s[at, :].astype(F32) + nrm * egain, 0.0).astype(BF)
-        agg[...] += mm(ptr_ref[:, at], msg)
+        agg[...] += mm_lt(msg, pr_ref[at, :])
         return carry
 
     lax.fori_loop(0, E // FWD_CHUNK, fwd, 0)
 
-    for c in copies[4:]:
-        c.wait()
     h = h_s[...]
     nw1 = nw1_s[...].astype(BF)
     nw2 = nw2_s[...].astype(BF)
     cn = cn_s[...].astype(F32)
-    aggb = agg[...].astype(BF)
+    aggb = jnp.transpose(agg[...]).astype(BF)
     y = jnp.concatenate([h, aggb], axis=1)
     act, dsil = silu_parts(mm(y, nw1))
     r = act.astype(BF)
@@ -229,14 +207,15 @@
 
     wg[7 * H : 7 * H + 1, :] = jnp.sum(gain_sum, axis=0, keepdims=True)
     da = da_s[...]
-    gs = mm(pts_ref[...], da).astype(BF)
-    gr = mm(ptr_ref[...], da).astype(BF)
+    gs_t = mm_lt(da, ps_ref[...]).astype(BF)
+    gr_t = mm_lt(da, pr_ref[...]).astype(BF)
+    table = jnp.concatenate([h, gh_s[...]], axis=0)
     wg[3 * H : 4 * H, :] = mm_lt(p_s[...], db_s[...])
-    wg[0:H, :] = mm_lt(e_s[...], da)
-    wg[H : 2 * H, :] = mm_lt(jnp.concatenate([h, gh_s[...]], axis=0), gs)
-    wg[2 * H : 3 * H, :] = mm_lt(h, gr)
-    dt = mm_rt(gs, w1s)
-    gnode_ref[...] += dt[:C] + mm_rt(gr, w1r)
+    wg[0:H, :] = jnp.transpose(mm_lt(da, e_s[...]))
+    wg[H : 2 * H, :] = jnp.transpose(mm(gs_t, table))
+    wg[2 * H : 3 * H, :] = jnp.transpose(mm(gr_t, h))
+    dt = jnp.transpose(mm(w1s, gs_t))
+    gnode_ref[...] += dt[:C] + jnp.transpose(mm(w1r, gr_t))
     dgh[...] = dt[C:]
     bfar_ref[...] = dgh[pl.ds(pl.multiple_of(upper * 3 * q, q), q), :].astype(BF)
     bone_ref[...] = dgh[pl.ds(pl.multiple_of((1 + odd) * q, q), q), :].astype(BF)
@@ -249,15 +228,13 @@
         out_copy(i).wait()
 
 
-def node_kernel(rows_hbm, gnode_ref, far_ref, one_ref, two_ref, out_ref, rows_s, ret, sems):
-    copies = start_all([(rows_hbm, rows_s)], sems)
+def node_kernel(rows_s, gnode_ref, far_ref, one_ref, two_ref, out_ref, ret):
     upper, odd = my_place()
     q = far_ref.shape[0]
     ret[...] = jnp.zeros_like(ret)
     ret[pl.ds(pl.multiple_of((1 - upper) * 3 * q, q), q), :] = far_ref[...]
     ret[pl.ds(pl.multiple_of((2 - odd) * q, q), q), :] = one_ref[...]
     ret[pl.ds(pl.multiple_of((1 + odd) * q, q), q), :] = two_ref[...]
-    copies[0].wait()
     out_ref[...] = gnode_ref[...] + mm(one_hot_rows(rows_s[...], out_ref.shape[0]), ret[...])
 
 
@@ -276,12 +253,7 @@
 
 HBM = pl.BlockSpec(memory_space=pltpu.HBM)
 VM = pl.BlockSpec(memory_space=pltpu.VMEM)
-SM = pl.BlockSpec(memory_space=pltpu.SMEM)
 MIB = 1024 * 1024
-
-
-def like(x):
-    return pltpu.VMEM(x.shape, x.dtype)
 
 
 def sds(shape, dtype):
@@ -344,12 +316,12 @@
     got = {}
     stages = stages_of(lax.axis_size("morton"))
     v = mine.astype(F32) + flip(oth, "dp", 1).astype(F32)
-    stride, width = stages[0]
-    j = lax.axis_index("morton") % width
-    pieces = v.astype(BF).reshape(width, v.shape[0] // width, v.shape[1])
-    parts = [pick(pieces, j).astype(F32)]
-    for d in range(1, width):
-        parts.append(flip_with(pick(pieces, j ^ d), d, extra, got).astype(F32))
+    low = lax.axis_index("morton") % 2
+    halves = v.astype(BF).reshape(2, v.shape[0] // 2, v.shape[1])
+    kept, given = pick(halves, low), pick(halves, 1 - low)
+    parts = [kept.astype(F32)]
+    for d in range(1, stages[0][1]):
+        parts.append(flip_with(given if d % 2 else kept, d, extra, got).astype(F32))
     v, early = lax.optimization_barrier((tree_sum(parts), early))
     for stride, width in stages[1:]:
         w = v.astype(BF)
@@ -360,8 +332,9 @@
     for by in list(extra):
         got[by] = flip(extra.pop(by), "morton", by)
     w = v.astype(BF)
-    stacked = jnp.stack([w] + [flip(w, "morton", d) for d in range(1, stages[0][1])])
-    mine = jnp.concatenate([pick(stacked, j ^ k) for k in range(stages[0][1])], axis=0)
+    back = flip(w, "morton", 1)
+    both = jnp.stack([w, back])
+    mine = jnp.concatenate([pick(both, low), pick(both, 1 - low)], axis=0)
     mine, done = lax.optimization_barrier((mine, finish(early, got)))
     return mine, flip(mine, "dp", 1), done
 
@@ -385,46 +358,43 @@
 
     ghost = sds((q, H), BF)
     far, one, two = call(
-        pack_kernel, "pack_ghosts", (ghost,) * 3, [HBM] * 2, (VM,) * 3,
-        [like(send_rows), like(h), pltpu.VMEM((128, 128), i32), pltpu.VMEM((G, 128), i32),
-         pltpu.VMEM((G, H), F32), dma((2,))],
+        pack_kernel, "pack_ghosts", (ghost,) * 3, [VM] * 2, (VM,) * 3,
+        [pltpu.VMEM((LANES, LANES), i32), pltpu.VMEM((G, LANES), BF),
+         pltpu.VMEM((G, LANES), BF), pltpu.VMEM((G, H), F32)],
         4_000_000_000, 8_000_000, 8,
     )(send_rows, h)
     far = flip(far, "morton", half)
     one = flip(one, "morton", 1)
     two = cross_pairs(two)
 
-    part, pg, pr, ptr, pts = call(
-        pre_kernel, "edge_pre",
-        (sds((E, H), F32), sds((E, G), BF), sds((E, C), BF), sds((C, E), BF), sds((T, E), BF)),
-        [HBM] * 5, (VM,) * 5,
-        [like(h), like(e), like(senders), like(receivers), like(edge_w1),
-         pltpu.VMEM((128, 128), i32), pltpu.VMEM((E, 128), i32), pltpu.VMEM((E, 128), i32),
-         pltpu.VMEM((H + 2 * C, H), BF), dma((5,))],
+    part, ps, pr = call(
+        pre_kernel, "edge_pre", (sds((E, H), F32), sds((E, T), BF), sds((E, C), BF)),
+        [VM] * 5, (VM,) * 3,
+        [pltpu.VMEM((LANES, LANES), i32)] + [pltpu.VMEM((E, LANES), BF)] * 4
+        + [pltpu.VMEM((H + 2 * C, H), BF)],
         2 * E * H * (H + 2 * C) * 4, 4 * E * (H + T), 24,
     )(h, e, senders, receivers, edge_w1)
 
     rows = -(-(7 * H + 16) // (pair * 32)) * (pair * 32)
     mine_shape = sds((rows // pair, H), BF)
-    hbm_in = [h, e, cn, ce, edge_w1, edge_w2, egain, node_w1, node_w2, ngain]
+    layer_in = [h, e, cn, ce, edge_w1, edge_w2, egain, node_w1, node_w2, ngain]
     gnode, gedge, bfar, bone, btwo, wmine, woth = call(
         main_kernel, "mesh_layer",
         (sds((C, H), F32), sds((E, H), F32), ghost, ghost, ghost, mine_shape, mine_shape),
-        [SM] + [VM] * 8 + [HBM] * 10,
+        [HBM] + [VM] * 16,
         (VM, HBM, VM, VM, VM, VM, VM),
-        [like(x) for x in hbm_in]
-        + [pltpu.VMEM((G, H), BF), pltpu.VMEM((E, H), BF), pltpu.VMEM((E, H), F32),
-           pltpu.VMEM((E, H), F32), pltpu.VMEM((E, 1), F32), pltpu.VMEM((C, H), F32),
+        [pltpu.VMEM((G, H), BF), pltpu.VMEM((E, H), BF), pltpu.VMEM((E, H), F32),
+           pltpu.VMEM((E, H), F32), pltpu.VMEM((E, 1), F32), pltpu.VMEM((H, C), F32),
            pltpu.VMEM((C, H), BF), pltpu.VMEM((E, H), BF), pltpu.VMEM((E, H), BF),
            pltpu.VMEM((E, H), F32), pltpu.VMEM((rows, H), F32), pltpu.VMEM((G, H), F32),
-           dma((10,)), dma((E // BWD_CHUNK,))],
+           pltpu.SMEM((1, 1), i32), dma, dma((E // BWD_CHUNK,))],
         2 * E * H * 4608, 8 * E * H, 36,
-    )(edge_count, part, pg, pr, ptr, pts, far, one, two, *hbm_in)
+    )(edge_count, part, ps, pr, far, one, two, *layer_in)
 
     def finish(rtwo, got):
         return call(
-            node_kernel, "node_grad", sds((C, H), F32), [HBM] + [VM] * 4, VM,
-            [like(send_rows), pltpu.VMEM((G, H), BF), dma((1,))],
+            node_kernel, "node_grad", sds((C, H), F32), [VM] * 5, VM,
+            [pltpu.VMEM((G, H), BF)],
             2 * C * G * H, 8 * C * H, 8,
         )(send_rows, gnode, got[half], got[1], rtwo)
 

time: 51.4 us -> 48.1 us (0.936)
  waiting for transfers between devices: 10.5 us -> 15.3 us
  Pallas kernels: 15.3 us -> 10.8 us
  starting transfers between devices: 22 us -> 18.3 us
    pallas_call x3, Pallas kernels: 7.2 us -> 4.13 us  [the longest x1 2.76 us: on_device(): call(pre_kernel, 'edge_pre', (sds((E, H), F32), sds((E, T), BF), sds((E,...]
    ppermute x13 -> x11, starting transfers between devices: 16.3 us -> 13.8 us  [flip(): return lax.ppermute(x, axis, [(i, i ^ by) for i in range(n)])]
    ppermute x2, waiting for transfers between devices: 3.94 us -> 6.53 us  [cross_pairs(): lax.ppermute(x, 'morton', [(i, (i + 1) % n if i % 2 else (i - 1) % n) for...]
    ppermute x13 -> x11, waiting for transfers between devices: 6.53 us -> 8.79 us  [flip(): return lax.ppermute(x, axis, [(i, i ^ by) for i in range(n)])]
    pallas_call x1, Pallas kernels: 7.31 us -> 5.89 us  [on_device(): call(main_kernel, 'mesh_layer', (sds((C, H), F32), sds((E, H), F32), ghos...]
    ppermute x2, starting transfers between devices: 5.63 us -> 4.56 us  [cross_pairs(): lax.ppermute(x, 'morton', [(i, (i + 1) % n if i % 2 else (i - 1) % n) for...]
  transfers between devices with their start and end apart: 15 -> 13, of which waited for: 6 -> 8; matrix products, arithmetic and copies ran while one was open for 0% -> 0% of each run, Pallas kernels for 13% -> 8%
where the time goes in v3:
time: 48.1 us; the launch traced here: 47.9 us
  starting transfers between devices  18.3 us (38%)
  waiting for transfers between devices  15.3 us (32%)
  Pallas kernels  10.8 us (22%)
  local copies, waits for them, and re-layouts  1.67 us (3%)
  between operations  1.59 us (3%)
    ppermute x11, starting transfers between devices, flip(): return lax.ppermute(x, axis, [(i, i ^ by) for i in range(n)])  13.8 us
    ppermute x11, waiting for transfers between devices, flip(): return lax.ppermute(x, axis, [(i, i ^ by) for i in range(n)])  8.79 us
    ppermute x2, waiting for transfers between devices, cross_pairs(): lax.ppermute(x, 'morton', [(i, (i + 1) % n if i % 2 else (i - 1) % n) for...  6.53 us
    pallas_call x1, Pallas kernels, on_device(): call(main_kernel, 'mesh_layer', (sds((C, H), F32), sds((E, H), F32), ghos...  5.89 us
    ppermute x2, starting transfers between devices, cross_pairs(): lax.ppermute(x, 'morton', [(i, (i + 1) % n if i % 2 else (i - 1) % n) for...  4.56 us
    pallas_call x1, Pallas kernels, on_device(): call(pre_kernel, 'edge_pre', (sds((E, H), F32), sds((E, T), BF), sds((E,...  2.76 us
    unnamed x30, local copies, waits for them, and re-layouts  1.65 us
    pallas_call x1, Pallas kernels, finish(): call(node_kernel, 'node_grad', sds((C, H), F32), [VM] * 5, VM, [pltpu.VME...  0.96 us
  transfers between devices with their start and end apart: 13, of which 8 were waited for; matrix products, arithmetic and copies ran while one was open for 0% of the time, Pallas kernels for 8%

profile of v3, /device:TPU:0, one launch (start us, length us, event | category | flops | bytes accessed | tf_op | source)
XLA Modules:
  0.0 47.9 jit_solution(11597494223845084861)
XLA Ops:
  0.6 0.0 copy-start
  0.6 0.7 %copy-done = s32[1,256]{1,0:T(1,128)S(1)} copy-done((s32[1,256]{1,0:T(1,128)S(1)}, s32[1,256]{1,0:T(1,128)}, u32[]{:S(2)}) %copy-start) | copy-done | bytes 1048
  1.3 0.9 %copy-done.5 = bf16[1,512,128]{2,1,0:T(8,128)(2,1)S(1)} copy-done((bf16[1,512,128]{2,1,0:T(8,128)(2,1)S(1)}, bf16[1,512,128]{2,1,0:T(8,128)(2,1)}, u32[]{:S(2)}) %copy-start.5) | copy-done | bytes 131096
  2.2 0.4 pack_ghosts.1
  2.7 4.1 %collective-permute-start = (bf16[64,128]{1,0:T(8,128)(2,1)S(1)}, bf16[64,128]{1,0:T(8,128)(2,1)S(1)}, u32[]{:S(2)}, u32[]{:S(2)}) collective-permute-start(bf16[64,128]{1,0:T(8,128)(2,1)S(1)} %get-tuple-element.34), channel_id=1, source_target_pairs={{0,16},{2,18},{4,20},{6,22},{8,24},{10,26},{12,28},{14,30},{16,0},... | collective-permute-start | bytes 49160 | tf_op jit(solution)/shard_map/ppermute | solution.py:278
  6.8 1.5 %collective-permute-start.1 = (bf16[64,128]{1,0:T(8,128)(2,1)S(1)}, bf16[64,128]{1,0:T(8,128)(2,1)S(1)}, u32[]{:S(2)}, u32[]{:S(2)}) collective-permute-start(bf16[64,128]{1,0:T(8,128)(2,1)S(1)} %get-tuple-element.35), channel_id=1, source_target_pairs={{0,2},{2,0},{4,6},{6,4},{8,10},{10,8},{12,14},{14,12},{16,18},{18,... | collective-permute-start | bytes 49160 | tf_op jit(solution)/shard_map/ppermute | solution.py:278
  8.3 2.3 %collective-permute-start.2 = (bf16[64,128]{1,0:T(8,128)(2,1)S(1)}, bf16[64,128]{1,0:T(8,128)(2,1)S(1)}, u32[]{:S(2)}, u32[]{:S(2)}) collective-permute-start(bf16[64,128]{1,0:T(8,128)(2,1)S(1)} %get-tuple-element.36), channel_id=1, source_target_pairs={{0,30},{2,4},{4,2},{6,8},{8,6},{10,12},{12,10},{14,16},{16,14},{18... | collective-permute-start | bytes 49160 | tf_op jit(solution)/shard_map/ppermute | solution.py:283
  10.6 0.0 copy-start.3
  10.6 0.0 copy-start.9
  10.6 0.0 copy-start.10
  10.7 2.8 %edge_pre.1 = (f32[2048,128]{1,0:T(8,128)S(1)}, bf16[2048,768]{1,0:T(8,128)(2,1)S(1)}, bf16[2048,512]{1,0:T(8,128)(2,1)S(1)}) custom-call(bf16[512,128]{1,0:T(8,128)(2,1)S(1)} %bitcast.25, bf16[2048,128]{1,0:T(8,128)(2,1)S(1)} %bitcast.21, s32[1,2048]{1,0:T(1,128)S(1)} %copy-done.11, s32[1,2048]{1,0:T(1,128)S(1)} %copy-done.12, f32[384,128]{1,0:T(8,128)S(1)} %copy-done.4), custom_call_target="tpu_custom_call" | custom-call | flops 2415919104 | bytes 7340032 | tf_op jit(solution)/shard_map/edge_pre/pallas_call | solution.py:370
  14.1 1.5 %collective-permute-done.2.two_ref = bf16[64,128]{1,0:T(8,128)(2,1)S(1)} collective-permute-done((bf16[64,128]{1,0:T(8,128)(2,1)S(1)}, bf16[64,128]{1,0:T(8,128)(2,1)S(1)}, u32[]{:S(2)}, u32[]{:S(2)}) %collective-permute-start.2) | collective-permute-done | bytes 16416 | tf_op jit(solution)/shard_map/ppermute | solution.py:283
  15.7 5.9 %mesh_layer.1 = (f32[512,128]{1,0:T(8,128)S(1)}, f32[2048,128]{1,0:T(8,128)}, bf16[64,128]{1,0:T(8,128)(2,1)S(1)}, bf16[64,128]{1,0:T(8,128)(2,1)S(1)}, bf16[64,...) custom-call(s32[1,1]{1,0:T(1,128)S(6)} %copy.22.count_hbm, ...), custom_call_target="tpu_custom_call" | custom-call | flops 2415919104 | bytes 2097152 | tf_op jit(solution)/shard_map/mesh_layer/pallas_call | solution.py:381
  21.6 0.1 collective-permute-start.3
  21.7 1.3 %collective-permute-done.3 = bf16[480,128]{1,0:T(8,128)(2,1)S(1)} collective-permute-done((bf16[480,128]{1,0:T(8,128)(2,1)S(1)}, bf16[480,128]{1,0:T(8,128)(2,1)S(1)}, u32[]{:S(2)}, u32[]{:S(2)}) %collective-permute-start.3) | collective-permute-done | bytes 122912 | tf_op jit(solution)/shard_map/ppermute | solution.py:278
  23.1 0.1 collective-permute-start.4
  23.1 0.7 %collective-permute-start.5 = (bf16[240,128]{1,0:T(8,128)(2,1)S(1)}, bf16[240,128]{1,0:T(8,128)(2,1)S(1)}, u32[]{:S(2)}, u32[]{:S(2)}) collective-permute-start(bf16[240,128]{1,0:T(8,128)(2,1)S(1)} %get-tuple-element.56), channel_id=1, source_target_pairs={{0,4},{2,6},{4,0},{6,2},{8,12},{10,14},{12,8},{14,10},{16,20},{18,... | collective-permute-start | bytes 184328 | tf_op jit(solution)/shard_map/ppermute | solution.py:278
  23.9 2.7 %collective-permute-start.6 = (bf16[240,128]{1,0:T(8,128)(2,1)S(1)}, bf16[240,128]{1,0:T(8,128)(2,1)S(1)}, u32[]{:S(2)}, u32[]{:S(2)}) collective-permute-start(bf16[240,128]{1,0:T(8,128)(2,1)S(1)} %get-tuple-element.57), channel_id=1, source_target_pairs={{0,6},{2,4},{4,2},{6,0},{8,14},{10,12},{12,10},{14,8},{16,22},{18,... | collective-permute-start | bytes 184328 | tf_op jit(solution)/shard_map/ppermute | solution.py:278
  26.6 2.3 %collective-permute-start.7 = (bf16[64,128]{1,0:T(8,128)(2,1)S(1)}, bf16[64,128]{1,0:T(8,128)(2,1)S(1)}, u32[]{:S(2)}, u32[]{:S(2)}) collective-permute-start(bf16[64,128]{1,0:T(8,128)(2,1)S(1)} %get-tuple-element.40), channel_id=1, source_target_pairs={{0,30},{2,4},{4,2},{6,8},{8,6},{10,12},{12,10},{14,16},{16,14},{18... | collective-permute-start | bytes 49160 | tf_op jit(solution)/shard_map/ppermute | solution.py:283
  28.9 0.1 collective-permute-done.6
  29.0 5.0 %collective-permute-done.7.two_ref = bf16[64,128]{1,0:T(8,128)(2,1)S(1)} collective-permute-done((bf16[64,128]{1,0:T(8,128)(2,1)S(1)}, bf16[64,128]{1,0:T(8,128)(2,1)S(1)}, u32[]{:S(2)}, u32[]{:S(2)}) %collective-permute-start.7) | collective-permute-done | bytes 16416 | tf_op jit(solution)/shard_map/ppermute | solution.py:283
  34.1 0.1 collective-permute-start.8
  34.1 4.3 %collective-permute-start.10 = (bf16[240,128]{1,0:T(8,128)(2,1)S(1)}, bf16[240,128]{1,0:T(8,128)(2,1)S(1)}, u32[]{:S(2)}, u32[]{:S(2)}) collective-permute-start(bf16[240,128]{1,0:T(8,128)(2,1)S(1)} %add_add_fusion), channel_id=1, source_target_pairs={{0,24},{2,26},{4,28},{6,30},{8,16},{10,18},{12,20},{14,22},{16,8},... | collective-permute-start | bytes 184328 | tf_op jit(solution)/shard_map/ppermute | solution.py:278
  38.4 1.3 %collective-permute-done.8 = bf16[240,128]{1,0:T(8,128)(2,1)S(1)} collective-permute-done((bf16[240,128]{1,0:T(8,128)(2,1)S(1)}, bf16[240,128]{1,0:T(8,128)(2,1)S(1)}, u32[]{:S(2)}, u32[]{:S(2)}) %collective-permute-start.8) | collective-permute-done | bytes 61472 | tf_op jit(solution)/shard_map/ppermute | solution.py:278
  39.7 1.6 %collective-permute-done.10 = bf16[240,128]{1,0:T(8,128)(2,1)S(1)} collective-permute-done((bf16[240,128]{1,0:T(8,128)(2,1)S(1)}, bf16[240,128]{1,0:T(8,128)(2,1)S(1)}, u32[]{:S(2)}, u32[]{:S(2)}) %collective-permute-start.10) | collective-permute-done | bytes 61472 | tf_op jit(solution)/shard_map/ppermute | solution.py:278
  41.3 0.1 collective-permute-start.11
  41.5 1.0 %node_grad.1 = f32[512,128]{1,0:T(8,128)} custom-call(s32[1,256]{1,0:T(1,128)S(1)} %copy-done.1, f32[512,128]{1,0:T(8,128)S(1)} %get-tuple-element.43.gnode_ref, bf16[64,128]{1,0:T(8,128)(2,1)S(1)} %slice.18.far_ref, bf16[64,128]{1,0:T(8,128)(2,1)S(1)} %slice.19.one_ref, bf16[64,128]{1,0:T(8,128)(2,1)S(1)} %collective-permute-done.7.two_ref), custom_call_target="tpu_custom_call" | custom-call | flops 33554432 | bytes 524288 | tf_op jit(solution)/shard_map/node_grad/pallas_call | solution.py:395
  42.4 3.2 %collective-permute-done.11 = bf16[240,128]{1,0:T(8,128)(2,1)S(1)} collective-permute-done((bf16[240,128]{1,0:T(8,128)(2,1)S(1)}, bf16[240,128]{1,0:T(8,128)(2,1)S(1)}, u32[]{:S(2)}, u32[]{:S(2)}) %collective-permute-start.11) | collective-permute-done | bytes 61472 | tf_op jit(solution)/shard_map/ppermute | solution.py:278
  45.6 0.1 fusion.3
  45.7 0.1 collective-permute-start.12
  45.8 1.3 %collective-permute-done.12.oth_ref = bf16[480,128]{1,0:T(8,128)(2,1)S(1)} collective-permute-done((bf16[480,128]{1,0:T(8,128)(2,1)S(1)}, bf16[480,128]{1,0:T(8,128)(2,1)S(1)}, u32[]{:S(2)}, u32[]{:S(2)}) %collective-permute-start.12) | collective-permute-done | bytes 122912 | tf_op jit(solution)/shard_map/ppermute | solution.py:278
  47.1 0.8 %weight_grads.1 = (f32[384,128]{1,0:T(8,128)}, f32[128,128]{1,0:T(8,128)}, f32[1,128]{1,0:T(1,128)}, f32[256,128]{1,0:T(8,128)}, f32[128,128]{1,0:T(8,128)}, /*index=5*/f32[1,128]{1,0:T(1,128)}) custom-call(bf16[480,128]{1,0:T(8,128)(2,1)S(1)} %pad_maximum_fusion.mine_ref, bf16[480,128]{1,0:T(8,128)(2,1)S(1)} %collective-permute-done.12.oth_ref), custom_call_target="tpu_custom_call" | custom-call | flops 122880 | bytes 983040 | tf_op jit(solution)/shard_map/weight_grads/pallas_call | solution.py:405
  (39 shorter events, 0.2 us)
Async XLA Ops:
  0.6 0.7 %copy-start = (s32[1,256]{1,0:T(1,128)S(1)}, s32[1,256]{1,0:T(1,128)}, u32[]{:S(2)}) copy-start(s32[1,256]{1,0:T(1,128)} %rows_s.3) | copy-start | bytes 3076
  1.3 0.9 %copy-start.5 = (bf16[1,512,128]{2,1,0:T(8,128)(2,1)S(1)}, bf16[1,512,128]{2,1,0:T(8,128)(2,1)}, u32[]{:S(2)}) copy-start(bf16[1,512,128]{2,1,0:T(8,128)(2,1)} %param.14) | copy-start | bytes 393220
  2.2 8.3 %copy-start.2 = (bf16[1,2048,128]{2,1,0:T(8,128)(2,1)S(1)}, bf16[1,2048,128]{2,1,0:T(8,128)(2,1)}, u32[]{:S(2)}) copy-start(bf16[1,2048,128]{2,1,0:T(8,128)(2,1)} %param.15) | copy-start | bytes 1572868
  2.2 8.3 %copy-start.4 = (f32[384,128]{1,0:T(8,128)S(1)}, f32[384,128]{1,0:T(8,128)}, u32[]{:S(2)}) copy-start(f32[384,128]{1,0:T(8,128)} %w1_s.3) | copy-start | bytes 589828
  2.2 8.3 %copy-start.6 = (bf16[1,512,128]{2,1,0:T(8,128)(2,1)S(1)}, bf16[1,512,128]{2,1,0:T(8,128)(2,1)}, u32[]{:S(2)}) copy-start(bf16[1,512,128]{2,1,0:T(8,128)(2,1)} %param.14) | copy-start | bytes 393220
  2.2 8.3 %copy-start.11 = (s32[1,2048]{1,0:T(1,128)S(1)}, s32[1,2048]{1,0:T(1,128)}, u32[]{:S(2)}) copy-start(s32[1,2048]{1,0:T(1,128)} %snd_s.1) | copy-start | bytes 24580
  2.2 8.3 %copy-start.12 = (s32[1,2048]{1,0:T(1,128)S(1)}, s32[1,2048]{1,0:T(1,128)}, u32[]{:S(2)}) copy-start(s32[1,2048]{1,0:T(1,128)} %rcv_s.1) | copy-start | bytes 24580
  2.7 11.4 %collective-permute-start = (bf16[64,128]{1,0:T(8,128)(2,1)S(1)}, bf16[64,128]{1,0:T(8,128)(2,1)S(1)}, u32[]{:S(2)}, u32[]{:S(2)}) collective-permute-start(bf16[64,128]{1,0:T(8,128)(2,1)S(1)} %get-tuple-element.34), channel_id=1, source_target_pairs={{0,16},{2,18},{4,20},{6,22},{8,24},{10,26},{12,28},{14,30},{16,0},... | collective-permute-start | bytes 49160 | tf_op jit(solution)/shard_map/ppermute | solution.py:278
  6.8 7.3 %collective-permute-start.1 = (bf16[64,128]{1,0:T(8,128)(2,1)S(1)}, bf16[64,128]{1,0:T(8,128)(2,1)S(1)}, u32[]{:S(2)}, u32[]{:S(2)}) collective-permute-start(bf16[64,128]{1,0:T(8,128)(2,1)S(1)} %get-tuple-element.35), channel_id=1, source_target_pairs={{0,2},{2,0},{4,6},{6,4},{8,10},{10,8},{12,14},{14,12},{16,18},{18,... | collective-permute-start | bytes 49160 | tf_op jit(solution)/shard_map/ppermute | solution.py:278
  8.3 7.3 %collective-permute-start.2 = (bf16[64,128]{1,0:T(8,128)(2,1)S(1)}, bf16[64,128]{1,0:T(8,128)(2,1)S(1)}, u32[]{:S(2)}, u32[]{:S(2)}) collective-permute-start(bf16[64,128]{1,0:T(8,128)(2,1)S(1)} %get-tuple-element.36), channel_id=1, source_target_pairs={{0,30},{2,4},{4,2},{6,8},{8,6},{10,12},{12,10},{14,16},{16,14},{18... | collective-permute-start | bytes 49160 | tf_op jit(solution)/shard_map/ppermute | solution.py:283
  10.6 5.0 %copy-start.3 = (bf16[1,2048,128]{2,1,0:T(8,128)(2,1)S(1)}, bf16[1,2048,128]{2,1,0:T(8,128)(2,1)}, u32[]{:S(2)}) copy-start(bf16[1,2048,128]{2,1,0:T(8,128)(2,1)} %param.17) | copy-start | bytes 1572868
  10.6 5.0 %copy-start.7 = (bf16[1,512,128]{2,1,0:T(8,128)(2,1)S(1)}, bf16[1,512,128]{2,1,0:T(8,128)(2,1)}, u32[]{:S(2)}) copy-start(bf16[1,512,128]{2,1,0:T(8,128)(2,1)} %param.16) | copy-start | bytes 393220
  10.6 5.0 %copy-start.8 = (f32[256,128]{1,0:T(8,128)S(1)}, f32[256,128]{1,0:T(8,128)}, u32[]{:S(2)}) copy-start(f32[256,128]{1,0:T(8,128)} %nw1_s.1) | copy-start | bytes 393220
  10.6 5.0 %copy-start.9 = (f32[128,128]{1,0:T(8,128)S(1)}, f32[128,128]{1,0:T(8,128)}, u32[]{:S(2)}) copy-start(f32[128,128]{1,0:T(8,128)} %w2_s.1) | copy-start | bytes 196612
  10.6 5.0 %copy-start.10 = (f32[128,128]{1,0:T(8,128)S(1)}, f32[128,128]{1,0:T(8,128)}, u32[]{:S(2)}) copy-start(f32[128,128]{1,0:T(8,128)} %nw2_s.1) | copy-start | bytes 196612
  10.6 5.0 %copy-start.13 = (f32[128]{0:T(128)S(1)}, f32[128]{0:T(128)}, u32[]{:S(2)}) copy-start(f32[128]{0:T(128)} %param.24) | copy-start | bytes 1540
  10.6 5.0 %copy-start.14 = (f32[128]{0:T(128)S(1)}, f32[128]{0:T(128)}, u32[]{:S(2)}) copy-start(f32[128]{0:T(128)} %param.27) | copy-start | bytes 1540
  15.7 25.8 %copy-start.1 = (s32[1,256]{1,0:T(1,128)S(1)}, s32[1,256]{1,0:T(1,128)}, u32[]{:S(2)}) copy-start(s32[1,256]{1,0:T(1,128)} %rows_s.3) | copy-start | bytes 3076
  21.6 1.4 %collective-permute-start.3 = (bf16[480,128]{1,0:T(8,128)(2,1)S(1)}, bf16[480,128]{1,0:T(8,128)(2,1)S(1)}, u32[]{:S(2)}, u32[]{:S(2)}) collective-permute-start(bf16[480,128]{1,0:T(8,128)(2,1)S(1)} %get-tuple-element.38), channel_id=1, source_target_pairs={{0,1},{1,0},{2,3},{3,2},{4,5},{5,4},{6,7},{7,6},{8,9},{9,8},{10,11... | collective-permute-start | bytes 368648 | tf_op jit(solution)/shard_map/ppermute | solution.py:278
  23.1 5.9 %collective-permute-start.4 = (bf16[304,128]{1,0:T(8,128)(2,1)S(1)}, bf16[304,128]{1,0:T(8,128)(2,1)S(1)}, u32[]{:S(2)}, u32[]{:S(2)}) collective-permute-start(bf16[304,128]{1,0:T(8,128)(2,1)S(1)} %pad_maximum_fusion.1), channel_id=1, source_target_pairs={{0,2},{2,0},{4,6},{6,4},{8,10},{10,8},{12,14},{14,12},{16,18},{18,... | collective-permute-start | bytes 233480 | tf_op jit(solution)/shard_map/ppermute | solution.py:278
  23.1 5.8 %collective-permute-start.5 = (bf16[240,128]{1,0:T(8,128)(2,1)S(1)}, bf16[240,128]{1,0:T(8,128)(2,1)S(1)}, u32[]{:S(2)}, u32[]{:S(2)}) collective-permute-start(bf16[240,128]{1,0:T(8,128)(2,1)S(1)} %get-tuple-element.56), channel_id=1, source_target_pairs={{0,4},{2,6},{4,0},{6,2},{8,12},{10,14},{12,8},{14,10},{16,20},{18,... | collective-permute-start | bytes 184328 | tf_op jit(solution)/shard_map/ppermute | solution.py:278
  23.9 5.1 %collective-permute-start.6 = (bf16[240,128]{1,0:T(8,128)(2,1)S(1)}, bf16[240,128]{1,0:T(8,128)(2,1)S(1)}, u32[]{:S(2)}, u32[]{:S(2)}) collective-permute-start(bf16[240,128]{1,0:T(8,128)(2,1)S(1)} %get-tuple-element.57), channel_id=1, source_target_pairs={{0,6},{2,4},{4,2},{6,0},{8,14},{10,12},{12,10},{14,8},{16,22},{18,... | collective-permute-start | bytes 184328 | tf_op jit(solution)/shard_map/ppermute | solution.py:278
  26.6 7.4 %collective-permute-start.7 = (bf16[64,128]{1,0:T(8,128)(2,1)S(1)}, bf16[64,128]{1,0:T(8,128)(2,1)S(1)}, u32[]{:S(2)}, u32[]{:S(2)}) collective-permute-start(bf16[64,128]{1,0:T(8,128)(2,1)S(1)} %get-tuple-element.40), channel_id=1, source_target_pairs={{0,30},{2,4},{4,2},{6,8},{8,6},{10,12},{12,10},{14,16},{16,14},{18... | collective-permute-start | bytes 49160 | tf_op jit(solution)/shard_map/ppermute | solution.py:283
  34.1 7.2 %collective-permute-start.9 = (bf16[304,128]{1,0:T(8,128)(2,1)S(1)}, bf16[304,128]{1,0:T(8,128)(2,1)S(1)}, u32[]{:S(2)}, u32[]{:S(2)}) collective-permute-start(bf16[304,128]{1,0:T(8,128)(2,1)S(1)} %pad_maximum_fusion.2), channel_id=1, source_target_pairs={{0,16},{2,18},{4,20},{6,22},{8,24},{10,26},{12,28},{14,30},{16,0},... | collective-permute-start | bytes 233480 | tf_op jit(solution)/shard_map/ppermute | solution.py:278
  34.1 5.6 %collective-permute-start.8 = (bf16[240,128]{1,0:T(8,128)(2,1)S(1)}, bf16[240,128]{1,0:T(8,128)(2,1)S(1)}, u32[]{:S(2)}, u32[]{:S(2)}) collective-permute-start(bf16[240,128]{1,0:T(8,128)(2,1)S(1)} %add_add_fusion), channel_id=1, source_target_pairs={{0,8},{2,10},{4,12},{6,14},{8,0},{10,2},{12,4},{14,6},{16,24},{18,... | collective-permute-start | bytes 184328 | tf_op jit(solution)/shard_map/ppermute | solution.py:278
  34.1 7.2 %collective-permute-start.10 = (bf16[240,128]{1,0:T(8,128)(2,1)S(1)}, bf16[240,128]{1,0:T(8,128)(2,1)S(1)}, u32[]{:S(2)}, u32[]{:S(2)}) collective-permute-start(bf16[240,128]{1,0:T(8,128)(2,1)S(1)} %add_add_fusion), channel_id=1, source_target_pairs={{0,24},{2,26},{4,28},{6,30},{8,16},{10,18},{12,20},{14,22},{16,8},... | collective-permute-start | bytes 184328 | tf_op jit(solution)/shard_map/ppermute | solution.py:278
  41.3 4.3 %collective-permute-start.11 = (bf16[240,128]{1,0:T(8,128)(2,1)S(1)}, bf16[240,128]{1,0:T(8,128)(2,1)S(1)}, u32[]{:S(2)}, u32[]{:S(2)}) collective-permute-start(bf16[240,128]{1,0:T(8,128)(2,1)S(1)} %add_convert_fusion.1), channel_id=1, source_target_pairs={{0,2},{2,0},{4,6},{6,4},{8,10},{10,8},{12,14},{14,12},{16,18},{18,... | collective-permute-start | bytes 184328 | tf_op jit(solution)/shard_map/ppermute | solution.py:278
  45.7 1.4 %collective-permute-start.12 = (bf16[480,128]{1,0:T(8,128)(2,1)S(1)}, bf16[480,128]{1,0:T(8,128)(2,1)S(1)}, u32[]{:S(2)}, u32[]{:S(2)}) collective-permute-start(bf16[480,128]{1,0:T(8,128)(2,1)S(1)} %pad_maximum_fusion.mine_ref), channel_id=1, source_target_pairs={{0,1},{1,0},{2,3},{3,2},{4,5},{5,4},{6,7},{7,6},{8,9},{9,8},{10,11... | collective-permute-start | bytes 368648 | tf_op jit(solution)/shard_map/ppermute | solution.py:278

commit v4 on v3

--- a/solution.py
+++ b/solution.py
@@ -6,6 +6,7 @@
 from jax.experimental import pallas as pl
 from jax.experimental.pallas import tpu as pltpu
 from jax.sharding import PartitionSpec as P
+
 
 BF = jnp.bfloat16
 F32 = jnp.float32
@@ -85,8 +86,8 @@
             at += 1
 
 
-def pack_kernel(rows_s, h_s, far_ref, one_ref, two_ref, tmat, low, high, got):
-    spread([rows_s], tmat, [(low, high)])
+def pack_kernel(meta_ref, h_s, far_ref, one_ref, two_ref, tmat, low, high, got):
+    spread([meta_ref.at[:, : low.shape[0]]], tmat, [(low, high)])
     hot = one_hot_cols(low[...], high[...], h_s.shape[0])
     got[...] = mm(hot, h_s[...])
     upper, odd = my_place()
@@ -109,27 +110,21 @@
     rhs[H : H + C, :] = mm(h, w1[H : 2 * H]).astype(BF)
     rhs[H + C :, :] = mm(h, w1[2 * H :]).astype(BF)
 
-    def step(i, carry):
-        at = pl.ds(pl.multiple_of(i * PRE_CHUNK, PRE_CHUNK), PRE_CHUNK)
+    for i in range(E // PRE_CHUNK):
+        at = pl.ds(i * PRE_CHUNK, PRE_CHUNK)
         p_s = one_hot_cols(low_s[at, :], high_s[at, :], T)
         p_r = one_hot_cols(low_r[at, :], high_r[at, :], C)
         ps_ref[at, :] = p_s
         pr_ref[at, :] = p_r
         part_ref[at, :] = mm(jnp.concatenate([e_s[at, :], p_s[:, :C], p_r], axis=1), rhs[...])
-        return carry
-
-    lax.fori_loop(0, E // PRE_CHUNK, step, 0)
 
 
 def main_kernel(
-    count_hbm, part_ref, ps_ref, pr_ref, far_ref, one_ref, two_ref,
+    count_ref, part_ref, ps_ref, pr_ref, far_ref, one_ref, two_ref,
     h_s, e_s, cn_s, ce_s, w1_s, w2_s, eg_s, nw1_s, nw2_s, ng_s,
     gnode_ref, gedge_hbm, bfar_ref, bone_ref, btwo_ref, wmine_ref, woth_ref,
-    gh_s, p_s, dsil_s, nrm_s, inv_s, agg, dagg_s, db_s, da_s, gedge_s, wg, dgh, count_s,
-    count_sem, out_sems,
+    gh_s, p_s, dsil_s, nrm_s, inv_s, agg, dagg_s, db_s, da_s, gedge_s, wg, dgh, out_sems,
 ):
-    count_copy = pltpu.make_async_copy(count_hbm, count_s, count_sem)
-    count_copy.start()
     C, H = h_s.shape
     E = e_s.shape[0]
     G = gh_s.shape[0]
@@ -145,8 +140,7 @@
     egain = eg_s[...]
     gtab = mm(gh_s[...], w1s).astype(BF)
     agg[...] = jnp.zeros_like(agg)
-    count_copy.wait()
-    count = count_s[0, 0]
+    count = count_ref[...]
 
     def fwd(i, carry):
         at = pl.ds(pl.multiple_of(i * FWD_CHUNK, FWD_CHUNK), FWD_CHUNK)
@@ -228,14 +222,14 @@
         out_copy(i).wait()
 
 
-def node_kernel(rows_s, gnode_ref, far_ref, one_ref, two_ref, out_ref, ret):
+def node_kernel(meta_ref, gnode_ref, far_ref, one_ref, two_ref, out_ref, ret):
     upper, odd = my_place()
     q = far_ref.shape[0]
     ret[...] = jnp.zeros_like(ret)
     ret[pl.ds(pl.multiple_of((1 - upper) * 3 * q, q), q), :] = far_ref[...]
     ret[pl.ds(pl.multiple_of((2 - odd) * q, q), q), :] = one_ref[...]
     ret[pl.ds(pl.multiple_of((1 + odd) * q, q), q), :] = two_ref[...]
-    out_ref[...] = gnode_ref[...] + mm(one_hot_rows(rows_s[...], out_ref.shape[0]), ret[...])
+    out_ref[...] = gnode_ref[...] + mm(one_hot_rows(meta_ref[:, : ret.shape[0]], out_ref.shape[0]), ret[...])
 
 
 def unpack_kernel(factor, mine_ref, oth_ref, g1, g2, gg, gn1, gn2, gng, wg):
@@ -260,7 +254,7 @@
     return jax.ShapeDtypeStruct(shape, dtype)
 
 
-def call(kernel, name, outs, in_specs, out_specs, scratch, flops, nbytes, limit):
+def call(kernel, outs, in_specs, out_specs, scratch, flops, nbytes, limit):
     return pl.pallas_call(
         kernel,
         out_shape=outs,
@@ -269,7 +263,6 @@
         scratch_shapes=scratch,
         compiler_params=pltpu.CompilerParams(vmem_limit_bytes=limit * MIB),
         cost_estimate=pl.CostEstimate(flops=flops, bytes_accessed=nbytes, transcendentals=0),
-        name=name,
     )
 
 
@@ -280,7 +273,8 @@
 
 def cross_pairs(x):
     n = lax.axis_size("morton")
-    return lax.ppermute(x, "morton", [(i, (i + 1) % n if i % 2 else (i - 1) % n) for i in range(n)])
+    pairs = [(i, (i + 1 if i % 2 else i - 1) % n) for i in range(n)]
+    return lax.ppermute(x, "morton", pairs)
 
 
 def pick(x, k):
@@ -321,7 +315,8 @@
     kept, given = pick(halves, low), pick(halves, 1 - low)
     parts = [kept.astype(F32)]
     for d in range(1, stages[0][1]):
-        parts.append(flip_with(given if d % 2 else kept, d, extra, got).astype(F32))
+        moved = flip_with(given if d % 2 else kept, d, extra, got)
+        parts.append(moved.astype(F32))
     v, early = lax.optimization_barrier((tree_sum(parts), early))
     for stride, width in stages[1:]:
         w = v.astype(BF)
@@ -339,7 +334,7 @@
     return mine, flip(mine, "dp", 1), done
 
 
-def on_device(
+def local_step(
     node_feat, edge_feat, cot_node, cot_edge, senders, receivers, send_rows, edge_count,
     edge_w1, edge_w2, edge_gain, node_w1, node_w2, node_gain,
 ):
@@ -353,57 +348,57 @@
     q = G // 4
     T = C + G
     i32 = jnp.int32
+    meta = jnp.maximum(send_rows, 0)
     dma = pltpu.SemaphoreType.DMA
     egain, ngain = edge_gain.reshape(1, H), node_gain.reshape(1, H)
 
     ghost = sds((q, H), BF)
     far, one, two = call(
-        pack_kernel, "pack_ghosts", (ghost,) * 3, [VM] * 2, (VM,) * 3,
+        pack_kernel, (ghost,) * 3, [VM] * 2, (VM,) * 3,
         [pltpu.VMEM((LANES, LANES), i32), pltpu.VMEM((G, LANES), BF),
          pltpu.VMEM((G, LANES), BF), pltpu.VMEM((G, H), F32)],
         4_000_000_000, 8_000_000, 8,
-    )(send_rows, h)
+    )(meta, h)
     far = flip(far, "morton", half)
     one = flip(one, "morton", 1)
     two = cross_pairs(two)
 
     part, ps, pr = call(
-        pre_kernel, "edge_pre", (sds((E, H), F32), sds((E, T), BF), sds((E, C), BF)),
+        pre_kernel, (sds((E, H), F32), sds((E, T), BF), sds((E, C), BF)),
         [VM] * 5, (VM,) * 3,
         [pltpu.VMEM((LANES, LANES), i32)] + [pltpu.VMEM((E, LANES), BF)] * 4
         + [pltpu.VMEM((H + 2 * C, H), BF)],
         2 * E * H * (H + 2 * C) * 4, 4 * E * (H + T), 24,
     )(h, e, senders, receivers, edge_w1)
 
-    rows = -(-(7 * H + 16) // (pair * 32)) * (pair * 32)
+    rows = -(-(7 * H + 16) // (pair * 16)) * (pair * 16)
     mine_shape = sds((rows // pair, H), BF)
     layer_in = [h, e, cn, ce, edge_w1, edge_w2, egain, node_w1, node_w2, ngain]
     gnode, gedge, bfar, bone, btwo, wmine, woth = call(
-        main_kernel, "mesh_layer",
+        main_kernel,
         (sds((C, H), F32), sds((E, H), F32), ghost, ghost, ghost, mine_shape, mine_shape),
-        [HBM] + [VM] * 16,
+        [VM] * 17,
         (VM, HBM, VM, VM, VM, VM, VM),
         [pltpu.VMEM((G, H), BF), pltpu.VMEM((E, H), BF), pltpu.VMEM((E, H), F32),
            pltpu.VMEM((E, H), F32), pltpu.VMEM((E, 1), F32), pltpu.VMEM((H, C), F32),
            pltpu.VMEM((C, H), BF), pltpu.VMEM((E, H), BF), pltpu.VMEM((E, H), BF),
            pltpu.VMEM((E, H), F32), pltpu.VMEM((rows, H), F32), pltpu.VMEM((G, H), F32),
-           pltpu.SMEM((1, 1), i32), dma, dma((E // BWD_CHUNK,))],
+           dma((E // BWD_CHUNK,))],
         2 * E * H * 4608, 8 * E * H, 36,
     )(edge_count, part, ps, pr, far, one, two, *layer_in)
 
     def finish(rtwo, got):
         return call(
-            node_kernel, "node_grad", sds((C, H), F32), [VM] * 5, VM,
+            node_kernel, sds((C, H), F32), [VM] * 5, VM,
             [pltpu.VMEM((G, H), BF)],
             2 * C * G * H, 8 * C * H, 8,
-        )(send_rows, gnode, got[half], got[1], rtwo)
-
-    mine, oth, grad_node = reduce_all(
-        wmine, woth, {1: bone, half: bfar}, cross_pairs(btwo), finish
-    )
+        )(meta, gnode, got[half], got[1], rtwo)
+
+    rtwo = cross_pairs(btwo)
+    mine, oth, grad_node = reduce_all(wmine, woth, {1: bone, half: bfar}, rtwo, finish)
     factor = float(pair * peers * E) ** -0.5
     g1, g2, gg, gn1, gn2, gng = call(
-        functools.partial(unpack_kernel, factor), "weight_grads",
+        functools.partial(unpack_kernel, factor),
         tuple(sds(s, F32) for s in ((3 * H, H), (H, H), (1, H), (2 * H, H), (H, H), (1, H))),
         [VM] * 2, (VM,) * 6, [pltpu.VMEM((rows, H), F32)], rows * H, 8 * rows * H, 8,
     )(mine, oth)
@@ -418,5 +413,5 @@
     in_specs = (cells,) * 4 + (flat,) * 4 + (P(),) * 6
     out_specs = (cells, cells) + (P(),) * 6
     return jax.shard_map(
-        on_device, mesh=mesh, in_specs=in_specs, out_specs=out_specs, check_vma=False
+        local_step, mesh=mesh, in_specs=in_specs, out_specs=out_specs, check_vma=False
     )

time: 48.1 us -> 47.6 us (0.990)
  Pallas kernels: 10.8 us -> 9.98 us
  other arithmetic: 0.19 us -> 0.87 us
  local copies, waits for them, and re-layouts: 1.67 us -> 0.99 us
    pallas_call x5, Pallas kernels: 10.8 us -> 9.98 us  [the longest x1 5.51 us: local_step(): call(main_kernel, (sds((C, H), F32), sds((E, H), F32), ghost, ghost, ghos...]
    max x0 -> x1, other arithmetic: none -> 0.68 us  [local_step(): meta = jnp.maximum(send_rows, 0)]
    unnamed x30 -> x26, local copies, waits for them, and re-layouts: 1.65 us -> 0.97 us
    ppermute x2, waiting for transfers between devices: 6.53 us -> 7.09 us  [cross_pairs(): return lax.ppermute(x, 'morton', pairs)]
  transfers between devices with their start and end apart: 13 -> 13, of which waited for: 8 -> 7; matrix products, arithmetic and copies ran while one was open for 0% -> 0% of each run, Pallas kernels for 8% -> 7%
where the time goes in v4:
time: 47.6 us; the launch traced here: 47.5 us
  starting transfers between devices  18.3 us (38%)
  waiting for transfers between devices  15.7 us (33%)
  Pallas kernels  9.98 us (21%)
  between operations  1.57 us (3%)
  local copies, waits for them, and re-layouts  0.99 us (2%)
  other arithmetic  0.87 us (2%)
    ppermute x11, starting transfers between devices, flip(): return lax.ppermute(x, axis, [(i, i ^ by) for i in range(n)])  13.8 us
    ppermute x11, waiting for transfers between devices, flip(): return lax.ppermute(x, axis, [(i, i ^ by) for i in range(n)])  8.64 us
    ppermute x2, waiting for transfers between devices, cross_pairs(): return lax.ppermute(x, 'morton', pairs)  7.09 us
    pallas_call x1, Pallas kernels, local_step(): call(main_kernel, (sds((C, H), F32), sds((E, H), F32), ghost, ghost, ghos...  5.51 us
    ppermute x2, starting transfers between devices, cross_pairs(): return lax.ppermute(x, 'morton', pairs)  4.56 us
    pallas_call x1, Pallas kernels, local_step(): call(pre_kernel, (sds((E, H), F32), sds((E, T), BF), sds((E, C), BF)), [V...  2.28 us
    unnamed x26, local copies, waits for them, and re-layouts  0.97 us
    pallas_call x1, Pallas kernels, finish(): call(node_kernel, sds((C, H), F32), [VM] * 5, VM, [pltpu.VMEM((G, H), BF)...  0.96 us
  transfers between devices with their start and end apart: 13, of which 7 were waited for; matrix products, arithmetic and copies ran while one was open for 0% of the time, Pallas kernels for 7%

profile of v4, /device:TPU:0, one launch (start us, length us, event | category | flops | bytes accessed | tf_op | source)
XLA Modules:
  0.0 47.5 jit_solution(15784240577169084819)
XLA Ops:
  0.6 0.7 %broadcast_maximum_fusion.meta_ref = s32[1,256]{1,0:T(1,128)S(1)} fusion(s32[1,256]{1,0:T(1,128)} %param.20), kind=kLoop, calls=%fused_computation.16 | loop fusion | flops 256 | bytes 2048 | tf_op jit(solution)/shard_map/max | solution.py:351
  1.3 0.9 %copy-done.3 = bf16[1,512,128]{2,1,0:T(8,128)(2,1)S(1)} copy-done((bf16[1,512,128]{2,1,0:T(8,128)(2,1)S(1)}, bf16[1,512,128]{2,1,0:T(8,128)(2,1)}, u32[]{:S(2)}) %copy-start.3) | copy-done | bytes 131096
  2.2 0.0 copy-start.10
  2.2 0.4 shard_map.198
  2.7 4.1 %collective-permute-start = (bf16[64,128]{1,0:T(8,128)(2,1)S(1)}, bf16[64,128]{1,0:T(8,128)(2,1)S(1)}, u32[]{:S(2)}, u32[]{:S(2)}) collective-permute-start(bf16[64,128]{1,0:T(8,128)(2,1)S(1)} %get-tuple-element.34), channel_id=1, source_target_pairs={{0,16},{2,18},{4,20},{6,22},{8,24},{10,26},{12,28},{14,30},{16,0},... | collective-permute-start | bytes 49160 | tf_op jit(solution)/shard_map/ppermute | solution.py:271
  6.8 1.5 %collective-permute-start.1 = (bf16[64,128]{1,0:T(8,128)(2,1)S(1)}, bf16[64,128]{1,0:T(8,128)(2,1)S(1)}, u32[]{:S(2)}, u32[]{:S(2)}) collective-permute-start(bf16[64,128]{1,0:T(8,128)(2,1)S(1)} %get-tuple-element.35), channel_id=1, source_target_pairs={{0,2},{2,0},{4,6},{6,4},{8,10},{10,8},{12,14},{14,12},{16,18},{18,... | collective-permute-start | bytes 49160 | tf_op jit(solution)/shard_map/ppermute | solution.py:271
  8.3 2.3 %collective-permute-start.2 = (bf16[64,128]{1,0:T(8,128)(2,1)S(1)}, bf16[64,128]{1,0:T(8,128)(2,1)S(1)}, u32[]{:S(2)}, u32[]{:S(2)}) collective-permute-start(bf16[64,128]{1,0:T(8,128)(2,1)S(1)} %get-tuple-element.36), channel_id=1, source_target_pairs={{0,30},{2,4},{4,2},{6,8},{8,6},{10,12},{12,10},{14,16},{16,14},{18... | collective-permute-start | bytes 49160 | tf_op jit(solution)/shard_map/ppermute | solution.py:277
  10.6 0.0 copy-start.1
  10.6 0.0 copy-start.5
  10.6 0.0 copy-start.8
  10.6 0.0 copy-start.11
  10.7 2.3 %shard_map.197 = (f32[2048,128]{1,0:T(8,128)S(1)}, bf16[2048,768]{1,0:T(8,128)(2,1)S(1)}, bf16[2048,512]{1,0:T(8,128)(2,1)S(1)}) custom-call(bf16[512,128]{1,0:T(8,128)(2,1)S(1)} %bitcast.25, bf16[2048,128]{1,0:T(8,128)(2,1)S(1)} %bitcast.21, s32[1,2048]{1,0:T(1,128)S(1)} %copy-done.9, s32[1,2048]{1,0:T(1,128)S(1)} %copy-done.10, f32[384,128]{1,0:T(8,128)S(1)} %copy-done.2), custom_call_target="tpu_custom_call" | custom-call | flops 2415919104 | bytes 7340032 | tf_op jit(solution)/shard_map/pallas_call | solution.py:366
  13.6 2.0 %collective-permute-done.2.two_ref = bf16[64,128]{1,0:T(8,128)(2,1)S(1)} collective-permute-done((bf16[64,128]{1,0:T(8,128)(2,1)S(1)}, bf16[64,128]{1,0:T(8,128)(2,1)S(1)}, u32[]{:S(2)}, u32[]{:S(2)}) %collective-permute-start.2) | collective-permute-done | bytes 16416 | tf_op jit(solution)/shard_map/ppermute | solution.py:277
  15.7 5.5 %shard_map.199 = (f32[512,128]{1,0:T(8,128)S(1)}, f32[2048,128]{1,0:T(8,128)}, bf16[64,128]{1,0:T(8,128)(2,1)S(1)}, bf16[64,128]{1,0:T(8,128)(2,1)S(1)}, bf16[64...) custom-call(s32[1,1]{1,0:T(1,128)S(6)} %copy.22.count_ref, ...), custom_call_target="tpu_custom_call" | custom-call | flops 2415919104 | bytes 2097152 | tf_op jit(solution)/shard_map/pallas_call | solution.py:377
  21.2 0.1 collective-permute-start.3
  21.3 1.3 %collective-permute-done.3 = bf16[464,128]{1,0:T(8,128)(2,1)S(1)} collective-permute-done((bf16[464,128]{1,0:T(8,128)(2,1)S(1)}, bf16[464,128]{1,0:T(8,128)(2,1)S(1)}, u32[]{:S(2)}, u32[]{:S(2)}) %collective-permute-start.3) | collective-permute-done | bytes 118816 | tf_op jit(solution)/shard_map/ppermute | solution.py:271
  22.7 0.1 collective-permute-start.4
  22.7 0.3 collective-permute-start.5
  23.0 3.2 %collective-permute-start.6 = (bf16[232,128]{1,0:T(8,128)(2,1)S(1)}, bf16[232,128]{1,0:T(8,128)(2,1)S(1)}, u32[]{:S(2)}, u32[]{:S(2)}) collective-permute-start(bf16[232,128]{1,0:T(8,128)(2,1)S(1)} %get-tuple-element.57), channel_id=1, source_target_pairs={{0,6},{2,4},{4,2},{6,0},{8,14},{10,12},{12,10},{14,8},{16,22},{18,... | collective-permute-start | bytes 178184 | tf_op jit(solution)/shard_map/ppermute | solution.py:271
  26.2 2.3 %collective-permute-start.7 = (bf16[64,128]{1,0:T(8,128)(2,1)S(1)}, bf16[64,128]{1,0:T(8,128)(2,1)S(1)}, u32[]{:S(2)}, u32[]{:S(2)}) collective-permute-start(bf16[64,128]{1,0:T(8,128)(2,1)S(1)} %get-tuple-element.40), channel_id=1, source_target_pairs={{0,30},{2,4},{4,2},{6,8},{8,6},{10,12},{12,10},{14,16},{16,14},{18... | collective-permute-start | bytes 49160 | tf_op jit(solution)/shard_map/ppermute | solution.py:277
  28.5 5.1 %collective-permute-done.7.two_ref = bf16[64,128]{1,0:T(8,128)(2,1)S(1)} collective-permute-done((bf16[64,128]{1,0:T(8,128)(2,1)S(1)}, bf16[64,128]{1,0:T(8,128)(2,1)S(1)}, u32[]{:S(2)}, u32[]{:S(2)}) %collective-permute-start.7) | collective-permute-done | bytes 16416 | tf_op jit(solution)/shard_map/ppermute | solution.py:277
  33.7 0.1 collective-permute-start.8
  33.7 4.3 %collective-permute-start.10 = (bf16[232,128]{1,0:T(8,128)(2,1)S(1)}, bf16[232,128]{1,0:T(8,128)(2,1)S(1)}, u32[]{:S(2)}, u32[]{:S(2)}) collective-permute-start(bf16[232,128]{1,0:T(8,128)(2,1)S(1)} %add_add_fusion), channel_id=1, source_target_pairs={{0,24},{2,26},{4,28},{6,30},{8,16},{10,18},{12,20},{14,22},{16,8},... | collective-permute-start | bytes 178184 | tf_op jit(solution)/shard_map/ppermute | solution.py:271
  38.0 1.2 %collective-permute-done.8 = bf16[232,128]{1,0:T(8,128)(2,1)S(1)} collective-permute-done((bf16[232,128]{1,0:T(8,128)(2,1)S(1)}, bf16[232,128]{1,0:T(8,128)(2,1)S(1)}, u32[]{:S(2)}, u32[]{:S(2)}) %collective-permute-start.8) | collective-permute-done | bytes 59424 | tf_op jit(solution)/shard_map/ppermute | solution.py:271
  39.2 1.6 %collective-permute-done.10 = bf16[232,128]{1,0:T(8,128)(2,1)S(1)} collective-permute-done((bf16[232,128]{1,0:T(8,128)(2,1)S(1)}, bf16[232,128]{1,0:T(8,128)(2,1)S(1)}, u32[]{:S(2)}, u32[]{:S(2)}) %collective-permute-start.10) | collective-permute-done | bytes 59424 | tf_op jit(solution)/shard_map/ppermute | solution.py:271
  40.9 0.1 collective-permute-start.11
  41.0 1.0 %shard_map.200 = f32[512,128]{1,0:T(8,128)} custom-call(s32[1,256]{1,0:T(1,128)S(1)} %broadcast_maximum_fusion.meta_ref, f32[512,128]{1,0:T(8,128)S(1)} %get-tuple-element.43.gnode_ref, bf16[64,128]{1,0:T(8,128)(2,1)S(1)} %slice.18.far_ref, bf16[64,128]{1,0:T(8,128)(2,1)S(1)} %slice.19.one_ref, bf16[64,128]{1,0:T(8,128)(2,1)S(1)} %collective-permute-done.7.two_ref), custom_call_target="tpu_custom_call" | custom-call | flops 33554432 | bytes 524288 | tf_op jit(solution)/shard_map/pallas_call | solution.py:391
  42.0 3.2 %collective-permute-done.11 = bf16[232,128]{1,0:T(8,128)(2,1)S(1)} collective-permute-done((bf16[232,128]{1,0:T(8,128)(2,1)S(1)}, bf16[232,128]{1,0:T(8,128)(2,1)S(1)}, u32[]{:S(2)}, u32[]{:S(2)}) %collective-permute-start.11) | collective-permute-done | bytes 59424 | tf_op jit(solution)/shard_map/ppermute | solution.py:271
  45.2 0.1 fusion.3
  45.2 0.1 collective-permute-start.12
  45.3 1.3 %collective-permute-done.12.oth_ref = bf16[464,128]{1,0:T(8,128)(2,1)S(1)} collective-permute-done((bf16[464,128]{1,0:T(8,128)(2,1)S(1)}, bf16[464,128]{1,0:T(8,128)(2,1)S(1)}, u32[]{:S(2)}, u32[]{:S(2)}) %collective-permute-start.12) | collective-permute-done | bytes 118816 | tf_op jit(solution)/shard_map/ppermute | solution.py:271
  46.6 0.8 %shard_map.201 = (f32[384,128]{1,0:T(8,128)}, f32[128,128]{1,0:T(8,128)}, f32[1,128]{1,0:T(1,128)}, f32[256,128]{1,0:T(8,128)}, f32[128,128]{1,0:T(8,128)}, /*index=5*/f32[1,128]{1,0:T(1,128)}) custom-call(bf16[464,128]{1,0:T(8,128)(2,1)S(1)} %pad_maximum_fusion.mine_ref, bf16[464,128]{1,0:T(8,128)(2,1)S(1)} %collective-permute-done.12.oth_ref), custom_call_target="tpu_custom_call" | custom-call | flops 118784 | bytes 950272 | tf_op jit(solution)/shard_map/pallas_call | solution.py:400
  (36 shorter events, 0.2 us)
Async XLA Ops:
  1.3 0.9 %copy-start.3 = (bf16[1,512,128]{2,1,0:T(8,128)(2,1)S(1)}, bf16[1,512,128]{2,1,0:T(8,128)(2,1)}, u32[]{:S(2)}) copy-start(bf16[1,512,128]{2,1,0:T(8,128)(2,1)} %param.14) | copy-start | bytes 393220
  2.2 8.3 %copy-start = (bf16[1,2048,128]{2,1,0:T(8,128)(2,1)S(1)}, bf16[1,2048,128]{2,1,0:T(8,128)(2,1)}, u32[]{:S(2)}) copy-start(bf16[1,2048,128]{2,1,0:T(8,128)(2,1)} %param.15) | copy-start | bytes 1572868
  2.2 8.3 %copy-start.2 = (f32[384,128]{1,0:T(8,128)S(1)}, f32[384,128]{1,0:T(8,128)}, u32[]{:S(2)}) copy-start(f32[384,128]{1,0:T(8,128)} %w1_s.3) | copy-start | bytes 589828
  2.2 8.3 %copy-start.4 = (bf16[1,512,128]{2,1,0:T(8,128)(2,1)S(1)}, bf16[1,512,128]{2,1,0:T(8,128)(2,1)}, u32[]{:S(2)}) copy-start(bf16[1,512,128]{2,1,0:T(8,128)(2,1)} %param.14) | copy-start | bytes 393220
  2.2 8.3 %copy-start.9 = (s32[1,2048]{1,0:T(1,128)S(1)}, s32[1,2048]{1,0:T(1,128)}, u32[]{:S(2)}) copy-start(s32[1,2048]{1,0:T(1,128)} %snd_s.1) | copy-start | bytes 24580
  2.2 8.3 %copy-start.10 = (s32[1,2048]{1,0:T(1,128)S(1)}, s32[1,2048]{1,0:T(1,128)}, u32[]{:S(2)}) copy-start(s32[1,2048]{1,0:T(1,128)} %rcv_s.1) | copy-start | bytes 24580
  2.7 10.9 %collective-permute-start = (bf16[64,128]{1,0:T(8,128)(2,1)S(1)}, bf16[64,128]{1,0:T(8,128)(2,1)S(1)}, u32[]{:S(2)}, u32[]{:S(2)}) collective-permute-start(bf16[64,128]{1,0:T(8,128)(2,1)S(1)} %get-tuple-element.34), channel_id=1, source_target_pairs={{0,16},{2,18},{4,20},{6,22},{8,24},{10,26},{12,28},{14,30},{16,0},... | collective-permute-start | bytes 49160 | tf_op jit(solution)/shard_map/ppermute | solution.py:271
  6.8 6.8 %collective-permute-start.1 = (bf16[64,128]{1,0:T(8,128)(2,1)S(1)}, bf16[64,128]{1,0:T(8,128)(2,1)S(1)}, u32[]{:S(2)}, u32[]{:S(2)}) collective-permute-start(bf16[64,128]{1,0:T(8,128)(2,1)S(1)} %get-tuple-element.35), channel_id=1, source_target_pairs={{0,2},{2,0},{4,6},{6,4},{8,10},{10,8},{12,14},{14,12},{16,18},{18,... | collective-permute-start | bytes 49160 | tf_op jit(solution)/shard_map/ppermute | solution.py:271
  8.3 7.3 %collective-permute-start.2 = (bf16[64,128]{1,0:T(8,128)(2,1)S(1)}, bf16[64,128]{1,0:T(8,128)(2,1)S(1)}, u32[]{:S(2)}, u32[]{:S(2)}) collective-permute-start(bf16[64,128]{1,0:T(8,128)(2,1)S(1)} %get-tuple-element.36), channel_id=1, source_target_pairs={{0,30},{2,4},{4,2},{6,8},{8,6},{10,12},{12,10},{14,16},{16,14},{18... | collective-permute-start | bytes 49160 | tf_op jit(solution)/shard_map/ppermute | solution.py:277
  10.6 5.0 %copy-start.1 = (bf16[1,2048,128]{2,1,0:T(8,128)(2,1)S(1)}, bf16[1,2048,128]{2,1,0:T(8,128)(2,1)}, u32[]{:S(2)}) copy-start(bf16[1,2048,128]{2,1,0:T(8,128)(2,1)} %param.17) | copy-start | bytes 1572868
  10.6 5.0 %copy-start.5 = (bf16[1,512,128]{2,1,0:T(8,128)(2,1)S(1)}, bf16[1,512,128]{2,1,0:T(8,128)(2,1)}, u32[]{:S(2)}) copy-start(bf16[1,512,128]{2,1,0:T(8,128)(2,1)} %param.16) | copy-start | bytes 393220
  10.6 5.0 %copy-start.6 = (f32[256,128]{1,0:T(8,128)S(1)}, f32[256,128]{1,0:T(8,128)}, u32[]{:S(2)}) copy-start(f32[256,128]{1,0:T(8,128)} %nw1_s.1) | copy-start | bytes 393220
  10.6 5.0 %copy-start.7 = (f32[128,128]{1,0:T(8,128)S(1)}, f32[128,128]{1,0:T(8,128)}, u32[]{:S(2)}) copy-start(f32[128,128]{1,0:T(8,128)} %w2_s.1) | copy-start | bytes 196612
  10.6 5.0 %copy-start.8 = (f32[128,128]{1,0:T(8,128)S(1)}, f32[128,128]{1,0:T(8,128)}, u32[]{:S(2)}) copy-start(f32[128,128]{1,0:T(8,128)} %nw2_s.1) | copy-start | bytes 196612
  10.6 5.0 %copy-start.11 = (f32[128]{0:T(128)S(1)}, f32[128]{0:T(128)}, u32[]{:S(2)}) copy-start(f32[128]{0:T(128)} %param.24) | copy-start | bytes 1540
  10.6 5.0 %copy-start.12 = (f32[128]{0:T(128)S(1)}, f32[128]{0:T(128)}, u32[]{:S(2)}) copy-start(f32[128]{0:T(128)} %param.27) | copy-start | bytes 1540
  21.2 1.4 %collective-permute-start.3 = (bf16[464,128]{1,0:T(8,128)(2,1)S(1)}, bf16[464,128]{1,0:T(8,128)(2,1)S(1)}, u32[]{:S(2)}, u32[]{:S(2)}) collective-permute-start(bf16[464,128]{1,0:T(8,128)(2,1)S(1)} %get-tuple-element.38), channel_id=1, source_target_pairs={{0,1},{1,0},{2,3},{3,2},{4,5},{5,4},{6,7},{7,6},{8,9},{9,8},{10,11... | collective-permute-start | bytes 356360 | tf_op jit(solution)/shard_map/ppermute | solution.py:271
  22.7 5.8 %collective-permute-start.4 = (bf16[296,128]{1,0:T(8,128)(2,1)S(1)}, bf16[296,128]{1,0:T(8,128)(2,1)S(1)}, u32[]{:S(2)}, u32[]{:S(2)}) collective-permute-start(bf16[296,128]{1,0:T(8,128)(2,1)S(1)} %pad_maximum_fusion.1), channel_id=1, source_target_pairs={{0,2},{2,0},{4,6},{6,4},{8,10},{10,8},{12,14},{14,12},{16,18},{18,... | collective-permute-start | bytes 227336 | tf_op jit(solution)/shard_map/ppermute | solution.py:271
  22.7 5.8 %collective-permute-start.5 = (bf16[232,128]{1,0:T(8,128)(2,1)S(1)}, bf16[232,128]{1,0:T(8,128)(2,1)S(1)}, u32[]{:S(2)}, u32[]{:S(2)}) collective-permute-start(bf16[232,128]{1,0:T(8,128)(2,1)S(1)} %get-tuple-element.56), channel_id=1, source_target_pairs={{0,4},{2,6},{4,0},{6,2},{8,12},{10,14},{12,8},{14,10},{16,20},{18,... | collective-permute-start | bytes 178184 | tf_op jit(solution)/shard_map/ppermute | solution.py:271
  23.0 5.5 %collective-permute-start.6 = (bf16[232,128]{1,0:T(8,128)(2,1)S(1)}, bf16[232,128]{1,0:T(8,128)(2,1)S(1)}, u32[]{:S(2)}, u32[]{:S(2)}) collective-permute-start(bf16[232,128]{1,0:T(8,128)(2,1)S(1)} %get-tuple-element.57), channel_id=1, source_target_pairs={{0,6},{2,4},{4,2},{6,0},{8,14},{10,12},{12,10},{14,8},{16,22},{18,... | collective-permute-start | bytes 178184 | tf_op jit(solution)/shard_map/ppermute | solution.py:271
  26.2 7.4 %collective-permute-start.7 = (bf16[64,128]{1,0:T(8,128)(2,1)S(1)}, bf16[64,128]{1,0:T(8,128)(2,1)S(1)}, u32[]{:S(2)}, u32[]{:S(2)}) collective-permute-start(bf16[64,128]{1,0:T(8,128)(2,1)S(1)} %get-tuple-element.40), channel_id=1, source_target_pairs={{0,30},{2,4},{4,2},{6,8},{8,6},{10,12},{12,10},{14,16},{16,14},{18... | collective-permute-start | bytes 49160 | tf_op jit(solution)/shard_map/ppermute | solution.py:277
  33.7 7.2 %collective-permute-start.9 = (bf16[296,128]{1,0:T(8,128)(2,1)S(1)}, bf16[296,128]{1,0:T(8,128)(2,1)S(1)}, u32[]{:S(2)}, u32[]{:S(2)}) collective-permute-start(bf16[296,128]{1,0:T(8,128)(2,1)S(1)} %pad_maximum_fusion.2), channel_id=1, source_target_pairs={{0,16},{2,18},{4,20},{6,22},{8,24},{10,26},{12,28},{14,30},{16,0},... | collective-permute-start | bytes 227336 | tf_op jit(solution)/shard_map/ppermute | solution.py:271
  33.7 5.5 %collective-permute-start.8 = (bf16[232,128]{1,0:T(8,128)(2,1)S(1)}, bf16[232,128]{1,0:T(8,128)(2,1)S(1)}, u32[]{:S(2)}, u32[]{:S(2)}) collective-permute-start(bf16[232,128]{1,0:T(8,128)(2,1)S(1)} %add_add_fusion), channel_id=1, source_target_pairs={{0,8},{2,10},{4,12},{6,14},{8,0},{10,2},{12,4},{14,6},{16,24},{18,... | collective-permute-start | bytes 178184 | tf_op jit(solution)/shard_map/ppermute | solution.py:271
  33.7 7.1 %collective-permute-start.10 = (bf16[232,128]{1,0:T(8,128)(2,1)S(1)}, bf16[232,128]{1,0:T(8,128)(2,1)S(1)}, u32[]{:S(2)}, u32[]{:S(2)}) collective-permute-start(bf16[232,128]{1,0:T(8,128)(2,1)S(1)} %add_add_fusion), channel_id=1, source_target_pairs={{0,24},{2,26},{4,28},{6,30},{8,16},{10,18},{12,20},{14,22},{16,8},... | collective-permute-start | bytes 178184 | tf_op jit(solution)/shard_map/ppermute | solution.py:271
  40.9 4.3 %collective-permute-start.11 = (bf16[232,128]{1,0:T(8,128)(2,1)S(1)}, bf16[232,128]{1,0:T(8,128)(2,1)S(1)}, u32[]{:S(2)}, u32[]{:S(2)}) collective-permute-start(bf16[232,128]{1,0:T(8,128)(2,1)S(1)} %add_convert_fusion.1), channel_id=1, source_target_pairs={{0,2},{2,0},{4,6},{6,4},{8,10},{10,8},{12,14},{14,12},{16,18},{18,... | collective-permute-start | bytes 178184 | tf_op jit(solution)/shard_map/ppermute | solution.py:271
  45.2 1.4 %collective-permute-start.12 = (bf16[464,128]{1,0:T(8,128)(2,1)S(1)}, bf16[464,128]{1,0:T(8,128)(2,1)S(1)}, u32[]{:S(2)}, u32[]{:S(2)}) collective-permute-start(bf16[464,128]{1,0:T(8,128)(2,1)S(1)} %pad_maximum_fusion.mine_ref), channel_id=1, source_target_pairs={{0,1},{1,0},{2,3},{3,2},{4,5},{5,4},{6,7},{7,6},{8,9},{9,8},{10,11... | collective-permute-start | bytes 356360 | tf_op jit(solution)/shard_map/ppermute | solution.py:271

commit v5 on v4

--- a/solution.py
+++ b/solution.py
@@ -86,8 +86,11 @@
             at += 1
 
 
-def pack_kernel(meta_ref, h_s, far_ref, one_ref, two_ref, tmat, low, high, got):
-    spread([meta_ref.at[:, : low.shape[0]]], tmat, [(low, high)])
+def digits_kernel(meta_ref, low, high, tmat):
+    spread([meta_ref], tmat, [(low, high)])
+
+
+def pack_kernel(low, high, h_s, far_ref, one_ref, two_ref, got):
     hot = one_hot_cols(low[...], high[...], h_s.shape[0])
     got[...] = mm(hot, h_s[...])
     upper, odd = my_place()
@@ -232,11 +235,15 @@
     out_ref[...] = gnode_ref[...] + mm(one_hot_rows(meta_ref[:, : ret.shape[0]], out_ref.shape[0]), ret[...])
 
 
-def unpack_kernel(factor, mine_ref, oth_ref, g1, g2, gg, gn1, gn2, gng, wg):
+def unpack_kernel(factor, p0, p1, p2, p3, g1, g2, gg, gn1, gn2, gng, wg):
     core = lax.axis_index("dp")
-    part, H = mine_ref.shape
-    wg[pl.ds(pl.multiple_of(core * part, 8), part), :] = mine_ref[...].astype(F32) * factor
-    wg[pl.ds(pl.multiple_of((1 - core) * part, 8), part), :] = oth_ref[...].astype(F32) * factor
+    low = lax.axis_index("morton") % 2
+    part, H = p0.shape
+    for ref, by, core_by in ((p0, 0, 0), (p1, 1, 0), (p2, 0, 1), (p3, 1, 1)):
+        side = core if core_by == 0 else 1 - core
+        bit = low if by == 0 else 1 - low
+        at = pl.multiple_of((2 * side + bit) * part, 8)
+        wg[pl.ds(at, part), :] = ref[...].astype(F32) * factor
     g1[...] = wg[0 : 3 * H, :]
     g2[...] = wg[3 * H : 4 * H, :]
     gn1[...] = wg[4 * H : 6 * H, :]
@@ -269,6 +276,14 @@
 def flip(x, axis, by):
     n = lax.axis_size(axis)
     return lax.ppermute(x, axis, [(i, i ^ by) for i in range(n)])
+
+
+def flip_both(x, by, core_by):
+    n, pair = lax.axis_size("morton"), lax.axis_size("dp")
+    moves = [
+        (m * pair + d, (m ^ by) * pair + (d ^ core_by)) for m in range(n) for d in range(pair)
+    ]
+    return lax.ppermute(x, ("morton", "dp"), moves)
 
 
 def cross_pairs(x):
@@ -327,11 +342,8 @@
     for by in list(extra):
         got[by] = flip(extra.pop(by), "morton", by)
     w = v.astype(BF)
-    back = flip(w, "morton", 1)
-    both = jnp.stack([w, back])
-    mine = jnp.concatenate([pick(both, low), pick(both, 1 - low)], axis=0)
-    mine, done = lax.optimization_barrier((mine, finish(early, got)))
-    return mine, flip(mine, "dp", 1), done
+    parts = [w, flip_both(w, 1, 0), flip_both(w, 0, 1), flip_both(w, 1, 1)]
+    return parts, finish(early, got)
 
 
 def local_step(
@@ -348,17 +360,18 @@
     q = G // 4
     T = C + G
     i32 = jnp.int32
-    meta = jnp.maximum(send_rows, 0)
     dma = pltpu.SemaphoreType.DMA
     egain, ngain = edge_gain.reshape(1, H), node_gain.reshape(1, H)
 
     ghost = sds((q, H), BF)
+    low, high = call(
+        digits_kernel, (sds((G, LANES), BF),) * 2, [VM], (VM,) * 2,
+        [pltpu.VMEM((LANES, LANES), i32)], 4_000_000_000, 8_000_000, 8,
+    )(send_rows)
     far, one, two = call(
-        pack_kernel, (ghost,) * 3, [VM] * 2, (VM,) * 3,
-        [pltpu.VMEM((LANES, LANES), i32), pltpu.VMEM((G, LANES), BF),
-         pltpu.VMEM((G, LANES), BF), pltpu.VMEM((G, H), F32)],
-        4_000_000_000, 8_000_000, 8,
-    )(meta, h)
+        pack_kernel, (ghost,) * 3, [VM] * 3, (VM,) * 3,
+        [pltpu.VMEM((G, H), F32)], 4_000_000_000, 8_000_000, 8,
+    )(low, high, h)
     far = flip(far, "morton", half)
     one = flip(one, "morton", 1)
     two = cross_pairs(two)
@@ -392,16 +405,16 @@
             node_kernel, sds((C, H), F32), [VM] * 5, VM,
             [pltpu.VMEM((G, H), BF)],
             2 * C * G * H, 8 * C * H, 8,
-        )(meta, gnode, got[half], got[1], rtwo)
+        )(send_rows, gnode, got[half], got[1], rtwo)
 
     rtwo = cross_pairs(btwo)
-    mine, oth, grad_node = reduce_all(wmine, woth, {1: bone, half: bfar}, rtwo, finish)
+    pieces, grad_node = reduce_all(wmine, woth, {1: bone, half: bfar}, rtwo, finish)
     factor = float(pair * peers * E) ** -0.5
     g1, g2, gg, gn1, gn2, gng = call(
         functools.partial(unpack_kernel, factor),
         tuple(sds(s, F32) for s in ((3 * H, H), (H, H), (1, H), (2 * H, H), (H, H), (1, H))),
-        [VM] * 2, (VM,) * 6, [pltpu.VMEM((rows, H), F32)], rows * H, 8 * rows * H, 8,
-    )(mine, oth)
+        [VM] * 4, (VM,) * 6, [pltpu.VMEM((rows, H), F32)], rows * H, 8 * rows * H, 8,
+    )(*pieces)
     return (
         grad_node[None], gedge[None], g1, g2, gg.reshape(H), gn1, gn2, gng.reshape(H),
     )

time: 47.6 us -> 45.8 us (0.962)
  waiting for transfers between devices: 15.7 us -> 13 us
  starting transfers between devices: 18.3 us -> 19.5 us
  other arithmetic: 0.87 us -> 0.12 us
    ppermute x11 -> x9, waiting for transfers between devices: 8.64 us -> 4.86 us  [flip(): return lax.ppermute(x, axis, [(i, i ^ by) for i in range(n)])]
    ppermute x0 -> x3, starting transfers between devices: none -> 2.19 us  [flip_both(): return lax.ppermute(x, ('morton', 'dp'), moves)]
    ppermute x0 -> x3, waiting for transfers between devices: none -> 1.56 us  [flip_both(): return lax.ppermute(x, ('morton', 'dp'), moves)]
    ppermute x11 -> x9, starting transfers between devices: 13.8 us -> 12.7 us  [flip(): return lax.ppermute(x, axis, [(i, i ^ by) for i in range(n)])]
    max x1 -> x0, other arithmetic: 0.68 us -> none  [local_step(): meta = jnp.maximum(send_rows, 0)]
    ppermute x2, waiting for transfers between devices: 7.09 us -> 6.61 us  [cross_pairs(): return lax.ppermute(x, 'morton', pairs)]
    unnamed x26 -> x28, local copies, waits for them, and re-layouts: 0.97 us -> 1.42 us
  transfers between devices with their start and end apart: 13 -> 14, of which waited for: 7 -> 7; matrix products, arithmetic and copies ran while one was open for 0% -> 0% of each run, Pallas kernels for 7% -> 7%
where the time goes in v5:
time: 45.8 us; the launch traced here: 45.6 us
  starting transfers between devices  19.5 us (43%)
  waiting for transfers between devices  13 us (28%)
  Pallas kernels  10 us (22%)
  between operations  1.54 us (3%)
  local copies, waits for them, and re-layouts  1.45 us (3%)
    ppermute x9, starting transfers between devices, flip(): return lax.ppermute(x, axis, [(i, i ^ by) for i in range(n)])  12.7 us
    ppermute x2, waiting for transfers between devices, cross_pairs(): return lax.ppermute(x, 'morton', pairs)  6.61 us
    pallas_call x1, Pallas kernels, local_step(): call(main_kernel, (sds((C, H), F32), sds((E, H), F32), ghost, ghost, ghos...  5.51 us
    ppermute x9, waiting for transfers between devices, flip(): return lax.ppermute(x, axis, [(i, i ^ by) for i in range(n)])  4.86 us
    ppermute x2, starting transfers between devices, cross_pairs(): return lax.ppermute(x, 'morton', pairs)  4.56 us
    pallas_call x1, Pallas kernels, local_step(): call(pre_kernel, (sds((E, H), F32), sds((E, T), BF), sds((E, C), BF)), [V...  2.28 us
    ppermute x3, starting transfers between devices, flip_both(): return lax.ppermute(x, ('morton', 'dp'), moves)  2.19 us
    ppermute x3, waiting for transfers between devices, flip_both(): return lax.ppermute(x, ('morton', 'dp'), moves)  1.56 us
  transfers between devices with their start and end apart: 14, of which 7 were waited for; matrix products, arithmetic and copies ran while one was open for 0% of the time, Pallas kernels for 7%

profile of v5, /device:TPU:0, one launch (start us, length us, event | category | flops | bytes accessed | tf_op | source)
XLA Modules:
  0.0 45.6 jit_solution(15838382037205884766)
XLA Ops:
  0.6 0.0 copy-start
  0.6 0.7 %copy-done = s32[1,256]{1,0:T(1,128)S(1)} copy-done((s32[1,256]{1,0:T(1,128)S(1)}, s32[1,256]{1,0:T(1,128)}, u32[]{:S(2)}) %copy-start) | copy-done | bytes 1048
  1.3 0.2 shard_map.198
  1.5 0.7 %copy-done.5 = bf16[1,512,128]{2,1,0:T(8,128)(2,1)S(1)} copy-done((bf16[1,512,128]{2,1,0:T(8,128)(2,1)S(1)}, bf16[1,512,128]{2,1,0:T(8,128)(2,1)}, u32[]{:S(2)}) %copy-start.5) | copy-done | bytes 131096
  2.2 0.2 shard_map.199
  2.5 4.1 %collective-permute-start = (bf16[64,128]{1,0:T(8,128)(2,1)S(1)}, bf16[64,128]{1,0:T(8,128)(2,1)S(1)}, u32[]{:S(2)}, u32[]{:S(2)}) collective-permute-start(bf16[64,128]{1,0:T(8,128)(2,1)S(1)} %get-tuple-element.36), channel_id=1, source_target_pairs={{0,16},{2,18},{4,20},{6,22},{8,24},{10,26},{12,28},{14,30},{16,0},... | collective-permute-start | bytes 49160 | tf_op jit(solution)/shard_map/ppermute | solution.py:278
  6.6 1.5 %collective-permute-start.1 = (bf16[64,128]{1,0:T(8,128)(2,1)S(1)}, bf16[64,128]{1,0:T(8,128)(2,1)S(1)}, u32[]{:S(2)}, u32[]{:S(2)}) collective-permute-start(bf16[64,128]{1,0:T(8,128)(2,1)S(1)} %get-tuple-element.37), channel_id=1, source_target_pairs={{0,2},{2,0},{4,6},{6,4},{8,10},{10,8},{12,14},{14,12},{16,18},{18,... | collective-permute-start | bytes 49160 | tf_op jit(solution)/shard_map/ppermute | solution.py:278
  8.1 2.3 %collective-permute-start.2 = (bf16[64,128]{1,0:T(8,128)(2,1)S(1)}, bf16[64,128]{1,0:T(8,128)(2,1)S(1)}, u32[]{:S(2)}, u32[]{:S(2)}) collective-permute-start(bf16[64,128]{1,0:T(8,128)(2,1)S(1)} %get-tuple-element.38), channel_id=1, source_target_pairs={{0,30},{2,4},{4,2},{6,8},{8,6},{10,12},{12,10},{14,16},{16,14},{18... | collective-permute-start | bytes 49160 | tf_op jit(solution)/shard_map/ppermute | solution.py:292
  10.4 0.0 copy-start.7
  10.4 0.0 copy-start.8
  10.4 0.0 copy-start.12
  10.5 2.3 %shard_map.197 = (f32[2048,128]{1,0:T(8,128)S(1)}, bf16[2048,768]{1,0:T(8,128)(2,1)S(1)}, bf16[2048,512]{1,0:T(8,128)(2,1)S(1)}) custom-call(bf16[512,128]{1,0:T(8,128)(2,1)S(1)} %bitcast.19, bf16[2048,128]{1,0:T(8,128)(2,1)S(1)} %bitcast.15, s32[1,2048]{1,0:T(1,128)S(1)} %copy-done.10, s32[1,2048]{1,0:T(1,128)S(1)} %copy-done.11, f32[384,128]{1,0:T(8,128)S(1)} %copy-done.4), custom_call_target="tpu_custom_call" | custom-call | flops 2415919104 | bytes 7340032 | tf_op jit(solution)/shard_map/pallas_call | solution.py:379
  13.4 2.0 %collective-permute-done.2.two_ref = bf16[64,128]{1,0:T(8,128)(2,1)S(1)} collective-permute-done((bf16[64,128]{1,0:T(8,128)(2,1)S(1)}, bf16[64,128]{1,0:T(8,128)(2,1)S(1)}, u32[]{:S(2)}, u32[]{:S(2)}) %collective-permute-start.2) | collective-permute-done | bytes 16416 | tf_op jit(solution)/shard_map/ppermute | solution.py:292
  15.5 5.5 %shard_map.200 = (f32[512,128]{1,0:T(8,128)S(1)}, f32[2048,128]{1,0:T(8,128)}, bf16[64,128]{1,0:T(8,128)(2,1)S(1)}, bf16[64,128]{1,0:T(8,128)(2,1)S(1)}, bf16[64...) custom-call(s32[1,1]{1,0:T(1,128)S(6)} %copy.22.count_ref, ...), custom_call_target="tpu_custom_call" | custom-call | flops 2415919104 | bytes 2097152 | tf_op jit(solution)/shard_map/pallas_call | solution.py:390
  21.0 0.1 collective-permute-start.3
  21.1 1.3 %collective-permute-done.3 = bf16[464,128]{1,0:T(8,128)(2,1)S(1)} collective-permute-done((bf16[464,128]{1,0:T(8,128)(2,1)S(1)}, bf16[464,128]{1,0:T(8,128)(2,1)S(1)}, u32[]{:S(2)}, u32[]{:S(2)}) %collective-permute-start.3) | collective-permute-done | bytes 118816 | tf_op jit(solution)/shard_map/ppermute | solution.py:278
  22.5 0.1 collective-permute-start.4
  22.6 0.3 collective-permute-start.6
  22.8 3.2 %collective-permute-start.5 = (bf16[232,128]{1,0:T(8,128)(2,1)S(1)}, bf16[232,128]{1,0:T(8,128)(2,1)S(1)}, u32[]{:S(2)}, u32[]{:S(2)}) collective-permute-start(bf16[232,128]{1,0:T(8,128)(2,1)S(1)} %get-tuple-element.54), channel_id=1, source_target_pairs={{0,4},{2,6},{4,0},{6,2},{8,12},{10,14},{12,8},{14,10},{16,20},{18,... | collective-permute-start | bytes 178184 | tf_op jit(solution)/shard_map/ppermute | solution.py:278
  26.0 2.3 %collective-permute-start.7 = (bf16[64,128]{1,0:T(8,128)(2,1)S(1)}, bf16[64,128]{1,0:T(8,128)(2,1)S(1)}, u32[]{:S(2)}, u32[]{:S(2)}) collective-permute-start(bf16[64,128]{1,0:T(8,128)(2,1)S(1)} %get-tuple-element.43), channel_id=1, source_target_pairs={{0,30},{2,4},{4,2},{6,8},{8,6},{10,12},{12,10},{14,16},{16,14},{18... | collective-permute-start | bytes 49160 | tf_op jit(solution)/shard_map/ppermute | solution.py:292
  28.3 0.5 %collective-permute-done.5 = bf16[232,128]{1,0:T(8,128)(2,1)S(1)} collective-permute-done((bf16[232,128]{1,0:T(8,128)(2,1)S(1)}, bf16[232,128]{1,0:T(8,128)(2,1)S(1)}, u32[]{:S(2)}, u32[]{:S(2)}) %collective-permute-start.5) | collective-permute-done | bytes 59424 | tf_op jit(solution)/shard_map/ppermute | solution.py:278
  28.9 4.6 %collective-permute-done.7.two_ref = bf16[64,128]{1,0:T(8,128)(2,1)S(1)} collective-permute-done((bf16[64,128]{1,0:T(8,128)(2,1)S(1)}, bf16[64,128]{1,0:T(8,128)(2,1)S(1)}, u32[]{:S(2)}, u32[]{:S(2)}) %collective-permute-start.7) | collective-permute-done | bytes 16416 | tf_op jit(solution)/shard_map/ppermute | solution.py:292
  33.5 0.2 collective-permute-start.10
  33.7 3.2 %collective-permute-start.9 = (bf16[232,128]{1,0:T(8,128)(2,1)S(1)}, bf16[232,128]{1,0:T(8,128)(2,1)S(1)}, u32[]{:S(2)}, u32[]{:S(2)}) collective-permute-start(bf16[232,128]{1,0:T(8,128)(2,1)S(1)} %add_add_fusion), channel_id=1, source_target_pairs={{0,8},{2,10},{4,12},{6,14},{8,0},{10,2},{12,4},{14,6},{16,24},{18,... | collective-permute-start | bytes 178184 | tf_op jit(solution)/shard_map/ppermute | solution.py:278
  37.0 2.7 %collective-permute-done.10 = bf16[232,128]{1,0:T(8,128)(2,1)S(1)} collective-permute-done((bf16[232,128]{1,0:T(8,128)(2,1)S(1)}, bf16[232,128]{1,0:T(8,128)(2,1)S(1)}, u32[]{:S(2)}, u32[]{:S(2)}) %collective-permute-start.10) | collective-permute-done | bytes 59424 | tf_op jit(solution)/shard_map/ppermute | solution.py:278
  39.7 0.4 collective-permute-done.9
  40.1 0.1 collective-permute-start.11
  40.2 0.1 collective-permute-start.12
  40.2 2.0 %collective-permute-start.13 = (bf16[232,128]{1,0:T(8,128)(2,1)S(1)}, bf16[232,128]{1,0:T(8,128)(2,1)S(1)}, u32[]{:S(2)}, u32[]{:S(2)}) collective-permute-start(bf16[232,128]{1,0:T(8,128)(2,1)S(1)} %add_convert_fusion.1.p0), channel_id=1, source_target_pairs={{0,3},{1,2},{2,1},{3,0},{4,7},{5,6},{6,5},{7,4},{8,11},{9,10},{10,... | collective-permute-start | bytes 178184 | tf_op jit(solution)/shard_map/ppermute | solution.py:286
  42.3 1.0 %shard_map.201 = f32[512,128]{1,0:T(8,128)} custom-call(s32[1,256]{1,0:T(1,128)S(1)} %copy-done.1, f32[512,128]{1,0:T(8,128)S(1)} %get-tuple-element.39.gnode_ref, bf16[64,128]{1,0:T(8,128)(2,1)S(1)} %slice.17.far_ref, bf16[64,128]{1,0:T(8,128)(2,1)S(1)} %slice.18.one_ref, bf16[64,128]{1,0:T(8,128)(2,1)S(1)} %collective-permute-done.7.two_ref), custom_call_target="tpu_custom_call" | custom-call | flops 33554432 | bytes 524288 | tf_op jit(solution)/shard_map/pallas_call | solution.py:404
  43.3 1.6 %collective-permute-done.11.p1 = bf16[232,128]{1,0:T(8,128)(2,1)S(1)} collective-permute-done((bf16[232,128]{1,0:T(8,128)(2,1)S(1)}, bf16[232,128]{1,0:T(8,128)(2,1)S(1)}, u32[]{:S(2)}, u32[]{:S(2)}) %collective-permute-start.11) | collective-permute-done | bytes 59424 | tf_op jit(solution)/shard_map/ppermute | solution.py:286
  44.8 0.8 %shard_map.202 = (f32[384,128]{1,0:T(8,128)}, f32[128,128]{1,0:T(8,128)}, f32[1,128]{1,0:T(1,128)}, f32[256,128]{1,0:T(8,128)}, f32[128,128]{1,0:T(8,128)}, /*index=5*/f32[1,128]{1,0:T(1,128)}) custom-call(bf16[232,128]{1,0:T(8,128)(2,1)S(1)} %add_convert_fusion.1.p0, bf16[232,128]{1,0:T(8,128)(2,1)S(1)} %collective-permute-done.11.p1, ...), custom_call_target="tpu_custom_call" | custom-call | flops 118784 | bytes 950272 | tf_op jit(solution)/shard_map/pallas_call | solution.py:413
  (38 shorter events, 0.2 us)
Async XLA Ops:
  0.6 0.7 %copy-start = (s32[1,256]{1,0:T(1,128)S(1)}, s32[1,256]{1,0:T(1,128)}, u32[]{:S(2)}) copy-start(s32[1,256]{1,0:T(1,128)} %meta_ref.3) | copy-start | bytes 3076
  1.3 0.9 %copy-start.5 = (bf16[1,512,128]{2,1,0:T(8,128)(2,1)S(1)}, bf16[1,512,128]{2,1,0:T(8,128)(2,1)}, u32[]{:S(2)}) copy-start(bf16[1,512,128]{2,1,0:T(8,128)(2,1)} %param.14) | copy-start | bytes 393220
  2.2 8.2 %copy-start.2 = (bf16[1,2048,128]{2,1,0:T(8,128)(2,1)S(1)}, bf16[1,2048,128]{2,1,0:T(8,128)(2,1)}, u32[]{:S(2)}) copy-start(bf16[1,2048,128]{2,1,0:T(8,128)(2,1)} %param.15) | copy-start | bytes 1572868
  2.2 8.2 %copy-start.4 = (f32[384,128]{1,0:T(8,128)S(1)}, f32[384,128]{1,0:T(8,128)}, u32[]{:S(2)}) copy-start(f32[384,128]{1,0:T(8,128)} %w1_s.3) | copy-start | bytes 589828
  2.2 8.2 %copy-start.10 = (s32[1,2048]{1,0:T(1,128)S(1)}, s32[1,2048]{1,0:T(1,128)}, u32[]{:S(2)}) copy-start(s32[1,2048]{1,0:T(1,128)} %snd_s.1) | copy-start | bytes 24580
  2.2 8.2 %copy-start.11 = (s32[1,2048]{1,0:T(1,128)S(1)}, s32[1,2048]{1,0:T(1,128)}, u32[]{:S(2)}) copy-start(s32[1,2048]{1,0:T(1,128)} %rcv_s.1) | copy-start | bytes 24580
  2.5 10.9 %collective-permute-start = (bf16[64,128]{1,0:T(8,128)(2,1)S(1)}, bf16[64,128]{1,0:T(8,128)(2,1)S(1)}, u32[]{:S(2)}, u32[]{:S(2)}) collective-permute-start(bf16[64,128]{1,0:T(8,128)(2,1)S(1)} %get-tuple-element.36), channel_id=1, source_target_pairs={{0,16},{2,18},{4,20},{6,22},{8,24},{10,26},{12,28},{14,30},{16,0},... | collective-permute-start | bytes 49160 | tf_op jit(solution)/shard_map/ppermute | solution.py:278
  6.6 6.8 %collective-permute-start.1 = (bf16[64,128]{1,0:T(8,128)(2,1)S(1)}, bf16[64,128]{1,0:T(8,128)(2,1)S(1)}, u32[]{:S(2)}, u32[]{:S(2)}) collective-permute-start(bf16[64,128]{1,0:T(8,128)(2,1)S(1)} %get-tuple-element.37), channel_id=1, source_target_pairs={{0,2},{2,0},{4,6},{6,4},{8,10},{10,8},{12,14},{14,12},{16,18},{18,... | collective-permute-start | bytes 49160 | tf_op jit(solution)/shard_map/ppermute | solution.py:278
  8.1 7.3 %collective-permute-start.2 = (bf16[64,128]{1,0:T(8,128)(2,1)S(1)}, bf16[64,128]{1,0:T(8,128)(2,1)S(1)}, u32[]{:S(2)}, u32[]{:S(2)}) collective-permute-start(bf16[64,128]{1,0:T(8,128)(2,1)S(1)} %get-tuple-element.38), channel_id=1, source_target_pairs={{0,30},{2,4},{4,2},{6,8},{8,6},{10,12},{12,10},{14,16},{16,14},{18... | collective-permute-start | bytes 49160 | tf_op jit(solution)/shard_map/ppermute | solution.py:292
  10.4 5.0 %copy-start.3 = (bf16[1,2048,128]{2,1,0:T(8,128)(2,1)S(1)}, bf16[1,2048,128]{2,1,0:T(8,128)(2,1)}, u32[]{:S(2)}) copy-start(bf16[1,2048,128]{2,1,0:T(8,128)(2,1)} %param.17) | copy-start | bytes 1572868
  10.4 5.0 %copy-start.6 = (bf16[1,512,128]{2,1,0:T(8,128)(2,1)S(1)}, bf16[1,512,128]{2,1,0:T(8,128)(2,1)}, u32[]{:S(2)}) copy-start(bf16[1,512,128]{2,1,0:T(8,128)(2,1)} %param.16) | copy-start | bytes 393220
  10.4 5.0 %copy-start.7 = (f32[256,128]{1,0:T(8,128)S(1)}, f32[256,128]{1,0:T(8,128)}, u32[]{:S(2)}) copy-start(f32[256,128]{1,0:T(8,128)} %nw1_s.1) | copy-start | bytes 393220
  10.4 5.0 %copy-start.8 = (f32[128,128]{1,0:T(8,128)S(1)}, f32[128,128]{1,0:T(8,128)}, u32[]{:S(2)}) copy-start(f32[128,128]{1,0:T(8,128)} %w2_s.1) | copy-start | bytes 196612
  10.4 5.0 %copy-start.9 = (f32[128,128]{1,0:T(8,128)S(1)}, f32[128,128]{1,0:T(8,128)}, u32[]{:S(2)}) copy-start(f32[128,128]{1,0:T(8,128)} %nw2_s.1) | copy-start | bytes 196612
  10.4 5.0 %copy-start.12 = (f32[128]{0:T(128)S(1)}, f32[128]{0:T(128)}, u32[]{:S(2)}) copy-start(f32[128]{0:T(128)} %param.24) | copy-start | bytes 1540
  10.5 5.0 %copy-start.13 = (f32[128]{0:T(128)S(1)}, f32[128]{0:T(128)}, u32[]{:S(2)}) copy-start(f32[128]{0:T(128)} %param.27) | copy-start | bytes 1540
  15.5 26.8 %copy-start.1 = (s32[1,256]{1,0:T(1,128)S(1)}, s32[1,256]{1,0:T(1,128)}, u32[]{:S(2)}) copy-start(s32[1,256]{1,0:T(1,128)} %meta_ref.3) | copy-start | bytes 3076
  21.0 1.4 %collective-permute-start.3 = (bf16[464,128]{1,0:T(8,128)(2,1)S(1)}, bf16[464,128]{1,0:T(8,128)(2,1)S(1)}, u32[]{:S(2)}, u32[]{:S(2)}) collective-permute-start(bf16[464,128]{1,0:T(8,128)(2,1)S(1)} %get-tuple-element.41), channel_id=1, source_target_pairs={{0,1},{1,0},{2,3},{3,2},{4,5},{5,4},{6,7},{7,6},{8,9},{9,8},{10,11... | collective-permute-start | bytes 356360 | tf_op jit(solution)/shard_map/ppermute | solution.py:278
  22.5 6.3 %collective-permute-start.4 = (bf16[296,128]{1,0:T(8,128)(2,1)S(1)}, bf16[296,128]{1,0:T(8,128)(2,1)S(1)}, u32[]{:S(2)}, u32[]{:S(2)}) collective-permute-start(bf16[296,128]{1,0:T(8,128)(2,1)S(1)} %pad_maximum_fusion), channel_id=1, source_target_pairs={{0,2},{2,0},{4,6},{6,4},{8,10},{10,8},{12,14},{14,12},{16,18},{18,... | collective-permute-start | bytes 227336 | tf_op jit(solution)/shard_map/ppermute | solution.py:278
  22.6 5.8 %collective-permute-start.6 = (bf16[232,128]{1,0:T(8,128)(2,1)S(1)}, bf16[232,128]{1,0:T(8,128)(2,1)S(1)}, u32[]{:S(2)}, u32[]{:S(2)}) collective-permute-start(bf16[232,128]{1,0:T(8,128)(2,1)S(1)} %get-tuple-element.55), channel_id=1, source_target_pairs={{0,6},{2,4},{4,2},{6,0},{8,14},{10,12},{12,10},{14,8},{16,22},{18,... | collective-permute-start | bytes 178184 | tf_op jit(solution)/shard_map/ppermute | solution.py:278
  22.8 6.0 %collective-permute-start.5 = (bf16[232,128]{1,0:T(8,128)(2,1)S(1)}, bf16[232,128]{1,0:T(8,128)(2,1)S(1)}, u32[]{:S(2)}, u32[]{:S(2)}) collective-permute-start(bf16[232,128]{1,0:T(8,128)(2,1)S(1)} %get-tuple-element.54), channel_id=1, source_target_pairs={{0,4},{2,6},{4,0},{6,2},{8,12},{10,14},{12,8},{14,10},{16,20},{18,... | collective-permute-start | bytes 178184 | tf_op jit(solution)/shard_map/ppermute | solution.py:278
  26.0 7.4 %collective-permute-start.7 = (bf16[64,128]{1,0:T(8,128)(2,1)S(1)}, bf16[64,128]{1,0:T(8,128)(2,1)S(1)}, u32[]{:S(2)}, u32[]{:S(2)}) collective-permute-start(bf16[64,128]{1,0:T(8,128)(2,1)S(1)} %get-tuple-element.43), channel_id=1, source_target_pairs={{0,30},{2,4},{4,2},{6,8},{8,6},{10,12},{12,10},{14,16},{16,14},{18... | collective-permute-start | bytes 49160 | tf_op jit(solution)/shard_map/ppermute | solution.py:292
  33.5 6.5 %collective-permute-start.8 = (bf16[296,128]{1,0:T(8,128)(2,1)S(1)}, bf16[296,128]{1,0:T(8,128)(2,1)S(1)}, u32[]{:S(2)}, u32[]{:S(2)}) collective-permute-start(bf16[296,128]{1,0:T(8,128)(2,1)S(1)} %pad_maximum_fusion.1), channel_id=1, source_target_pairs={{0,16},{2,18},{4,20},{6,22},{8,24},{10,26},{12,28},{14,30},{16,0},... | collective-permute-start | bytes 227336 | tf_op jit(solution)/shard_map/ppermute | solution.py:278
  33.5 6.2 %collective-permute-start.10 = (bf16[232,128]{1,0:T(8,128)(2,1)S(1)}, bf16[232,128]{1,0:T(8,128)(2,1)S(1)}, u32[]{:S(2)}, u32[]{:S(2)}) collective-permute-start(bf16[232,128]{1,0:T(8,128)(2,1)S(1)} %add_add_fusion), channel_id=1, source_target_pairs={{0,24},{2,26},{4,28},{6,30},{8,16},{10,18},{12,20},{14,22},{16,8},... | collective-permute-start | bytes 178184 | tf_op jit(solution)/shard_map/ppermute | solution.py:278
  33.7 6.3 %collective-permute-start.9 = (bf16[232,128]{1,0:T(8,128)(2,1)S(1)}, bf16[232,128]{1,0:T(8,128)(2,1)S(1)}, u32[]{:S(2)}, u32[]{:S(2)}) collective-permute-start(bf16[232,128]{1,0:T(8,128)(2,1)S(1)} %add_add_fusion), channel_id=1, source_target_pairs={{0,8},{2,10},{4,12},{6,14},{8,0},{10,2},{12,4},{14,6},{16,24},{18,... | collective-permute-start | bytes 178184 | tf_op jit(solution)/shard_map/ppermute | solution.py:278
  40.1 4.7 %collective-permute-start.11 = (bf16[232,128]{1,0:T(8,128)(2,1)S(1)}, bf16[232,128]{1,0:T(8,128)(2,1)S(1)}, u32[]{:S(2)}, u32[]{:S(2)}) collective-permute-start(bf16[232,128]{1,0:T(8,128)(2,1)S(1)} %add_convert_fusion.1.p0), channel_id=1, source_target_pairs={{0,2},{1,3},{2,0},{3,1},{4,6},{5,7},{6,4},{7,5},{8,10},{9,11},{10,... | collective-permute-start | bytes 178184 | tf_op jit(solution)/shard_map/ppermute | solution.py:286
  40.2 4.6 %collective-permute-start.12 = (bf16[232,128]{1,0:T(8,128)(2,1)S(1)}, bf16[232,128]{1,0:T(8,128)(2,1)S(1)}, u32[]{:S(2)}, u32[]{:S(2)}) collective-permute-start(bf16[232,128]{1,0:T(8,128)(2,1)S(1)} %add_convert_fusion.1.p0), channel_id=1, source_target_pairs={{0,1},{1,0},{2,3},{3,2},{4,5},{5,4},{6,7},{7,6},{8,9},{9,8},{10,11... | collective-permute-start | bytes 178184 | tf_op jit(solution)/shard_map/ppermute | solution.py:286
  40.2 4.6 %collective-permute-start.13 = (bf16[232,128]{1,0:T(8,128)(2,1)S(1)}, bf16[232,128]{1,0:T(8,128)(2,1)S(1)}, u32[]{:S(2)}, u32[]{:S(2)}) collective-permute-start(bf16[232,128]{1,0:T(8,128)(2,1)S(1)} %add_convert_fusion.1.p0), channel_id=1, source_target_pairs={{0,3},{1,2},{2,1},{3,0},{4,7},{5,6},{6,5},{7,4},{8,11},{9,10},{10,... | collective-permute-start | bytes 178184 | tf_op jit(solution)/shard_map/ppermute | solution.py:286
